TPU v7x, 128 devices: a whole 4x4x4 slice. The times are simulated.
128 devices in a mesh: dom: 128 (over x, z, y, core).
Axes of the slice: x: 4, y: 4, z: 4, core: 2. Of those that a mesh axis runs over, the one named last changes fastest.
Arguments:
- states: float32 [19, 524288], P(None, 'dom'), may hold values from 0 to 1
- region: int32 [524288], P('dom'), may hold values from 0 to 2
- half_volt: float32 [3, 18], replicated, may hold values from 0.2 to 0.8
- slopes: float32 [3, 18], replicated, may hold values from 0.05 to 0.2
- rates: float32 [3, 18], replicated, may hold values from 0.02 to 0.9
- conductance: float32 [3, 18], replicated, may hold values from 0.05 to 0.5
- reversal: float32 [3, 18], replicated, may hold values from -1 to 1
- stiffness: float32 [4096, 128, 128], P('dom'), as said below
- preconditioner: float32 [4096, 128, 128], P('dom'), as said below
- slots: int32 [524288], P('dom'), may hold values from 0 to 262143
- slot_gain: float32 [16384], replicated, may hold values from 0.5 to 2
- owner: int32 [524288, 1], P('dom'), may hold values from 0 to 127, as said below
- cell: int32 [524288], P('dom'), may hold values from 0 to 8191
- source_gain: float32 [524288], P('dom'), may hold values from 0.5 to 2
- torso_conduct: float32 [8192, 128], P('dom'), may hold values from 0.04 to 40
Outputs:
- new_states: float32 [19, 524288], P(None, 'dom')
- heart_potential: float32 [524288], P('dom')
- torso_potential: float32 [8192, 128], P('dom')
Inputs may be any that keep to these rules, and one draw needn't show every extreme that they name: `slots`: slots of 16384 or more mark nodes off the interface. A heart node on device i has an owner among the eight torso devices i - 3 to i + 3 and i + 128 // 2 (indices wrapping around the axis); among the heart nodes of one device at most 1024 have the same owner, and that many do in every draw. `stiffness`: each tile's block is symmetric positive definite. `preconditioner`: each tile's block is the inverse of the stiffness block.
All inputs are finite; a program needn't handle non-finite values.
Results may differ from a plain program's by a relative error of at most 0.0001.
Values sent between devices are 32-bit elements; how exact they have to be, the bound alone decides.
No kernel may reach another device: no remote copies, remote signals or barrier semaphores. Data moves between devices by JAX's collectives and lax.ppermute only.
A program may use at most 64 MiB of HBM per device.

v0:
```python
import jax
import jax.numpy as jnp
from jax import lax
from jax.sharding import Mesh
from jax.sharding import PartitionSpec as P

ITERS_H = 3
ITERS_T = 2
DOM = ("dom_0", "dom_1", "dom_2", "dom_3")


time_step = 0.2
heart_low = 1.0
heart_high = 4.0
highest = lax.Precision.HIGHEST


def cut_along(x, dim, peers):
    lengths = x.shape
    parts = x.reshape(*lengths[:dim], peers, lengths[dim] // peers, *lengths[dim + 1 :])
    return jnp.moveaxis(parts, dim, 0)


def sent_and_summed(x, axis, dim):
    peers = lax.axis_size(axis)
    parts = lax.all_to_all(cut_along(x, dim, peers), axis, 0, 0, tiled=True)
    return jnp.sum(parts, axis=0)


def sum_in_two_steps(x, axes, dim):
    far, near = axes
    parts = cut_along(x, dim, lax.axis_size(far))
    nearer = sent_and_summed(parts, near, dim + 1)
    arrived = lax.all_to_all(nearer, far, split_axis=0, concat_axis=0, tiled=True)
    return arrived.sum(axis=0)


def padded_to(lines, peers):
    spare = -lines.shape[0] % peers
    if not spare:
        return lines
    return jnp.concatenate([lines, jnp.zeros((spare, *lines.shape[1:]), lines.dtype)])


def sent_to_all(x, axis):
    peers = lax.axis_size(axis)
    return lax.all_to_all(jnp.broadcast_to(x[None], (peers, *x.shape)), axis, 0, 0, tiled=True)


def in_order(parts, dim):
    parts = jnp.moveaxis(parts, 0, dim)
    lengths = parts.shape
    return parts.reshape(*lengths[:dim], lengths[dim] * lengths[dim + 1], *lengths[dim + 2 :])


def gather_axes(x, axes, dim):
    far, near = axes
    parts = sent_to_all(sent_to_all(x, far), near)
    return in_order(parts.swapaxes(0, 1).reshape(-1, *x.shape), dim)


def sum_by_parts(x, axes):
    lines = x.reshape(-1)
    own = sum_in_two_steps(
        padded_to(lines, lax.axis_size(axes[0]) * lax.axis_size(axes[1])), axes, 0
    )
    whole = gather_axes(own, axes, 0)
    return whole[: len(lines)].reshape(x.shape)


def with_halo(cells, sides, width):
    for axis, dim in sides:
        count = lax.axis_size(axis)
        ends = count - 1
        head = lax.slice_in_dim(cells, 0, width, axis=dim)
        tail = lax.slice_in_dim(cells, cells.shape[dim] - width, cells.shape[dim], axis=dim)
        cells = jnp.concatenate(
            [
                lax.ppermute(tail, axis, [(i, (i + 1) % count) for i in range(ends)]),
                cells,
                lax.ppermute(head, axis, [((i + 1) % count, i) for i in range(ends)]),
            ],
            axis=dim,
        )
    return cells


def from_behind(x, axis, by):
    peers = lax.axis_size(axis)
    return lax.ppermute(x, axis, [(i, (i + by) % peers) for i in range(peers)])


def over_copies(x, axis):
    return sent_to_all(x, axis).min(axis=0)


def over_axes(x, axes):
    far, near = axes
    nearer = over_copies(x, near)
    return over_copies(nearer, far)


def taken_together(x, axis):
    everything = sent_to_all(x, axis)
    return jnp.sum(everything, axis=0)


def one_axis_at_a_time(x, axes):
    far, near = axes
    nearer = taken_together(x, near)
    return taken_together(nearer, far)


def ionic_step(states, region, half_volt, slopes, rates, conductance, reversal):
    volt = states[0]
    labels = (region[None, :] == jnp.arange(half_volt.shape[0], dtype=jnp.int32)[:, None]).astype(
        jnp.float32
    )

    def lookup(table):
        return jnp.dot(table.T, labels, precision=highest)

    target = jax.nn.sigmoid((volt[None, :] - lookup(half_volt)) / lookup(slopes))
    gates = target + (states[1:] - target) * jnp.exp(-lookup(rates))
    current = jnp.sum(lookup(conductance) * gates * (volt[None, :] - lookup(reversal)), axis=0)
    return jnp.concatenate([(volt - time_step * current)[None, :], gates], axis=0)


def tile_apply(mats, field):
    return jnp.einsum("tij,tj->ti", mats, field.reshape(-1, 128), precision=highest).reshape(-1)


def couple(field, slot_index, slot_gain):
    count = slot_gain.shape[0]
    partial_sum = jax.ops.segment_sum(field, slot_index, num_segments=count + 1)[:count]
    coupled = slot_gain * sum_by_parts(partial_sum, (("dom_0", "dom_1", "dom_2"), "dom_3"))
    extended = jnp.concatenate([coupled, jnp.zeros((1,), jnp.float32)])
    return extended[slot_index]


def torso_apply(field, diagonal):
    padded = with_halo(field, ((DOM, 0),), 1)
    padded = jnp.pad(padded, ((0, 0), (1, 1)))
    beside = padded[2:, 1:-1] + padded[:-2, 1:-1] + padded[1:-1, 2:] + padded[1:-1, :-2]
    return diagonal * field - beside


def body(
    states,
    region,
    half_volt,
    slopes,
    rates,
    conductance,
    reversal,
    stiffness,
    preconditioner,
    slots,
    slot_gain,
    owner,
    cell,
    source_gain,
    torso_conduct,
):
    new_states = ionic_step(states, region, half_volt, slopes, rates, conductance, reversal)
    count = slot_gain.shape[0]
    slot_index = jnp.where(slots < count, slots, count)
    center = (heart_high + heart_low) / 2.0
    half_width = (heart_high - heart_low) / 2.0
    sigma_ratio = center / half_width
    resid = tile_apply(stiffness, new_states[0])
    update = tile_apply(preconditioner, resid) / center
    potential = update
    ratio_now = 1.0 / sigma_ratio
    for iteration in range(ITERS_H):
        resid = resid - (tile_apply(stiffness, update) + couple(update, slot_index, slot_gain))
        ratio_next = 1.0 / (2.0 * sigma_ratio - ratio_now)
        update = ratio_next * ratio_now * update + 2.0 * ratio_next / half_width * tile_apply(
            preconditioner, resid
        )
        potential = potential + update
        ratio_now = ratio_next
    deposit = potential * source_gain
    row_count = torso_conduct.shape[0]
    cells_dev = row_count * 128
    devices = lax.axis_size(DOM)
    node_count = deposit.shape[0]
    capacity = node_count // 4
    here = lax.axis_index(DOM)
    distance = (owner[:, 0] - here + devices) % devices
    position = jnp.where(distance == devices // 2, 7, (distance + 3) % devices)
    onehot = (position[:, None] == jnp.arange(8, dtype=jnp.int32)[None, :]).astype(jnp.int32)
    rank = jnp.sum(jnp.cumsum(onehot, axis=0) * onehot, axis=1) - 1
    values = jnp.zeros((8, capacity), jnp.float32).at[position, rank].set(deposit)
    targets = jnp.zeros((8, capacity), jnp.float32).at[position, rank].set(cell.astype(jnp.float32))
    packed = jnp.stack([values, targets], axis=1)
    received = []
    for neighbour in range(8):
        stride = devices // 2 if neighbour == 7 else neighbour - 3
        received.append(from_behind(packed[neighbour], DOM, stride))
    arrived = jnp.stack(received, axis=0)
    source = jax.ops.segment_sum(
        arrived[:, 0].reshape(-1),
        arrived[:, 1].reshape(-1).astype(jnp.int32),
        num_segments=cells_dev,
    ).reshape(row_count, 128)
    diagonal = 4.0 + torso_conduct
    smallest = over_axes(jnp.min(torso_conduct), (("dom_0", "dom_1", "dom_2"), "dom_3"))
    low_bound = smallest / (4.0 + smallest)
    high_bound = (8.0 + smallest) / (4.0 + smallest)
    t_center = (high_bound + low_bound) / 2.0
    t_half = (high_bound - low_bound) / 2.0
    t_sigma = t_center / t_half
    t_resid = source
    t_update = t_resid / diagonal / t_center
    field = t_update
    t_ratio = 1.0 / t_sigma
    for iteration in range(ITERS_T):
        t_resid = t_resid - torso_apply(t_update, diagonal)
        t_next = 1.0 / (2.0 * t_sigma - t_ratio)
        t_update = t_next * t_ratio * t_update + 2.0 * t_next / t_half * (t_resid / diagonal)
        field = field + t_update
        t_ratio = t_next
    total = one_axis_at_a_time(jnp.sum(field), (("dom_0", "dom_1", "dom_2"), "dom_3"))
    grounded = field - total / (cells_dev * devices)
    return (new_states, potential, grounded)


def solution(mesh):
    torus = Mesh(mesh.devices.reshape(4, 4, 4, 2), ("dom_0", "dom_1", "dom_2", "dom_3"))
    placed = (
        P(None, DOM),
        P(DOM),
        P(),
        P(),
        P(),
        P(),
        P(),
        P(DOM, None, None),
        P(DOM, None, None),
        P(DOM),
        P(),
        P(DOM, None),
        P(DOM),
        P(DOM),
        P(DOM, None),
    )
    return jax.shard_map(
        body,
        mesh=torus,
        in_specs=placed,
        out_specs=(P(None, DOM), P(DOM), P(DOM, None)),
        check_vma=False,
    )
```

profile of v0, /device:TPU:1, one launch (start us, length us, event | category | flops | bytes accessed | tf_op | source)
XLA Modules:
  0.0 458.7 jit_solution(14156327603952337329)
XLA Ops:
  0.7 1.1 slice.95
  1.7 1.1 convolution_subtract_fusion.1
  2.9 1.2 fusion.10
  5.4 3.4 fusion.76
  8.7 3.4 fusion.41
  12.2 27.2 %scatter_custom_fusion = f32[16385]{0:T(1024)S(1)} fusion(s32[4096]{0:T(1024)S(1)} %get-tuple-element.26, f32[4096]{0:T(1024)S(1)} %get-tuple-element.27, f32[]{:T(128)} %constant.34.clone.1), kind=kCustom, calls=%fused_computation.77 | custom fusion | flops 4096 | bytes 65544 | tf_op jit(solution)/shard_map/scatter-add | solution.py:135
  39.4 4.6 %all_to_all.99 = f32[2,64,128]{2,1,0:T(8,128)S(1)} all-to-all(f32[2,64,128]{2,1,0:T(8,128)S(1)} %copy.33), channel_id=1, replica_groups=mesh['dom_0'=4,'dom_1'=4,'dom_2'=4,'dom_3'=2] {'dom_3'}, dimensions={0} | all-to-all | bytes 131072 | tf_op jit(solution)/shard_map/all_to_all | solution.py:26
  44.7 11.7 %all-to-all-start.1 = ((f32[64,1,128]{2,1,0:T(1,128)}), f32[64,1,128]{2,1,0:T(1,128)S(1)}, u32[]{:S(2)}, u32[]{:S(2)}) async-start(f32[64,1,128]{2,1,0:T(1,128)} %bitcast.23), calls=%async_computation.1 | async-start | bytes 65536 | tf_op jit(solution)/shard_map/all_to_all | solution.py:34
  56.3 3.4 fusion.77
  59.9 2.3 reduce-window.6
  63.1 1.7 all-to-all-done.1
  64.9 0.6 broadcast_in_dim.39
  65.5 8.2 %all-to-all-start.2 = ((f32[64,1,128]{2,1,0:T(1,128)}), f32[64,1,128]{2,1,0:T(1,128)S(1)}, u32[]{:S(2)}, u32[]{:S(2)}) async-start(f32[64,1,128]{2,1,0:T(1,128)} %broadcast_in_dim.39), calls=%async_computation.2 | async-start | bytes 65536 | tf_op jit(solution)/shard_map/all_to_all | solution.py:47
  74.5 7.6 %all-to-all-done.2 = f32[64,1,128]{2,1,0:T(1,128)S(1)} async-done(((f32[64,1,128]{2,1,0:T(1,128)}), f32[64,1,128]{2,1,0:T(1,128)S(1)}, u32[]{:S(2)}, u32[]{:S(2)}) %all-to-all-start.2) | async-done | bytes 32800 | tf_op jit(solution)/shard_map/all_to_all | solution.py:47
  82.1 5.8 %all_to_all.100 = f32[2,64,128]{2,1,0:T(8,128)S(1)} all-to-all(f32[2,64,128]{2,1,0:T(8,128)S(1)} %broadcast_in_dim.41), channel_id=1, replica_groups=mesh['dom_0'=4,'dom_1'=4,'dom_2'=4,'dom_3'=2] {'dom_3'}, dimensions={0} | all-to-all | bytes 131072 | tf_op jit(solution)/shard_map/all_to_all | solution.py:47
  88.0 23.0 %gather_fusion = f32[4096]{0:T(1024)S(1)} fusion(f32[16385]{0:T(1024)S(1)} %pad_maximum_fusion.3, s32[4096]{0:T(1024)S(1)} %get-tuple-element.25), kind=kCustom, calls=%fused_computation | custom fusion | bytes 49152 | tf_op jit(solution)/shard_map/gather | solution.py:138
  111.0 4.9 %fusion.78 = f32[32,1,128]{2,1,0:T(1,128)S(1)} fusion(f32[32,128,1]{1,2,0:T(1,128)S(1)} %bitcast.222, f32[32,128,128]{2,1,0:T(8,128)} %param.23), kind=kOutput, calls=%fused_computation.169 | convolution fusion | flops 6291456 | bytes 2129920 | tf_op jit(solution)/shard_map/tij,tj->ti/dot_general | solution.py:130
  116.0 27.2 %scatter_custom_fusion.1 = f32[16385]{0:T(1024)S(1)} fusion(s32[4096]{0:T(1024)S(1)} %get-tuple-element.26, f32[4096]{0:T(1024)S(1)} %bitcast.201, f32[]{:T(128)} %constant.34.clone.1), kind=kCustom, calls=%fused_computation.75 | custom fusion | flops 4096 | bytes 65544 | tf_op jit(solution)/shard_map/scatter-add | solution.py:135
  143.2 3.4 all_to_all.101
  146.7 1.2 broadcast_in_dim.51
  147.9 3.5 all-to-all-start.12
  152.4 4.9 %all-to-all-start.5 = ((f32[64,1,128]{2,1,0:T(1,128)}), f32[64,1,128]{2,1,0:T(1,128)S(1)}, u32[]{:S(2)}, u32[]{:S(2)}) async-start(f32[64,1,128]{2,1,0:T(1,128)} %bitcast.39), calls=%async_computation.5 | async-start | bytes 65536 | tf_op jit(solution)/shard_map/all_to_all | solution.py:34
  157.3 15.5 %scatter_custom_fusion.5 = f32[8192]{0:T(1024)S(1)} fusion(s32[4096]{0:T(1024)S(1)} %broadcast_select_fusion, f32[4096]{0:T(1024)S(1)} %convert_element_type.26, f32[]{:T(128)} %constant.34.clone.1), kind=kCustom, calls=%fused_computation.131 | custom fusion | bytes 32772
  173.5 0.6 broadcast_in_dim.43
  174.2 10.0 %all-to-all-start.6 = ((f32[64,1,128]{2,1,0:T(1,128)}), f32[64,1,128]{2,1,0:T(1,128)S(1)}, u32[]{:S(2)}, u32[]{:S(2)}) async-start(f32[64,1,128]{2,1,0:T(1,128)} %broadcast_in_dim.43), calls=%async_computation.6 | async-start | bytes 65536 | tf_op jit(solution)/shard_map/all_to_all | solution.py:47
  184.2 3.4 fusion.79
  187.5 5.1 %all-to-all-done.6 = f32[64,1,128]{2,1,0:T(1,128)S(1)} async-done(((f32[64,1,128]{2,1,0:T(1,128)}), f32[64,1,128]{2,1,0:T(1,128)S(1)}, u32[]{:S(2)}, u32[]{:S(2)}) %all-to-all-start.6) | async-done | bytes 32800 | tf_op jit(solution)/shard_map/all_to_all | solution.py:47
  192.6 5.8 %all_to_all.102 = f32[2,64,128]{2,1,0:T(8,128)S(1)} all-to-all(f32[2,64,128]{2,1,0:T(8,128)S(1)} %broadcast_in_dim.45), channel_id=1, replica_groups=mesh['dom_0'=4,'dom_1'=4,'dom_2'=4,'dom_3'=2] {'dom_3'}, dimensions={0} | all-to-all | bytes 131072 | tf_op jit(solution)/shard_map/all_to_all | solution.py:47
  198.5 23.0 %gather_fusion.1 = f32[4096]{0:T(1024)S(1)} fusion(f32[16385]{0:T(1024)S(1)} %pad_maximum_fusion.2, s32[4096]{0:T(1024)S(1)} %get-tuple-element.25), kind=kCustom, calls=%fused_computation.1 | custom fusion | bytes 49152 | tf_op jit(solution)/shard_map/gather | solution.py:138
  221.5 4.9 %fusion.80 = f32[32,1,128]{2,1,0:T(1,128)S(1)} fusion(f32[32,128,1]{1,2,0:T(1,128)S(1)} %bitcast.223, f32[32,128,128]{2,1,0:T(8,128)} %param.23), kind=kOutput, calls=%fused_computation.171 | convolution fusion | flops 6291456 | bytes 2129920 | tf_op jit(solution)/shard_map/tij,tj->ti/dot_general | solution.py:130
  226.5 27.2 %scatter_custom_fusion.2 = f32[16385]{0:T(1024)S(1)} fusion(s32[4096]{0:T(1024)S(1)} %get-tuple-element.26, f32[4096]{0:T(1024)S(1)} %bitcast_add_fusion.2, f32[]{:T(128)} %constant.34.clone.1), kind=kCustom, calls=%fused_computation.73 | custom fusion | flops 4096 | bytes 65544 | tf_op jit(solution)/shard_map/scatter-add | solution.py:135
  253.8 3.4 all_to_all.103
  257.8 4.9 %all-to-all-start.9 = ((f32[64,1,128]{2,1,0:T(1,128)}), f32[64,1,128]{2,1,0:T(1,128)S(1)}, u32[]{:S(2)}, u32[]{:S(2)}) async-start(f32[64,1,128]{2,1,0:T(1,128)} %bitcast.55), calls=%async_computation.9 | async-start | bytes 65536 | tf_op jit(solution)/shard_map/all_to_all | solution.py:34
  262.7 8.3 %all-to-all-done.9 = f32[64,1,128]{2,1,0:T(1,128)S(1)} async-done(((f32[64,1,128]{2,1,0:T(1,128)}), f32[64,1,128]{2,1,0:T(1,128)S(1)}, u32[]{:S(2)}, u32[]{:S(2)}) %all-to-all-start.9) | async-done | bytes 32800 | tf_op jit(solution)/shard_map/all_to_all | solution.py:34
  271.8 4.7 %all-to-all-start.10 = ((f32[64,1,128]{2,1,0:T(1,128)}), f32[64,1,128]{2,1,0:T(1,128)S(1)}, u32[]{:S(2)}, u32[]{:S(2)}) async-start(f32[64,1,128]{2,1,0:T(1,128)} %broadcast_in_dim.46), calls=%async_computation.10 | async-start | bytes 65536 | tf_op jit(solution)/shard_map/all_to_all | solution.py:47
  276.5 3.4 fusion.81
  279.8 5.0 %all-to-all-done.10 = f32[64,1,128]{2,1,0:T(1,128)S(1)} async-done(((f32[64,1,128]{2,1,0:T(1,128)}), f32[64,1,128]{2,1,0:T(1,128)S(1)}, u32[]{:S(2)}, u32[]{:S(2)}) %all-to-all-start.10) | async-done | bytes 32800 | tf_op jit(solution)/shard_map/all_to_all | solution.py:47
  284.8 6.6 %all_to_all.104 = f32[2,64,128]{2,1,0:T(8,128)S(1)} all-to-all(f32[2,64,128]{2,1,0:T(8,128)S(1)} %broadcast_in_dim.48), channel_id=1, replica_groups=mesh['dom_0'=4,'dom_1'=4,'dom_2'=4,'dom_3'=2] {'dom_3'}, dimensions={0} | all-to-all | bytes 131072 | tf_op jit(solution)/shard_map/all_to_all | solution.py:47
  291.5 1.3 broadcast_in_dim.52
  292.7 4.8 %all-to-all-start.13 = ((f32[64,1,1]{2,1,0:T(1,128)}), f32[64,1,1]{2,1,0:T(1,128)S(1)}, u32[]{:S(2)}, u32[]{:S(2)}) async-start(f32[64,1,1]{2,1,0:T(1,128)} %broadcast_in_dim.52), calls=%async_computation.13 | async-start | bytes 65536 | tf_op jit(solution)/shard_map/all_to_all | solution.py:47
  297.7 23.0 %gather_fusion.2 = f32[4096]{0:T(1024)S(1)} fusion(f32[16385]{0:T(1024)S(1)} %pad_maximum_fusion.1, s32[4096]{0:T(1024)S(1)} %get-tuple-element.25), kind=kCustom, calls=%fused_computation.2 | custom fusion | bytes 49152 | tf_op jit(solution)/shard_map/gather | solution.py:138
  320.8 4.9 %fusion.82 = f32[32,1,128]{2,1,0:T(1,128)S(1)} fusion(f32[32,128,1]{1,2,0:T(1,128)S(1)} %bitcast.239, f32[32,128,128]{2,1,0:T(8,128)} %param.23), kind=kOutput, calls=%fused_computation.173 | convolution fusion | flops 6291456 | bytes 2129920 | tf_op jit(solution)/shard_map/tij,tj->ti/dot_general | solution.py:130
  326.3 15.5 %scatter_custom_fusion.4 = f32[8192]{0:T(1024)S(1)} fusion(s32[4096]{0:T(1024)S(1)} %broadcast_select_fusion, f32[4096]{0:T(1024)S(1)} %get-tuple-element.5, f32[]{:T(128)} %constant.34.clone.1), kind=kCustom, calls=%fused_computation.133 | custom fusion | bytes 32772
  342.0 7.5 %collective-permute-start = (f32[2,1024]{1,0:T(2,128)S(1)}, f32[2,1024]{1,0:T(2,128)S(1)}, u32[]{:S(2)}, u32[]{:S(2)}) collective-permute-start(f32[2,1024]{1,0:T(2,128)S(1)} %get-tuple-element.12), channel_id=1, source_target_pairs={{0,125},{1,126},{2,127},{3,0},{4,1},{5,2},{6,3},{7,4},{8,5},{9,6},... | collective-permute-start | bytes 24584 | tf_op jit(solution)/shard_map/ppermute | solution.py:90
  349.4 0.7 reduce_min.29
  352.1 0.6 collective-permute-start.1
  352.8 0.6 collective-permute-start.2
  353.4 1.1 collective-permute-start.4
  354.5 0.9 collective-permute-start.5
  356.3 6.3 %collective-permute-done.5 = f32[2,1024]{1,0:T(2,128)S(1)} collective-permute-done((f32[2,1024]{1,0:T(2,128)S(1)}, f32[2,1024]{1,0:T(2,128)S(1)}, u32[]{:S(2)}, u32[]{:S(2)}) %collective-permute-start.5) | collective-permute-done | bytes 8224 | tf_op jit(solution)/shard_map/ppermute | solution.py:90
  362.6 1.6 collective-permute-done.6
  364.3 50.1 %scatter_custom_fusion.3 = f32[8192]{0:T(1024)S(1)} fusion(s32[8192]{0:T(1024)S(1)} %bitcast.244, f32[8192]{0:T(1024)S(1)} %bitcast.243, f32[]{:T(128)} %constant.34.clone.1), kind=kCustom, calls=%fused_computation.135 | custom fusion | flops 8192 | bytes 32772 | tf_op jit(solution)/shard_map/scatter-add | solution.py:202
  414.5 2.4 collective-permute-start.8
  416.9 3.2 collective-permute-start.9
  420.9 1.9 collective-permute-start.10
  422.9 4.2 collective-permute-start.11
  427.8 0.7 fusion.69
  428.6 0.6 broadcast_in_dim.53
  429.2 3.4 all_to_all.105
  433.2 1.3 broadcast_in_dim.54
  434.4 13.5 %all-to-all-start.15 = ((f32[64,1,1]{2,1,0:T(1,128)}), f32[64,1,1]{2,1,0:T(1,128)S(1)}, u32[]{:S(2)}, u32[]{:S(2)}) async-start(f32[64,1,1]{2,1,0:T(1,128)} %broadcast_in_dim.54), calls=%async_computation.15 | async-start | bytes 65536 | tf_op jit(solution)/shard_map/all_to_all | solution.py:47
  448.0 0.8 pad_maximum_fusion
  448.8 7.6 %all-to-all-done.15 = f32[64,1,1]{2,1,0:T(1,128)S(1)} async-done(((f32[64,1,1]{2,1,0:T(1,128)}), f32[64,1,1]{2,1,0:T(1,128)S(1)}, u32[]{:S(2)}, u32[]{:S(2)}) %all-to-all-start.15) | async-done | bytes 288 | tf_op jit(solution)/shard_map/all_to_all | solution.py:47
  456.3 0.7 reduce_sum.109
  (118 shorter events, 11.4 us)
Async XLA Ops:
  0.6 4.7 %copy-start = (f32[32,128,128]{2,1,0:T(8,128)S(1)}, f32[32,128,128]{2,1,0:T(8,128)}, u32[]{:S(2)}) copy-start(f32[32,128,128]{2,1,0:T(8,128)} %param.22) | copy-start | bytes 6291460
  0.6 3.4 copy-start.4
  0.7 3.4 copy-start.5
  0.7 3.4 copy-start.10
  2.8 1.7 copy-start.11
  2.8 2.1 copy-start.12
  4.1 4.6 %copy-start.1 = (f32[32,128,128]{2,1,0:T(8,128)S(1)}, f32[32,128,128]{2,1,0:T(8,128)}, u32[]{:S(2)}) copy-start(f32[32,128,128]{2,1,0:T(8,128)} %param.23) | copy-start | bytes 6291460
  5.4 6.8 %copy-start.6 = (s32[4096]{0:T(1024)S(1)}, s32[4096]{0:T(1024)}, u32[]{:S(2)}) copy-start(s32[4096]{0:T(1024)} %param.24) | copy-start | bytes 49156
  8.7 51.0 %copy-start.7 = (s32[4096,1]{0,1:T(1,128)S(1)}, s32[4096,1]{0,1:T(1,128)}, u32[]{:S(2)}) copy-start(s32[4096,1]{0,1:T(1,128)} %param.26) | copy-start | bytes 49156
  12.1 50.9 %copy-start.14 = (s32[2]{0:T(128)S(1)}, s32[2]{0:T(128)}, u32[]{:S(2)}) copy-start(s32[2]{0:T(128)} %constant.120) | copy-start | bytes 28
  12.1 61.6 %copy-start.13 = (s32[2]{0:T(128)S(1)}, s32[2]{0:T(128)}, u32[]{:S(2)}) copy-start(s32[2]{0:T(128)} %constant.117) | copy-start | bytes 28
  12.2 61.7 %copy-start.3 = (f32[64,128]{1,0:T(8,128)S(1)}, f32[64,128]{1,0:T(8,128)}, u32[]{:S(2)}) copy-start(f32[64,128]{1,0:T(8,128)} %param.29) | copy-start | bytes 98308
  39.4 48.5 %copy-start.2 = (f32[16384]{0:T(1024)S(1)}, f32[16384]{0:T(1024)}, u32[]{:S(2)}) copy-start(f32[16384]{0:T(1024)} %param.25) | copy-start | bytes 196612
  44.7 20.1 %all-to-all-start.1 = ((f32[64,1,128]{2,1,0:T(1,128)}), f32[64,1,128]{2,1,0:T(1,128)S(1)}, u32[]{:S(2)}, u32[]{:S(2)}) async-start(f32[64,1,128]{2,1,0:T(1,128)} %bitcast.23), calls=%async_computation.1 | async-start | bytes 65536 | tf_op jit(solution)/shard_map/all_to_all | solution.py:34
  65.5 16.6 %all-to-all-start.2 = ((f32[64,1,128]{2,1,0:T(1,128)}), f32[64,1,128]{2,1,0:T(1,128)S(1)}, u32[]{:S(2)}, u32[]{:S(2)}) async-start(f32[64,1,128]{2,1,0:T(1,128)} %broadcast_in_dim.39), calls=%async_computation.2 | async-start | bytes 65536 | tf_op jit(solution)/shard_map/all_to_all | solution.py:47
  111.0 46.3 %copy-start.9 = (s32[4096]{0:T(1024)S(1)}, s32[4096]{0:T(1024)}, u32[]{:S(2)}) copy-start(s32[4096]{0:T(1024)} %param.27) | copy-start | bytes 49156
  147.9 4.5 all-to-all-start.12
  152.4 21.1 %all-to-all-start.5 = ((f32[64,1,128]{2,1,0:T(1,128)}), f32[64,1,128]{2,1,0:T(1,128)S(1)}, u32[]{:S(2)}, u32[]{:S(2)}) async-start(f32[64,1,128]{2,1,0:T(1,128)} %bitcast.39), calls=%async_computation.5 | async-start | bytes 65536 | tf_op jit(solution)/shard_map/all_to_all | solution.py:34
  174.2 18.5 %all-to-all-start.6 = ((f32[64,1,128]{2,1,0:T(1,128)}), f32[64,1,128]{2,1,0:T(1,128)S(1)}, u32[]{:S(2)}, u32[]{:S(2)}) async-start(f32[64,1,128]{2,1,0:T(1,128)} %broadcast_in_dim.43), calls=%async_computation.6 | async-start | bytes 65536 | tf_op jit(solution)/shard_map/all_to_all | solution.py:47
  257.8 13.2 %all-to-all-start.9 = ((f32[64,1,128]{2,1,0:T(1,128)}), f32[64,1,128]{2,1,0:T(1,128)S(1)}, u32[]{:S(2)}, u32[]{:S(2)}) async-start(f32[64,1,128]{2,1,0:T(1,128)} %bitcast.55), calls=%async_computation.9 | async-start | bytes 65536 | tf_op jit(solution)/shard_map/all_to_all | solution.py:34
  271.8 13.0 %all-to-all-start.10 = ((f32[64,1,128]{2,1,0:T(1,128)}), f32[64,1,128]{2,1,0:T(1,128)S(1)}, u32[]{:S(2)}, u32[]{:S(2)}) async-start(f32[64,1,128]{2,1,0:T(1,128)} %broadcast_in_dim.46), calls=%async_computation.10 | async-start | bytes 65536 | tf_op jit(solution)/shard_map/all_to_all | solution.py:47
  292.7 56.7 %all-to-all-start.13 = ((f32[64,1,1]{2,1,0:T(1,128)}), f32[64,1,1]{2,1,0:T(1,128)S(1)}, u32[]{:S(2)}, u32[]{:S(2)}) async-start(f32[64,1,1]{2,1,0:T(1,128)} %broadcast_in_dim.52), calls=%async_computation.13 | async-start | bytes 65536 | tf_op jit(solution)/shard_map/all_to_all | solution.py:47
  320.7 5.0 %copy-start.8 = (f32[4096]{0:T(1024)S(1)}, f32[4096]{0:T(1024)}, u32[]{:S(2)}) copy-start(f32[4096]{0:T(1024)} %param.28) | copy-start | bytes 49156
  342.0 12.6 %collective-permute-start = (f32[2,1024]{1,0:T(2,128)S(1)}, f32[2,1024]{1,0:T(2,128)S(1)}, u32[]{:S(2)}, u32[]{:S(2)}) collective-permute-start(f32[2,1024]{1,0:T(2,128)S(1)} %get-tuple-element.12), channel_id=1, source_target_pairs={{0,125},{1,126},{2,127},{3,0},{4,1},{5,2},{6,3},{7,4},{8,5},{9,6},... | collective-permute-start | bytes 24584 | tf_op jit(solution)/shard_map/ppermute | solution.py:90
  352.1 3.3 collective-permute-start.1
  352.8 3.2 collective-permute-start.2
  353.4 2.9 collective-permute-start.3
  353.4 2.9 collective-permute-start.4
  354.5 8.1 %collective-permute-start.5 = (f32[2,1024]{1,0:T(2,128)S(1)}, f32[2,1024]{1,0:T(2,128)S(1)}, u32[]{:S(2)}, u32[]{:S(2)}) collective-permute-start(f32[2,1024]{1,0:T(2,128)S(1)} %get-tuple-element.17), channel_id=1, source_target_pairs={{0,2},{1,3},{2,4},{3,5},{4,6},{5,7},{6,8},{7,9},{8,10},{9,11},{10,... | collective-permute-start | bytes 24584 | tf_op jit(solution)/shard_map/ppermute | solution.py:90
  355.4 8.8 %collective-permute-start.6 = (f32[2,1024]{1,0:T(2,128)S(1)}, f32[2,1024]{1,0:T(2,128)S(1)}, u32[]{:S(2)}, u32[]{:S(2)}) collective-permute-start(f32[2,1024]{1,0:T(2,128)S(1)} %get-tuple-element.18), channel_id=1, source_target_pairs={{0,3},{1,4},{2,5},{3,6},{4,7},{5,8},{6,9},{7,10},{8,11},{9,12},{10... | collective-permute-start | bytes 24584 | tf_op jit(solution)/shard_map/ppermute | solution.py:90
  355.9 8.3 %collective-permute-start.7 = (f32[2,1024]{1,0:T(2,128)S(1)}, f32[2,1024]{1,0:T(2,128)S(1)}, u32[]{:S(2)}, u32[]{:S(2)}) collective-permute-start(f32[2,1024]{1,0:T(2,128)S(1)} %get-tuple-element.11), channel_id=1, source_target_pairs={{0,64},{1,65},{2,66},{3,67},{4,68},{5,69},{6,70},{7,71},{8,72},{9,... | collective-permute-start | bytes 24584 | tf_op jit(solution)/shard_map/ppermute | solution.py:90
  414.5 5.7 %collective-permute-start.8 = (f32[1,128]{1,0:T(1,128)S(1)}, f32[1,128]{1,0:T(1,128)S(1)}, u32[]{:S(2)}, u32[]{:S(2)}) collective-permute-start(f32[1,128]{1,0:T(1,128)S(1)} %get-tuple-element.22), channel_id=1, source_target_pairs={{1,0},{2,1},{3,2},{4,3},{5,4},{6,5},{7,6},{8,7},{9,8},{10,9},{11,1... | collective-permute-start | bytes 1544 | tf_op jit(solution)/shard_map/ppermute | solution.py:81
  416.9 3.9 collective-permute-start.9
  420.9 6.2 %collective-permute-start.10 = (f32[1,128]{1,0:T(1,128)S(1)}, f32[1,128]{1,0:T(1,128)S(1)}, u32[]{:S(2)}, u32[]{:S(2)}) collective-permute-start(f32[1,128]{1,0:T(1,128)S(1)} %get-tuple-element.20), channel_id=1, source_target_pairs={{1,0},{2,1},{3,2},{4,3},{5,4},{6,5},{7,6},{8,7},{9,8},{10,9},{11,1... | collective-permute-start | bytes 1544 | tf_op jit(solution)/shard_map/ppermute | solution.py:81
  422.9 4.9 %collective-permute-start.11 = (f32[1,128]{1,0:T(1,128)S(1)}, f32[1,128]{1,0:T(1,128)S(1)}, u32[]{:S(2)}, u32[]{:S(2)}) collective-permute-start(f32[1,128]{1,0:T(1,128)S(1)} %get-tuple-element.19), channel_id=1, source_target_pairs={{0,1},{1,2},{2,3},{3,4},{4,5},{5,6},{6,7},{7,8},{8,9},{9,10},{10,1... | collective-permute-start | bytes 1544 | tf_op jit(solution)/shard_map/ppermute | solution.py:79
  434.4 21.9 %all-to-all-start.15 = ((f32[64,1,1]{2,1,0:T(1,128)}), f32[64,1,1]{2,1,0:T(1,128)S(1)}, u32[]{:S(2)}, u32[]{:S(2)}) async-start(f32[64,1,1]{2,1,0:T(1,128)} %broadcast_in_dim.54), calls=%async_computation.15 | async-start | bytes 65536 | tf_op jit(solution)/shard_map/all_to_all | solution.py:47
where the time goes:
time: 467 us; the launch traced here: 459 us
  other arithmetic  144 us (31%)
  local copies, waits for them, and re-layouts  108 us (23%)
  starting transfers between devices  89.4 us (19%)
  waiting for transfers between devices  44.7 us (10%)
  matrix products  35.1 us (8%)
  blocking collectives  33 us (7%)
  between operations  4.74 us (1%)
    scatter-add x3, other arithmetic, couple(): jax.ops.segment_sum(field, slot_index, num_segments=count + 1)[:count]  81.7 us
    gather x3, local copies, waits for them, and re-layouts, couple(): return extended[slot_index]  69.1 us
    scatter-add x1, other arithmetic, body(): jax.ops.segment_sum(arrived[:, 0].reshape(-1), arrived[:, 1].reshape(-1)....  50.1 us
    all_to_all x6, starting transfers between devices, sent_to_all(): lax.all_to_all(jnp.broadcast_to(x[None], (peers, *x.shape)), axis, 0, 0,...  44.8 us
    dot_general x8, matrix products, tile_apply(): jnp.einsum('tij,tj->ti', mats, field.reshape(-1, 128), precision=highest)  31.6 us
    unnamed x39, local copies, waits for them, and re-layouts  31.2 us
    all_to_all x6, waiting for transfers between devices, sent_to_all(): lax.all_to_all(jnp.broadcast_to(x[None], (peers, *x.shape)), axis, 0, 0,...  25.6 us
    all_to_all x4, blocking collectives, sent_to_all(): lax.all_to_all(jnp.broadcast_to(x[None], (peers, *x.shape)), axis, 0, 0,...  21.5 us
  transfers between devices with their start and end apart: 21, of which 11 were waited for; matrix products, arithmetic and copies ran while one was open for 17% of the time, Pallas kernels for 0%

commit v1 on v0

v1 whole, which is shorter than its diff:
```python
import jax
import jax.numpy as jnp
from jax import lax
from jax.experimental import pallas as pl
from jax.experimental.pallas import tpu as pltpu
from jax.sharding import Mesh
from jax.sharding import PartitionSpec as P

ITERS_H = 3
AXES = ("a", "b", "c", "d")
TIME_STEP = 0.2
CENTER = 2.5
HALF = 1.5
SIGMA = CENTER / HALF
F32 = jnp.float32
BF16 = jnp.bfloat16
TILES = 32
LANES = 128
SLOT_ROWS = 128
PAYLOAD = 136
TORSO = 64


def chebyshev_factors(count):
    ratio = 1.0 / SIGMA
    factors = []
    for _ in range(count):
        following = 1.0 / (2.0 * SIGMA - ratio)
        factors.append((following * ratio, 2.0 * following / HALF))
        ratio = following
    return factors


FACTORS = chebyshev_factors(ITERS_H)


def high_low(x):
    high = x.astype(BF16).astype(F32)
    return high, x - high


def tile_products(mats, x_ref, out_ref):
    lane = lax.broadcasted_iota(jnp.int32, (LANES, LANES), 1)
    columns = jnp.zeros((LANES, LANES), F32)
    for t in range(TILES):
        summed = jnp.sum(mats[t] * x_ref[t : t + 1, :], axis=1, keepdims=True)
        columns = jnp.where(lane == t, summed, columns)
    out_ref[...] = jnp.transpose(columns)[:TILES, :]


def slot_sums(slots_ref, w_ref, row_ref, col_ref):
    down = lax.broadcasted_iota(jnp.int32, (LANES, LANES), 0)
    for t in range(TILES):
        here = slice(t * LANES, (t + 1) * LANES)
        slot = slots_ref[t : t + 1, :]
        high, low = high_low(w_ref[t : t + 1, :])
        match = down == (slot >> 7)
        row_ref[0:LANES, here] = jnp.where(match, high, 0.0).astype(BF16)
        row_ref[LANES:, here] = jnp.where(match, low, 0.0).astype(BF16)
        col_ref[:, here] = jnp.where(down == (slot & 127), 1.0, 0.0).astype(BF16)
    both = lax.dot_general(
        row_ref[...], col_ref[...], (((1,), (1,)), ((), ())), preferred_element_type=F32
    )
    return both[:LANES] + both[LANES:]


def slot_values(slots_ref, values, pick_ref, out_ref):
    down = lax.broadcasted_iota(jnp.int32, (LANES, LANES), 0)
    high, low = high_low(jnp.transpose(values))
    table = jnp.concatenate([high.astype(BF16), low.astype(BF16)], axis=1)
    for t in range(TILES):
        here = slice(t * LANES, (t + 1) * LANES)
        match = jnp.where(down == (slots_ref[t : t + 1, :] >> 7), 1.0, 0.0).astype(BF16)
        pick_ref[0:LANES, here] = match
        pick_ref[LANES:, here] = match
    for t in range(TILES):
        here = slice(t * LANES, (t + 1) * LANES)
        rows = jnp.dot(table, pick_ref[:, here], preferred_element_type=F32)
        chosen = jnp.where(down == (slots_ref[t : t + 1, :] & 127), rows, 0.0)
        out_ref[t : t + 1, :] = jnp.sum(chosen, axis=0, keepdims=True)


def ionic_kernel(
    states_hbm, region_hbm, half_hbm, slope_hbm, rate_hbm, cond_hbm, rev_hbm,
    slots_hbm, conduct_hbm, gain_hbm, stiff_hbm, precond_hbm,
    states_out, resid_out, update_out, payload_out, slots_out, gain_out, stiff_out, precond_out,
    states_ref, region_ref, half_ref, slope_ref, rate_ref, cond_ref, rev_ref,
    conduct_ref, table_ref, volt_ref, row_ref, col_ref, sems,
):
    pairs = (
        (half_hbm, half_ref), (slope_hbm, slope_ref), (rate_hbm, rate_ref), (cond_hbm, cond_ref),
        (rev_hbm, rev_ref), (region_hbm, region_ref), (states_hbm, states_ref),
        (slots_hbm, slots_out), (conduct_hbm, conduct_ref),
        (stiff_hbm, stiff_out), (precond_hbm, precond_out), (gain_hbm, gain_out),
    )
    copies = [pltpu.make_async_copy(x, y, sems.at[k]) for k, (x, y) in enumerate(pairs)]
    for copy in copies:
        copy.start()
    table_ref[...] = jnp.zeros_like(table_ref)
    for copy in copies[:7]:
        copy.wait()
    for k, ref in enumerate((half_ref, slope_ref, rate_ref, cond_ref, rev_ref)):
        table_ref[8 * k : 8 * k + 3, 0:18] = ref[...]
    tables = jnp.transpose(pltpu.roll(table_ref[...], 1, 1))[:24]
    row = lax.broadcasted_iota(jnp.int32, (24, 1), 0)

    def column(k, r):
        return tables[:, 8 * k + r : 8 * k + r + 1]

    half = [column(0, r) for r in range(3)]
    gain = [1.0 / jnp.where((row == 0) | (row > 18), 1.0, column(1, r)) for r in range(3)]
    decay = [jnp.exp(-column(2, r)) for r in range(3)]
    cond = [column(3, r) for r in range(3)]
    rev = [column(4, r) for r in range(3)]
    first = lax.broadcasted_iota(jnp.int32, (19, LANES), 0) == 0
    for t in range(TILES):
        here = slice(t * LANES, (t + 1) * LANES)
        old = states_ref[:, here]
        volt = old[0:1, :]
        region = region_ref[t : t + 1, :]

        def lookup(choices):
            a, b, c = (x[:19] for x in choices)
            return jnp.where(region == 0, a, jnp.where(region == 1, b, c))

        target = 1.0 / (1.0 + jnp.exp((lookup(half) - volt) * lookup(gain)))
        gates = target + (old - target) * lookup(decay)
        flow = lookup(cond) * gates * (volt - lookup(rev))
        current = jnp.sum(jnp.where(first, 0.0, flow), axis=0, keepdims=True)
        new_volt = volt - TIME_STEP * current
        states_out[:, here] = jnp.where(first, new_volt, gates)
        volt_ref[t : t + 1, :] = new_volt
    for copy in copies[7:9]:
        copy.wait()
    payload_out[SLOT_ROWS:, :] = jnp.min(conduct_ref[...].reshape(8, 8, LANES), axis=0)
    copies[9].wait()
    tile_products(stiff_out, volt_ref, resid_out)
    copies[10].wait()
    tile_products(precond_out, resid_out, update_out)
    copies[11].wait()
    update_out[...] = update_out[...] * (1.0 / CENTER)
    payload_out[0:SLOT_ROWS, :] = slot_sums(slots_out, update_out, row_ref, col_ref)


def heart_step(
    index, payload_ref, gain_ref, slots_ref, stiff_ref, precond_ref, resid_ref, update_ref,
    potential_ref, coupled_ref, work_ref, pick_ref, resid_out, update_out, potential_out,
):
    slot_values(slots_ref, gain_ref[...] * payload_ref[0:SLOT_ROWS, :], pick_ref, coupled_ref)
    tile_products(stiff_ref, update_ref, work_ref)
    resid = resid_ref[...] - (work_ref[...] + coupled_ref[...])
    resid_out[...] = resid
    tile_products(precond_ref, resid_out, work_ref)
    keep, add = FACTORS[index]
    update = keep * update_ref[...] + add * work_ref[...]
    update_out[...] = update
    potential_out[...] = potential_ref[...] + update


def torso_solve(source_ref, conduct_ref, smallest, at_top, at_bottom):
    rows = TORSO + 16
    low = smallest / (4.0 + smallest)
    high = (8.0 + smallest) / (4.0 + smallest)
    center = (high + low) / 2.0
    half = (high - low) / 2.0
    sigma = center / half
    down = lax.broadcasted_iota(jnp.int32, (rows, LANES), 0)
    across = lax.broadcasted_iota(jnp.int32, (rows, LANES), 1)
    inside = ((down >= 8) | jnp.logical_not(at_top)) & ((down < 8 + TORSO) | jnp.logical_not(at_bottom))
    inside = inside & (down >= 6) & (down < 10 + TORSO)
    diagonal = 4.0 + conduct_ref
    inverse = 1.0 / diagonal

    def apply(u):
        u = jnp.where(inside, u, 0.0)
        up = pltpu.roll(u, 1, 0)
        dn = pltpu.roll(u, rows - 1, 0)
        left = jnp.where(across == 0, 0.0, pltpu.roll(u, 1, 1))
        right = jnp.where(across == LANES - 1, 0.0, pltpu.roll(u, LANES - 1, 1))
        return diagonal * u - (up + dn + left + right)

    resid = source_ref
    update = resid * inverse / center
    field = update
    ratio = 1.0 / sigma
    for _ in range(2):
        resid = resid - apply(update)
        following = 1.0 / (2.0 * sigma - ratio)
        update = following * ratio * update + 2.0 * following / half * (resid * inverse)
        field = field + update
        ratio = following
    return field


def first_step_kernel(
    here_ref, payload_ref, gain_ref, slots_ref, stiff_ref, precond_ref, resid_ref, update_ref, conduct_ref,
    resid_out, update_out, potential_out, payload_out, weight_out, smallest_out,
    coupled_ref, work_ref, pick_ref, row_ref, col_ref,
):
    heart_step(
        0, payload_ref, gain_ref, slots_ref, stiff_ref, precond_ref, resid_ref, update_ref,
        update_ref, coupled_ref, work_ref, pick_ref, resid_out, update_out, potential_out,
    )
    payload_out[...] = slot_sums(slots_ref, update_out, row_ref, col_ref)
    smallest = jnp.min(jnp.min(payload_ref[SLOT_ROWS:, :], axis=0, keepdims=True), axis=1, keepdims=True)
    smallest_out[...] = jnp.broadcast_to(smallest, (8, LANES))
    ones = jnp.ones((TORSO + 16, LANES), F32)
    field = torso_solve(
        ones, conduct_ref[...], smallest, here_ref[0] == 0, here_ref[0] == here_ref[1] - 1
    )
    weight_out[...] = field[8 : 8 + TORSO]


def second_step_kernel(
    payload_ref, gain_ref, slots_ref, stiff_ref, precond_ref, resid_ref, update_ref, potential_ref,
    resid_out, update_out, potential_out, payload_out,
    coupled_ref, work_ref, pick_ref, row_ref, col_ref,
):
    heart_step(
        1, payload_ref, gain_ref, slots_ref, stiff_ref, precond_ref, resid_ref, update_ref,
        potential_ref, coupled_ref, work_ref, pick_ref, resid_out, update_out, potential_out,
    )
    payload_out[...] = slot_sums(slots_ref, update_out, row_ref, col_ref)


def last_step_kernel(
    here_ref, payload_ref, gain_ref, slots_ref, stiff_ref, precond_ref, resid_ref, update_ref,
    potential_ref, owner_ref, cell_ref, scale_ref,
    potential_out, own_out, across_out, far_out, partner_out, next_out,
    coupled_ref, work_ref, pick_ref, resid_out, update_out, row_ref, col_ref,
):
    heart_step(
        2, payload_ref, gain_ref, slots_ref, stiff_ref, precond_ref, resid_ref, update_ref,
        potential_ref, coupled_ref, work_ref, pick_ref, resid_out, update_out, potential_out,
    )
    devices = here_ref[1]
    me = here_ref[0]
    ahead = owner_ref[...] - me + devices
    ahead = jnp.where(lax.rem(me, 2) == 1, ahead, 2 * devices - ahead)
    ahead = lax.rem(ahead, devices)
    kind = jnp.where(ahead == devices // 2, 1, 0)
    for k, value in ((2, 3), (3, devices - 1), (4, devices - 3), (5, devices - 2), (6, 2), (7, 1)):
        kind = jnp.where(ahead == value, k, kind)
    cell = cell_ref[...]
    row = (kind & 3) * TORSO + (cell >> 7)
    col = (kind >> 2) * LANES + (cell & 127)
    deposit = potential_out[...] * scale_ref[...]
    down = lax.broadcasted_iota(jnp.int32, (256, LANES), 0)
    for t in range(TILES):
        here = slice(t * LANES, (t + 1) * LANES)
        high, low = high_low(deposit[t : t + 1, :])
        match = down == row[t : t + 1, :]
        row_ref[0:256, here] = jnp.where(match, high, 0.0).astype(BF16)
        row_ref[256:, here] = jnp.where(match, low, 0.0).astype(BF16)
        col_ref[:, here] = jnp.where(down == col[t : t + 1, :], 1.0, 0.0).astype(BF16)
    both = lax.dot_general(
        row_ref[...], col_ref[...], (((1,), (1,)), ((), ())), preferred_element_type=F32
    )
    both = both[:256] + both[256:]

    def deposited(k):
        return both[(k % 4) * TORSO : (k % 4 + 1) * TORSO, (k // 4) * LANES : (k // 4 + 1) * LANES]

    own_out[...] = deposited(0)
    across_out[...] = deposited(1)
    far_out[...] = deposited(2)
    for k in range(3):
        partner_out[k * TORSO : (k + 1) * TORSO, :] = deposited(3 + k)
    for k in range(2):
        next_out[k * TORSO : (k + 1) * TORSO, :] = deposited(6 + k)


def source_kernel(
    here_ref, weight_ref, own_ref, across_ref, far_ref, partner_ref, next_ref, handed_ref,
    source_out, block_out,
):
    source = own_ref[...] + across_ref[...] + far_ref[...] + partner_ref[0:TORSO]
    source = source + next_ref[0:TORSO] + handed_ref[...]
    source_out[...] = source
    share = jnp.sum(jnp.sum(source * weight_ref[...], axis=0, keepdims=True), axis=1, keepdims=True)
    block_out[:, 0:LANES] = jnp.broadcast_to(share, (block_out.shape[0], LANES))
    peer = lax.broadcasted_iota(jnp.int32, (block_out.shape[0], LANES), 0)
    me = here_ref[0]
    for k in range(2):
        behind = jnp.where(peer == me - 1, source[k : k + 1], 0.0)
        ahead = jnp.where(peer == me + 1, source[TORSO - 2 + k : TORSO - 1 + k], behind)
        block_out[:, (1 + k) * LANES : (2 + k) * LANES] = ahead


def field_kernel(here_ref, block_ref, source_ref, conduct_ref, smallest_ref, out_ref, wide_ref):
    me = here_ref[0]
    devices = block_ref.shape[0]
    total = jnp.sum(jnp.sum(block_ref[:, 0:1], axis=0, keepdims=True), axis=1, keepdims=True)
    peer = lax.broadcasted_iota(jnp.int32, (devices, LANES), 0)
    wide_ref[...] = jnp.zeros_like(wide_ref)
    wide_ref[8 : 8 + TORSO, :] = source_ref[...]
    for k in range(2):
        rows = block_ref[:, (1 + k) * LANES : (2 + k) * LANES]
        above = jnp.sum(jnp.where(peer == me - 1, rows, 0.0), axis=0, keepdims=True)
        below = jnp.sum(jnp.where(peer == me + 1, rows, 0.0), axis=0, keepdims=True)
        wide_ref[6 + k : 7 + k, :] = above
        wide_ref[8 + TORSO + k : 9 + TORSO + k, :] = below
    field = torso_solve(
        wide_ref[...], conduct_ref[...], smallest_ref[0:1, 0:1], me == 0, me == devices - 1
    )
    out_ref[...] = field[8 : 8 + TORSO] - total * (1.0 / (devices * TORSO * LANES))


def call(kernel, outs, scratch, smem, flops, args, space=pltpu.VMEM):
    spec = [pl.BlockSpec(memory_space=pltpu.SMEM)] * smem
    if space == pltpu.HBM:
        args = [pltpu.with_memory_space_constraint(x, space) for x in args]
    spec += [pl.BlockSpec(memory_space=space)] * (len(args) - smem)
    return pl.pallas_call(
        kernel,
        out_shape=[s if isinstance(s, jax.ShapeDtypeStruct) else jax.ShapeDtypeStruct(s, F32) for s in outs],
        in_specs=spec,
        out_specs=[pl.BlockSpec(memory_space=pltpu.VMEM)] * len(outs),
        scratch_shapes=scratch,
        compiler_params=pltpu.CompilerParams(vmem_limit_bytes=16 * 1024 * 1024),
        cost_estimate=pl.CostEstimate(flops=flops, bytes_accessed=1 << 20, transcendentals=0),
    )(*args)


def place(i):
    return [i // 32, (i // 8) % 4, (i // 2) % 4, i % 2]


def index(c):
    return ((c[0] * 4 + c[1]) * 4 + c[2]) * 2 + c[3]


def permuted(x, move):
    return lax.ppermute(x, AXES, [(i, index(move(place(i)))) for i in range(128)])


def other_core(c):
    return c[:3] + [1 - c[3]]


def shifted(axis, by):
    def move(c):
        c = list(c)
        c[axis] = (c[axis] + by) % 4
        return c

    return move


def combined(parts, rows):
    total = parts[0]
    for part in parts[1:]:
        total = total + part
    if rows == SLOT_ROWS:
        return total
    least = parts[0]
    for part in parts[1:]:
        least = jnp.minimum(least, part)
    line = lax.broadcasted_iota(jnp.int32, total.shape, 0)
    return jnp.where(line < SLOT_ROWS, total, least)


def over_all(x):
    rows = x.shape[0]
    x = combined([x, permuted(x, other_core)], rows)
    for axis in range(3):
        x = combined([x] + [permuted(x, shifted(axis, k)) for k in (2, 1, 3)], rows)
    return x


def from_behind(x, by, count):
    return lax.ppermute(x, AXES, [(i, (i + by) % count) for i in range(count)])


def body(
    states, region, half_volt, slopes, rates, conductance, reversal, stiffness, preconditioner,
    slots, slot_gain, owner, cell, source_gain, torso_conduct,
):
    devices = lax.axis_size(AXES)
    here = lax.axis_index(AXES)
    node = (TILES, LANES)
    tile = (TORSO, LANES)
    grid = (SLOT_ROWS, LANES)
    region, slots, owner, cell, source_gain = (
        x.reshape(node) for x in (region, slots, owner, cell, source_gain)
    )
    gain = slot_gain.reshape(grid)
    whom = jnp.stack([here, jnp.int32(devices)]).astype(jnp.int32)
    mats = stiffness.shape
    rowspace = pltpu.VMEM((256, 4096), BF16)
    colspace = pltpu.VMEM((128, 4096), BF16)
    nodespace = pltpu.VMEM(node, F32)
    pickspace = pltpu.VMEM((256, 4096), BF16)
    tablespace = pltpu.VMEM((3, 18), F32)
    indexspace = pltpu.VMEM(node, jnp.int32)

    new_states, resid, update, payload, slots, gain, stiffness, preconditioner = call(
        ionic_kernel,
        [states.shape, node, node, (PAYLOAD, LANES), jax.ShapeDtypeStruct(node, jnp.int32), grid, mats, mats],
        [pltpu.VMEM(states.shape, F32), indexspace] + [tablespace] * 5
        + [pltpu.VMEM(tile, F32), pltpu.VMEM((128, 128), F32), nodespace, rowspace,
           colspace, pltpu.SemaphoreType.DMA((12,))],
        0, 40000000,
        (states, region, half_volt, slopes, rates, conductance, reversal, slots, torso_conduct,
         gain, stiffness, preconditioner),
        pltpu.HBM,
    )
    above = from_behind(torso_conduct[TORSO - 8 :], 1, devices)
    below = from_behind(torso_conduct[:8], -1, devices)
    conduct = jnp.concatenate([above, torso_conduct, below], axis=0)
    payload = over_all(payload)
    resid, update, potential, payload, weight, smallest = call(
        first_step_kernel,
        [node, node, node, grid, tile, (8, LANES)],
        [nodespace, nodespace, pickspace, rowspace, colspace],
        1, 40000000,
        (whom, payload, gain, slots, stiffness, preconditioner, resid, update, conduct),
    )
    payload = over_all(payload)
    resid, update, potential, payload = call(
        second_step_kernel,
        [node, node, node, grid],
        [nodespace, nodespace, pickspace, rowspace, colspace],
        0, 40000000,
        (payload, gain, slots, stiffness, preconditioner, resid, update, potential),
    )
    payload = over_all(payload)
    potential, own, across, far, partner, nearby = call(
        last_step_kernel,
        [node, tile, tile, tile, (3 * TORSO, LANES), (2 * TORSO, LANES)],
        [nodespace, nodespace, pickspace, nodespace, nodespace,
         pltpu.VMEM((512, 4096), BF16), pltpu.VMEM((256, 4096), BF16)],
        1, 40000000,
        (whom, payload, gain, slots, stiffness, preconditioner, resid, update, potential,
         owner, cell, source_gain),
    )
    partner = permuted(partner, other_core)
    far = lax.ppermute(far, AXES, [(i, (i + 3 if i % 2 else i - 3) % devices) for i in range(devices)])
    across = from_behind(across, devices // 2, devices)
    nearby = lax.ppermute(
        nearby + partner[TORSO:], AXES, [(i, (i + 2 if i % 2 else i - 2) % devices) for i in range(devices)]
    )
    handed = permuted(nearby[TORSO:], other_core)
    source, blocks = call(
        source_kernel,
        [tile, (devices, 3 * LANES)],
        [], 1, 1000000,
        (whom, weight, own, across, far, partner, nearby, handed),
    )
    blocks = lax.all_to_all(blocks, AXES, 0, 0, tiled=True)
    (grounded,) = call(
        field_kernel, [tile], [pltpu.VMEM((TORSO + 16, LANES), F32)], 1, 4000000,
        (whom, blocks, source, conduct, smallest),
    )
    return new_states, potential.reshape(-1), grounded


def solution(mesh):
    torus = Mesh(mesh.devices.reshape(4, 4, 4, 2), AXES)
    dom = P(AXES)
    placed = (
        P(None, AXES), dom, P(), P(), P(), P(), P(), P(AXES, None, None), P(AXES, None, None),
        dom, P(), P(AXES, None), dom, dom, P(AXES, None),
    )
    return jax.shard_map(
        body, mesh=torus, in_specs=placed, out_specs=(P(None, AXES), dom, P(AXES, None)), check_vma=False
    )
```

time: 467 us -> 152 us (0.33); the launches traced: 459 us -> 151 us
  other arithmetic: 144 us -> 0.58 us
  local copies, waits for them, and re-layouts: 108 us -> 3.87 us
  matrix products: 35.1 us -> 0 us
  starting transfers between devices: 89.4 us -> 58.8 us
  Pallas kernels: 0 us -> 19.7 us
  blocking collectives: 33 us -> 19.7 us
    scatter-add x4 -> x0, other arithmetic: 132 us -> none  [the longest x3 81.7 us: couple(): jax.ops.segment_sum(field, slot_index, num_segments=count + 1)[:count]]
    gather x3 -> x0, local copies, waits for them, and re-layouts: 69.1 us -> none  [couple(): return extended[slot_index]]
    all_to_all x9 -> x0, starting transfers between devices: 66.2 us -> none  [the longest x6 44.8 us: sent_to_all(): lax.all_to_all(jnp.broadcast_to(x[None], (peers, *x.shape)), axis, 0, 0,...]
    ppermute x12 -> x37, waiting for transfers between devices: 9.05 us -> 47.9 us  [the longest x32 42.2 us: permuted(): lax.ppermute(x, AXES, [(i, index(move(place(i)))) for i in range(128)])]
    all_to_all x9 -> x0, waiting for transfers between devices: 35.7 us -> none  [the longest x6 25.6 us: sent_to_all(): lax.all_to_all(jnp.broadcast_to(x[None], (peers, *x.shape)), axis, 0, 0,...]
    ppermute x12 -> x37, starting transfers between devices: 23.3 us -> 58.8 us  [the longest x32 53 us: permuted(): lax.ppermute(x, AXES, [(i, index(move(place(i)))) for i in range(128)])]
    dot_general x13 -> x0, matrix products: 35.1 us -> none  [the longest x8 31.6 us: tile_apply(): jnp.einsum('tij,tj->ti', mats, field.reshape(-1, 128), precision=highest)]
    unnamed x39 -> x15, local copies, waits for them, and re-layouts: 31.2 us -> 2.96 us
  transfers between devices with their start and end apart: 21 -> 37, of which waited for: 11 -> 26; matrix products, arithmetic and copies ran while one was open for 17% -> 0% of each run, Pallas kernels for 0% -> 3%
where the time goes in v1:
time: 152 us; the launch traced here: 151 us
  starting transfers between devices  58.8 us (39%)
  waiting for transfers between devices  47.9 us (32%)
  Pallas kernels  19.7 us (13%)
  blocking collectives  19.7 us (13%)
  local copies, waits for them, and re-layouts  3.87 us (3%)
    ppermute x32, starting transfers between devices, permuted(): lax.ppermute(x, AXES, [(i, index(move(place(i)))) for i in range(128)])  53 us
    ppermute x32, waiting for transfers between devices, permuted(): lax.ppermute(x, AXES, [(i, index(move(place(i)))) for i in range(128)])  42.2 us
    all_to_all x1, blocking collectives, body(): blocks = lax.all_to_all(blocks, AXES, 0, 0, tiled=True)  19.7 us
    pallas_call x6, Pallas kernels, call(): pl.pallas_call(kernel, out_shape=[s if isinstance(s, jax.ShapeDtypeStruct...  19.7 us
    ppermute x1, waiting for transfers between devices, body(): lax.ppermute(nearby + partner[TORSO:], AXES, [(i, (i + 2 if i % 2 else i...  5.66 us
    ppermute x3, starting transfers between devices, from_behind(): return lax.ppermute(x, AXES, [(i, (i + by) % count) for i in range(count)])  3.3 us
  transfers between devices with their start and end apart: 37, of which 26 were waited for; matrix products, arithmetic and copies ran while one was open for 0% of the time, Pallas kernels for 3%

profile of v1, /device:TPU:1, one launch (start us, length us, event | category | flops | bytes accessed | tf_op | source)
XLA Modules:
  0.0 151.3 jit_solution(17316911448608190727)
XLA Ops:
  0.6 0.7 fusion
  1.3 1.4 collective-permute-start.11
  2.7 1.3 collective-permute-start.10
  4.0 5.2 %shard_map.166 = (f32[19,4096]{1,0:T(8,128)}, f32[32,128]{1,0:T(8,128)S(1)}, f32[32,128]{1,0:T(8,128)S(1)}, f32[136,128]{1,0:T(8,128)S(1)}, s32[32,128]{1,0:T(8,...) custom-call(f32[19,4096]{1,0:T(8,128)} %states_hbm.1, ...), custom_call_target="tpu_custom_call" | custom-call | flops 40000000 | bytes 1048576 | tf_op jit(solution)/shard_map/pallas_call | solution.py:314
  9.2 1.3 copy-done
  10.5 6.9 %collective-permute-start = (f32[136,128]{1,0:T(8,128)S(1)}, f32[136,128]{1,0:T(8,128)S(1)}, u32[]{:S(2)}, u32[]{:S(2)}) collective-permute-start(f32[136,128]{1,0:T(8,128)S(1)} %get-tuple-element.30), channel_id=1, source_target_pairs={{0,1},{1,0},{2,3},{3,2},{4,5},{5,4},{6,7},{7,6},{8,9},{9,8},{10,11... | collective-permute-start | bytes 208904 | tf_op jit(solution)/shard_map/ppermute | solution.py:334
  17.6 0.8 collective-permute-done
  18.4 0.1 minimum_select_fusion.3
  18.5 0.6 collective-permute-start.3
  19.1 0.9 collective-permute-start.2
  20.0 0.5 collective-permute-start.1
  20.6 1.2 collective-permute-done.3
  21.7 1.8 %collective-permute-done.2 = f32[136,128]{1,0:T(8,128)S(1)} collective-permute-done((f32[136,128]{1,0:T(8,128)S(1)}, f32[136,128]{1,0:T(8,128)S(1)}, u32[]{:S(2)}, u32[]{:S(2)}) %collective-permute-start.2) | collective-permute-done | bytes 69664 | tf_op jit(solution)/shard_map/ppermute | solution.py:334
  23.5 1.3 collective-permute-done.1
  24.8 0.1 minimum_select_fusion.2
  24.9 0.1 collective-permute-start.6
  25.0 1.5 collective-permute-start.5
  26.4 1.7 %collective-permute-done.6 = f32[136,128]{1,0:T(8,128)S(1)} collective-permute-done((f32[136,128]{1,0:T(8,128)S(1)}, f32[136,128]{1,0:T(8,128)S(1)}, u32[]{:S(2)}, u32[]{:S(2)}) %collective-permute-start.6) | collective-permute-done | bytes 69664 | tf_op jit(solution)/shard_map/ppermute | solution.py:334
  28.1 1.3 collective-permute-done.5
  29.4 1.7 %collective-permute-done.4 = f32[136,128]{1,0:T(8,128)S(1)} collective-permute-done((f32[136,128]{1,0:T(8,128)S(1)}, f32[136,128]{1,0:T(8,128)S(1)}, u32[]{:S(2)}, u32[]{:S(2)}) %collective-permute-start.4) | collective-permute-done | bytes 69664 | tf_op jit(solution)/shard_map/ppermute | solution.py:334
  31.1 0.1 minimum_select_fusion.1
  31.2 7.0 %collective-permute-start.9 = (f32[136,128]{1,0:T(8,128)S(1)}, f32[136,128]{1,0:T(8,128)S(1)}, u32[]{:S(2)}, u32[]{:S(2)}) collective-permute-start(f32[136,128]{1,0:T(8,128)S(1)} %minimum_select_fusion.1), channel_id=1, source_target_pairs={{0,6},{1,7},{2,0},{3,1},{4,2},{5,3},{6,4},{7,5},{8,14},{9,15},{10,... | collective-permute-start | bytes 208904 | tf_op jit(solution)/shard_map/ppermute | solution.py:334
  38.2 1.3 collective-permute-start.7
  39.5 0.1 collective-permute-done.9
  39.6 3.7 %collective-permute-done.8 = f32[136,128]{1,0:T(8,128)S(1)} collective-permute-done((f32[136,128]{1,0:T(8,128)S(1)}, f32[136,128]{1,0:T(8,128)S(1)}, u32[]{:S(2)}, u32[]{:S(2)}) %collective-permute-start.8) | collective-permute-done | bytes 69664 | tf_op jit(solution)/shard_map/ppermute | solution.py:334
  43.3 0.1 minimum_select_fusion.payload_ref
  43.4 1.6 %copy-done.1 = f32[32,128,128]{2,1,0:T(8,128)S(1)} copy-done((f32[32,128,128]{2,1,0:T(8,128)S(1)}, f32[32,128,128]{2,1,0:T(8,128)}, u32[]{:S(2)}) %copy-start.1) | copy-done | bytes 2097176
  45.0 3.9 %shard_map.167 = (f32[32,128]{1,0:T(8,128)S(1)}, f32[32,128]{1,0:T(8,128)S(1)}, f32[32,128]{1,0:T(8,128)S(1)}, f32[128,128]{1,0:T(8,128)S(1)}, f32[64,128]{1,0:T(8,128)S(1)}, /*index=5*/f32[8,128]{1,0:T(8,128)S(1)}) custom-call(s32[2]{0:T(128)S(1)} %pad_add_fusion.here_ref, f32[136,128]{1,0:T(8,128)S(1)} %minimum_select_fusion.payload_ref, ...), custom_call_target="tpu_custom_call" | custom-call | flops 40000000 | bytes 1048576 | tf_op jit(solution)/shard_map/pallas_call | solution.py:314
  48.9 3.7 %collective-permute-start.12 = (f32[128,128]{1,0:T(8,128)S(1)}, f32[128,128]{1,0:T(8,128)S(1)}, u32[]{:S(2)}, u32[]{:S(2)}) collective-permute-start(f32[128,128]{1,0:T(8,128)S(1)} %get-tuple-element.37), channel_id=1, source_target_pairs={{0,1},{1,0},{2,3},{3,2},{4,5},{5,4},{6,7},{7,6},{8,9},{9,8},{10,11... | collective-permute-start | bytes 196616 | tf_op jit(solution)/shard_map/ppermute | solution.py:334
  52.7 0.9 collective-permute-done.12
  53.6 2.0 %collective-permute-start.15 = (f32[128,128]{1,0:T(8,128)S(1)}, f32[128,128]{1,0:T(8,128)S(1)}, u32[]{:S(2)}, u32[]{:S(2)}) collective-permute-start(f32[128,128]{1,0:T(8,128)S(1)} %add.115), channel_id=1, source_target_pairs={{0,96},{1,97},{2,98},{3,99},{4,100},{5,101},{6,102},{7,103},{8,104... | collective-permute-start | bytes 196616 | tf_op jit(solution)/shard_map/ppermute | solution.py:334
  55.5 1.3 collective-permute-start.13
  56.9 5.0 %collective-permute-done.14 = f32[128,128]{1,0:T(8,128)S(1)} collective-permute-done((f32[128,128]{1,0:T(8,128)S(1)}, f32[128,128]{1,0:T(8,128)S(1)}, u32[]{:S(2)}, u32[]{:S(2)}) %collective-permute-start.14) | collective-permute-done | bytes 65568 | tf_op jit(solution)/shard_map/ppermute | solution.py:334
  61.9 2.6 %collective-permute-start.18 = (f32[128,128]{1,0:T(8,128)S(1)}, f32[128,128]{1,0:T(8,128)S(1)}, u32[]{:S(2)}, u32[]{:S(2)}) collective-permute-start(f32[128,128]{1,0:T(8,128)S(1)} %add_add_fusion.5), channel_id=1, source_target_pairs={{0,24},{1,25},{2,26},{3,27},{4,28},{5,29},{6,30},{7,31},{8,0},{9,1... | collective-permute-start | bytes 196616 | tf_op jit(solution)/shard_map/ppermute | solution.py:334
  64.5 1.4 collective-permute-start.16
  65.9 3.3 %collective-permute-done.17 = f32[128,128]{1,0:T(8,128)S(1)} collective-permute-done((f32[128,128]{1,0:T(8,128)S(1)}, f32[128,128]{1,0:T(8,128)S(1)}, u32[]{:S(2)}, u32[]{:S(2)}) %collective-permute-start.17) | collective-permute-done | bytes 65568 | tf_op jit(solution)/shard_map/ppermute | solution.py:334
  69.2 0.3 collective-permute-done.16
  69.5 2.6 %collective-permute-start.21 = (f32[128,128]{1,0:T(8,128)S(1)}, f32[128,128]{1,0:T(8,128)S(1)}, u32[]{:S(2)}, u32[]{:S(2)}) collective-permute-start(f32[128,128]{1,0:T(8,128)S(1)} %add_add_fusion.4), channel_id=1, source_target_pairs={{0,6},{1,7},{2,0},{3,1},{4,2},{5,3},{6,4},{7,5},{8,14},{9,15},{10,... | collective-permute-start | bytes 196616 | tf_op jit(solution)/shard_map/ppermute | solution.py:334
  72.1 1.3 collective-permute-start.19
  73.4 3.7 %collective-permute-done.20 = f32[128,128]{1,0:T(8,128)S(1)} collective-permute-done((f32[128,128]{1,0:T(8,128)S(1)}, f32[128,128]{1,0:T(8,128)S(1)}, u32[]{:S(2)}, u32[]{:S(2)}) %collective-permute-start.20) | collective-permute-done | bytes 65568 | tf_op jit(solution)/shard_map/ppermute | solution.py:334
  77.2 3.3 %shard_map.168 = (f32[32,128]{1,0:T(8,128)S(1)}, f32[32,128]{1,0:T(8,128)S(1)}, f32[32,128]{1,0:T(8,128)S(1)}, f32[128,128]{1,0:T(8,128)S(1)}) custom-call(f32[128,128]{1,0:T(8,128)S(1)} %add_add_fusion.3.payload_ref, f32[128,128]{1,0:T(8,128)S(1)} %get-tuple-element.31.gain_ref, s32[32,128]{1,0:T(8,128)S(1)} %get-tuple-element.32.slots_ref, ...), custom_call_target="tpu_custom_call" | custom-call | flops 40000000 | bytes 1048576 | tf_op jit(solution)/shard_map/pallas_call | solution.py:314
  80.5 3.7 %collective-permute-start.22 = (f32[128,128]{1,0:T(8,128)S(1)}, f32[128,128]{1,0:T(8,128)S(1)}, u32[]{:S(2)}, u32[]{:S(2)}) collective-permute-start(f32[128,128]{1,0:T(8,128)S(1)} %get-tuple-element.41), channel_id=1, source_target_pairs={{0,1},{1,0},{2,3},{3,2},{4,5},{5,4},{6,7},{7,6},{8,9},{9,8},{10,11... | collective-permute-start | bytes 196616 | tf_op jit(solution)/shard_map/ppermute | solution.py:334
  84.2 0.9 collective-permute-done.22
  85.1 2.3 %collective-permute-start.25 = (f32[128,128]{1,0:T(8,128)S(1)}, f32[128,128]{1,0:T(8,128)S(1)}, u32[]{:S(2)}, u32[]{:S(2)}) collective-permute-start(f32[128,128]{1,0:T(8,128)S(1)} %add.125), channel_id=1, source_target_pairs={{0,96},{1,97},{2,98},{3,99},{4,100},{5,101},{6,102},{7,103},{8,104... | collective-permute-start | bytes 196616 | tf_op jit(solution)/shard_map/ppermute | solution.py:334
  87.4 1.3 collective-permute-start.23
  88.7 5.0 %collective-permute-done.24 = f32[128,128]{1,0:T(8,128)S(1)} collective-permute-done((f32[128,128]{1,0:T(8,128)S(1)}, f32[128,128]{1,0:T(8,128)S(1)}, u32[]{:S(2)}, u32[]{:S(2)}) %collective-permute-start.24) | collective-permute-done | bytes 65568 | tf_op jit(solution)/shard_map/ppermute | solution.py:334
  93.7 2.6 %collective-permute-start.28 = (f32[128,128]{1,0:T(8,128)S(1)}, f32[128,128]{1,0:T(8,128)S(1)}, u32[]{:S(2)}, u32[]{:S(2)}) collective-permute-start(f32[128,128]{1,0:T(8,128)S(1)} %add_add_fusion.2), channel_id=1, source_target_pairs={{0,24},{1,25},{2,26},{3,27},{4,28},{5,29},{6,30},{7,31},{8,0},{9,1... | collective-permute-start | bytes 196616 | tf_op jit(solution)/shard_map/ppermute | solution.py:334
  96.4 1.3 collective-permute-start.26
  97.7 3.7 %collective-permute-done.27 = f32[128,128]{1,0:T(8,128)S(1)} collective-permute-done((f32[128,128]{1,0:T(8,128)S(1)}, f32[128,128]{1,0:T(8,128)S(1)}, u32[]{:S(2)}, u32[]{:S(2)}) %collective-permute-start.27) | collective-permute-done | bytes 65568 | tf_op jit(solution)/shard_map/ppermute | solution.py:334
  101.4 2.6 %collective-permute-start.31 = (f32[128,128]{1,0:T(8,128)S(1)}, f32[128,128]{1,0:T(8,128)S(1)}, u32[]{:S(2)}, u32[]{:S(2)}) collective-permute-start(f32[128,128]{1,0:T(8,128)S(1)} %add_add_fusion.1), channel_id=1, source_target_pairs={{0,6},{1,7},{2,0},{3,1},{4,2},{5,3},{6,4},{7,5},{8,14},{9,15},{10,... | collective-permute-start | bytes 196616 | tf_op jit(solution)/shard_map/ppermute | solution.py:334
  104.0 1.3 collective-permute-start.29
  105.4 3.7 %collective-permute-done.30 = f32[128,128]{1,0:T(8,128)S(1)} collective-permute-done((f32[128,128]{1,0:T(8,128)S(1)}, f32[128,128]{1,0:T(8,128)S(1)}, u32[]{:S(2)}, u32[]{:S(2)}) %collective-permute-start.30) | collective-permute-done | bytes 65568 | tf_op jit(solution)/shard_map/ppermute | solution.py:334
  109.1 5.3 %shard_map.169 = (f32[32,128]{1,0:T(8,128)}, f32[64,128]{1,0:T(8,128)S(1)}, f32[64,128]{1,0:T(8,128)S(1)}, f32[64,128]{1,0:T(8,128)S(1)}, f32[192,128]{1,0:T(8,128)S(1)}, /*index=5*/f32[128,128]{1,0:T(8,128)S(1)}) custom-call(s32[2]{0:T(128)S(1)} %pad_add_fusion.here_ref, f32[128,128]{1,0:T(8,128)S(1)} %add_add_fusion.payload_ref, ...), custom_call_target="tpu_custom_call" | custom-call | flops 40000000 | bytes 1048576 | tf_op jit(solution)/shard_map/pallas_call | solution.py:314
  114.4 3.7 %collective-permute-start.34 = (f32[192,128]{1,0:T(8,128)S(1)}, f32[192,128]{1,0:T(8,128)S(1)}, u32[]{:S(2)}, u32[]{:S(2)}) collective-permute-start(f32[192,128]{1,0:T(8,128)S(1)} %get-tuple-element.50), channel_id=1, source_target_pairs={{0,1},{1,0},{2,3},{3,2},{4,5},{5,4},{6,7},{7,6},{8,9},{9,8},{10,11... | collective-permute-start | bytes 294920 | tf_op jit(solution)/shard_map/ppermute | solution.py:334
  118.2 0.9 collective-permute-done.34.partner_ref
  119.2 0.6 collective-permute-start.32
  119.8 2.4 %collective-permute-start.33 = (f32[64,128]{1,0:T(8,128)S(1)}, f32[64,128]{1,0:T(8,128)S(1)}, u32[]{:S(2)}, u32[]{:S(2)}) collective-permute-start(f32[64,128]{1,0:T(8,128)S(1)} %get-tuple-element.49), channel_id=1, source_target_pairs={{0,125},{1,4},{2,127},{3,6},{4,1},{5,8},{6,3},{7,10},{8,5},{9,12},... | collective-permute-start | bytes 98312 | tf_op jit(solution)/shard_map/ppermute | solution.py:438
  122.2 5.7 %collective-permute-done.35.next_ref = f32[128,128]{1,0:T(8,128)S(1)} collective-permute-done((f32[128,128]{1,0:T(8,128)S(1)}, f32[128,128]{1,0:T(8,128)S(1)}, u32[]{:S(2)}, u32[]{:S(2)}) %collective-permute-start.35) | collective-permute-done | bytes 65568 | tf_op jit(solution)/shard_map/ppermute | solution.py:440
  127.9 0.6 collective-permute-start.36
  128.5 0.9 collective-permute-done.36.handed_ref
  129.4 0.6 shard_map.170
  130.0 0.2 copy.18
  130.2 19.7 %all_to_all.11 = f32[128,1,384]{2,1,0:T(1,128)S(1)} all-to-all(f32[128,1,384]{2,1,0:T(1,128)S(1)} %copy.18), channel_id=1, replica_groups=mesh['a'=4,'b'=4,'c'=4,'d'=2] {'a','b','c','d'}, dimensions={0} | all-to-all | bytes 393216 | tf_op jit(solution)/shard_map/all_to_all | solution.py:450
  149.9 1.4 shard_map.171
  (51 shorter events, 0.7 us)
Async XLA Ops:
  1.3 38.1 %collective-permute-start.11 = (f32[8,128]{1,0:T(8,128)S(1)}, f32[8,128]{1,0:T(8,128)S(1)}, u32[]{:S(2)}, u32[]{:S(2)}) collective-permute-start(f32[8,128]{1,0:T(8,128)S(1)} %get-tuple-element.55), channel_id=1, source_target_pairs={{0,127},{1,0},{2,1},{3,2},{4,3},{5,4},{6,5},{7,6},{8,7},{9,8},{10,... | collective-permute-start | bytes 12296 | tf_op jit(solution)/shard_map/ppermute | solution.py:372
  2.7 17.8 %collective-permute-start.10 = (f32[8,128]{1,0:T(8,128)S(1)}, f32[8,128]{1,0:T(8,128)S(1)}, u32[]{:S(2)}, u32[]{:S(2)}) collective-permute-start(f32[8,128]{1,0:T(8,128)S(1)} %get-tuple-element.56), channel_id=1, source_target_pairs={{0,1},{1,2},{2,3},{3,4},{4,5},{5,6},{6,7},{7,8},{8,9},{9,10},{10,1... | collective-permute-start | bytes 12296 | tf_op jit(solution)/shard_map/ppermute | solution.py:372
  4.0 22.4 %copy-start.5 = (f32[64,128]{1,0:T(8,128)S(1)}, f32[64,128]{1,0:T(8,128)}, u32[]{:S(2)}) copy-start(f32[64,128]{1,0:T(8,128)} %conduct_hbm.1) | copy-start | bytes 98308
  9.2 1.3 copy-start
  10.5 7.8 %collective-permute-start = (f32[136,128]{1,0:T(8,128)S(1)}, f32[136,128]{1,0:T(8,128)S(1)}, u32[]{:S(2)}, u32[]{:S(2)}) collective-permute-start(f32[136,128]{1,0:T(8,128)S(1)} %get-tuple-element.30), channel_id=1, source_target_pairs={{0,1},{1,0},{2,3},{3,2},{4,5},{5,4},{6,7},{7,6},{8,9},{9,8},{10,11... | collective-permute-start | bytes 208904 | tf_op jit(solution)/shard_map/ppermute | solution.py:334
  18.5 3.2 %collective-permute-start.3 = (f32[136,128]{1,0:T(8,128)S(1)}, f32[136,128]{1,0:T(8,128)S(1)}, u32[]{:S(2)}, u32[]{:S(2)}) collective-permute-start(f32[136,128]{1,0:T(8,128)S(1)} %minimum_select_fusion.3), channel_id=1, source_target_pairs={{0,96},{1,97},{2,98},{3,99},{4,100},{5,101},{6,102},{7,103},{8,104... | collective-permute-start | bytes 208904 | tf_op jit(solution)/shard_map/ppermute | solution.py:334
  19.1 4.4 %collective-permute-start.2 = (f32[136,128]{1,0:T(8,128)S(1)}, f32[136,128]{1,0:T(8,128)S(1)}, u32[]{:S(2)}, u32[]{:S(2)}) collective-permute-start(f32[136,128]{1,0:T(8,128)S(1)} %minimum_select_fusion.3), channel_id=1, source_target_pairs={{0,32},{1,33},{2,34},{3,35},{4,36},{5,37},{6,38},{7,39},{8,40},{9,... | collective-permute-start | bytes 208904 | tf_op jit(solution)/shard_map/ppermute | solution.py:334
  20.0 4.8 %collective-permute-start.1 = (f32[136,128]{1,0:T(8,128)S(1)}, f32[136,128]{1,0:T(8,128)S(1)}, u32[]{:S(2)}, u32[]{:S(2)}) collective-permute-start(f32[136,128]{1,0:T(8,128)S(1)} %minimum_select_fusion.3), channel_id=1, source_target_pairs={{0,64},{1,65},{2,66},{3,67},{4,68},{5,69},{6,70},{7,71},{8,72},{9,... | collective-permute-start | bytes 208904 | tf_op jit(solution)/shard_map/ppermute | solution.py:334
  24.9 3.2 %collective-permute-start.6 = (f32[136,128]{1,0:T(8,128)S(1)}, f32[136,128]{1,0:T(8,128)S(1)}, u32[]{:S(2)}, u32[]{:S(2)}) collective-permute-start(f32[136,128]{1,0:T(8,128)S(1)} %minimum_select_fusion.2), channel_id=1, source_target_pairs={{0,24},{1,25},{2,26},{3,27},{4,28},{5,29},{6,30},{7,31},{8,0},{9,1... | collective-permute-start | bytes 208904 | tf_op jit(solution)/shard_map/ppermute | solution.py:334
  25.0 4.4 %collective-permute-start.5 = (f32[136,128]{1,0:T(8,128)S(1)}, f32[136,128]{1,0:T(8,128)S(1)}, u32[]{:S(2)}, u32[]{:S(2)}) collective-permute-start(f32[136,128]{1,0:T(8,128)S(1)} %minimum_select_fusion.2), channel_id=1, source_target_pairs={{0,8},{1,9},{2,10},{3,11},{4,12},{5,13},{6,14},{7,15},{8,16},{9,17... | collective-permute-start | bytes 208904 | tf_op jit(solution)/shard_map/ppermute | solution.py:334
  26.4 4.7 %collective-permute-start.4 = (f32[136,128]{1,0:T(8,128)S(1)}, f32[136,128]{1,0:T(8,128)S(1)}, u32[]{:S(2)}, u32[]{:S(2)}) collective-permute-start(f32[136,128]{1,0:T(8,128)S(1)} %minimum_select_fusion.2), channel_id=1, source_target_pairs={{0,16},{1,17},{2,18},{3,19},{4,20},{5,21},{6,22},{7,23},{8,24},{9,... | collective-permute-start | bytes 208904 | tf_op jit(solution)/shard_map/ppermute | solution.py:334
  31.2 8.4 %collective-permute-start.9 = (f32[136,128]{1,0:T(8,128)S(1)}, f32[136,128]{1,0:T(8,128)S(1)}, u32[]{:S(2)}, u32[]{:S(2)}) collective-permute-start(f32[136,128]{1,0:T(8,128)S(1)} %minimum_select_fusion.1), channel_id=1, source_target_pairs={{0,6},{1,7},{2,0},{3,1},{4,2},{5,3},{6,4},{7,5},{8,14},{9,15},{10,... | collective-permute-start | bytes 208904 | tf_op jit(solution)/shard_map/ppermute | solution.py:334
  38.2 5.1 %collective-permute-start.8 = (f32[136,128]{1,0:T(8,128)S(1)}, f32[136,128]{1,0:T(8,128)S(1)}, u32[]{:S(2)}, u32[]{:S(2)}) collective-permute-start(f32[136,128]{1,0:T(8,128)S(1)} %minimum_select_fusion.1), channel_id=1, source_target_pairs={{0,2},{1,3},{2,4},{3,5},{4,6},{5,7},{6,0},{7,1},{8,10},{9,11},{10,... | collective-permute-start | bytes 208904 | tf_op jit(solution)/shard_map/ppermute | solution.py:334
  38.2 5.1 %collective-permute-start.7 = (f32[136,128]{1,0:T(8,128)S(1)}, f32[136,128]{1,0:T(8,128)S(1)}, u32[]{:S(2)}, u32[]{:S(2)}) collective-permute-start(f32[136,128]{1,0:T(8,128)S(1)} %minimum_select_fusion.1), channel_id=1, source_target_pairs={{0,4},{1,5},{2,6},{3,7},{4,0},{5,1},{6,2},{7,3},{8,12},{9,13},{10,... | collective-permute-start | bytes 208904 | tf_op jit(solution)/shard_map/ppermute | solution.py:334
  43.4 1.6 %copy-start.1 = (f32[32,128,128]{2,1,0:T(8,128)S(1)}, f32[32,128,128]{2,1,0:T(8,128)}, u32[]{:S(2)}) copy-start(f32[32,128,128]{2,1,0:T(8,128)} %copy-done) | copy-start | bytes 6291460
  48.9 4.6 %collective-permute-start.12 = (f32[128,128]{1,0:T(8,128)S(1)}, f32[128,128]{1,0:T(8,128)S(1)}, u32[]{:S(2)}, u32[]{:S(2)}) collective-permute-start(f32[128,128]{1,0:T(8,128)S(1)} %get-tuple-element.37), channel_id=1, source_target_pairs={{0,1},{1,0},{2,3},{3,2},{4,5},{5,4},{6,7},{7,6},{8,9},{9,8},{10,11... | collective-permute-start | bytes 196616 | tf_op jit(solution)/shard_map/ppermute | solution.py:334
  53.6 3.3 %collective-permute-start.15 = (f32[128,128]{1,0:T(8,128)S(1)}, f32[128,128]{1,0:T(8,128)S(1)}, u32[]{:S(2)}, u32[]{:S(2)}) collective-permute-start(f32[128,128]{1,0:T(8,128)S(1)} %add.115), channel_id=1, source_target_pairs={{0,96},{1,97},{2,98},{3,99},{4,100},{5,101},{6,102},{7,103},{8,104... | collective-permute-start | bytes 196616 | tf_op jit(solution)/shard_map/ppermute | solution.py:334
  55.5 6.3 %collective-permute-start.14 = (f32[128,128]{1,0:T(8,128)S(1)}, f32[128,128]{1,0:T(8,128)S(1)}, u32[]{:S(2)}, u32[]{:S(2)}) collective-permute-start(f32[128,128]{1,0:T(8,128)S(1)} %add.115), channel_id=1, source_target_pairs={{0,32},{1,33},{2,34},{3,35},{4,36},{5,37},{6,38},{7,39},{8,40},{9,... | collective-permute-start | bytes 196616 | tf_op jit(solution)/shard_map/ppermute | solution.py:334
  55.5 6.3 %collective-permute-start.13 = (f32[128,128]{1,0:T(8,128)S(1)}, f32[128,128]{1,0:T(8,128)S(1)}, u32[]{:S(2)}, u32[]{:S(2)}) collective-permute-start(f32[128,128]{1,0:T(8,128)S(1)} %add.115), channel_id=1, source_target_pairs={{0,64},{1,65},{2,66},{3,67},{4,68},{5,69},{6,70},{7,71},{8,72},{9,... | collective-permute-start | bytes 196616 | tf_op jit(solution)/shard_map/ppermute | solution.py:334
  61.9 4.0 %collective-permute-start.18 = (f32[128,128]{1,0:T(8,128)S(1)}, f32[128,128]{1,0:T(8,128)S(1)}, u32[]{:S(2)}, u32[]{:S(2)}) collective-permute-start(f32[128,128]{1,0:T(8,128)S(1)} %add_add_fusion.5), channel_id=1, source_target_pairs={{0,24},{1,25},{2,26},{3,27},{4,28},{5,29},{6,30},{7,31},{8,0},{9,1... | collective-permute-start | bytes 196616 | tf_op jit(solution)/shard_map/ppermute | solution.py:334
  64.5 4.7 %collective-permute-start.17 = (f32[128,128]{1,0:T(8,128)S(1)}, f32[128,128]{1,0:T(8,128)S(1)}, u32[]{:S(2)}, u32[]{:S(2)}) collective-permute-start(f32[128,128]{1,0:T(8,128)S(1)} %add_add_fusion.5), channel_id=1, source_target_pairs={{0,8},{1,9},{2,10},{3,11},{4,12},{5,13},{6,14},{7,15},{8,16},{9,17... | collective-permute-start | bytes 196616 | tf_op jit(solution)/shard_map/ppermute | solution.py:334
  64.5 5.0 %collective-permute-start.16 = (f32[128,128]{1,0:T(8,128)S(1)}, f32[128,128]{1,0:T(8,128)S(1)}, u32[]{:S(2)}, u32[]{:S(2)}) collective-permute-start(f32[128,128]{1,0:T(8,128)S(1)} %add_add_fusion.5), channel_id=1, source_target_pairs={{0,16},{1,17},{2,18},{3,19},{4,20},{5,21},{6,22},{7,23},{8,24},{9,... | collective-permute-start | bytes 196616 | tf_op jit(solution)/shard_map/ppermute | solution.py:334
  69.5 3.9 %collective-permute-start.21 = (f32[128,128]{1,0:T(8,128)S(1)}, f32[128,128]{1,0:T(8,128)S(1)}, u32[]{:S(2)}, u32[]{:S(2)}) collective-permute-start(f32[128,128]{1,0:T(8,128)S(1)} %add_add_fusion.4), channel_id=1, source_target_pairs={{0,6},{1,7},{2,0},{3,1},{4,2},{5,3},{6,4},{7,5},{8,14},{9,15},{10,... | collective-permute-start | bytes 196616 | tf_op jit(solution)/shard_map/ppermute | solution.py:334
  72.1 5.0 %collective-permute-start.20 = (f32[128,128]{1,0:T(8,128)S(1)}, f32[128,128]{1,0:T(8,128)S(1)}, u32[]{:S(2)}, u32[]{:S(2)}) collective-permute-start(f32[128,128]{1,0:T(8,128)S(1)} %add_add_fusion.4), channel_id=1, source_target_pairs={{0,2},{1,3},{2,4},{3,5},{4,6},{5,7},{6,0},{7,1},{8,10},{9,11},{10,... | collective-permute-start | bytes 196616 | tf_op jit(solution)/shard_map/ppermute | solution.py:334
  72.1 5.0 %collective-permute-start.19 = (f32[128,128]{1,0:T(8,128)S(1)}, f32[128,128]{1,0:T(8,128)S(1)}, u32[]{:S(2)}, u32[]{:S(2)}) collective-permute-start(f32[128,128]{1,0:T(8,128)S(1)} %add_add_fusion.4), channel_id=1, source_target_pairs={{0,4},{1,5},{2,6},{3,7},{4,0},{5,1},{6,2},{7,3},{8,12},{9,13},{10,... | collective-permute-start | bytes 196616 | tf_op jit(solution)/shard_map/ppermute | solution.py:334
  77.2 31.9 %copy-start.2 = (s32[4096,1]{0,1:T(1,128)S(1)}, s32[4096,1]{0,1:T(1,128)}, u32[]{:S(2)}) copy-start(s32[4096,1]{0,1:T(1,128)} %param.26) | copy-start | bytes 49156
  77.2 31.9 %copy-start.3 = (s32[4096]{0:T(1024)S(1)}, s32[4096]{0:T(1024)}, u32[]{:S(2)}) copy-start(s32[4096]{0:T(1024)} %param.27) | copy-start | bytes 49156
  77.2 31.9 %copy-start.4 = (f32[4096]{0:T(1024)S(1)}, f32[4096]{0:T(1024)}, u32[]{:S(2)}) copy-start(f32[4096]{0:T(1024)} %param.28) | copy-start | bytes 49156
  80.5 4.6 %collective-permute-start.22 = (f32[128,128]{1,0:T(8,128)S(1)}, f32[128,128]{1,0:T(8,128)S(1)}, u32[]{:S(2)}, u32[]{:S(2)}) collective-permute-start(f32[128,128]{1,0:T(8,128)S(1)} %get-tuple-element.41), channel_id=1, source_target_pairs={{0,1},{1,0},{2,3},{3,2},{4,5},{5,4},{6,7},{7,6},{8,9},{9,8},{10,11... | collective-permute-start | bytes 196616 | tf_op jit(solution)/shard_map/ppermute | solution.py:334
  85.1 3.6 %collective-permute-start.25 = (f32[128,128]{1,0:T(8,128)S(1)}, f32[128,128]{1,0:T(8,128)S(1)}, u32[]{:S(2)}, u32[]{:S(2)}) collective-permute-start(f32[128,128]{1,0:T(8,128)S(1)} %add.125), channel_id=1, source_target_pairs={{0,96},{1,97},{2,98},{3,99},{4,100},{5,101},{6,102},{7,103},{8,104... | collective-permute-start | bytes 196616 | tf_op jit(solution)/shard_map/ppermute | solution.py:334
  87.4 6.3 %collective-permute-start.24 = (f32[128,128]{1,0:T(8,128)S(1)}, f32[128,128]{1,0:T(8,128)S(1)}, u32[]{:S(2)}, u32[]{:S(2)}) collective-permute-start(f32[128,128]{1,0:T(8,128)S(1)} %add.125), channel_id=1, source_target_pairs={{0,32},{1,33},{2,34},{3,35},{4,36},{5,37},{6,38},{7,39},{8,40},{9,... | collective-permute-start | bytes 196616 | tf_op jit(solution)/shard_map/ppermute | solution.py:334
  87.4 6.3 %collective-permute-start.23 = (f32[128,128]{1,0:T(8,128)S(1)}, f32[128,128]{1,0:T(8,128)S(1)}, u32[]{:S(2)}, u32[]{:S(2)}) collective-permute-start(f32[128,128]{1,0:T(8,128)S(1)} %add.125), channel_id=1, source_target_pairs={{0,64},{1,65},{2,66},{3,67},{4,68},{5,69},{6,70},{7,71},{8,72},{9,... | collective-permute-start | bytes 196616 | tf_op jit(solution)/shard_map/ppermute | solution.py:334
  93.7 3.9 %collective-permute-start.28 = (f32[128,128]{1,0:T(8,128)S(1)}, f32[128,128]{1,0:T(8,128)S(1)}, u32[]{:S(2)}, u32[]{:S(2)}) collective-permute-start(f32[128,128]{1,0:T(8,128)S(1)} %add_add_fusion.2), channel_id=1, source_target_pairs={{0,24},{1,25},{2,26},{3,27},{4,28},{5,29},{6,30},{7,31},{8,0},{9,1... | collective-permute-start | bytes 196616 | tf_op jit(solution)/shard_map/ppermute | solution.py:334
  96.4 5.0 %collective-permute-start.27 = (f32[128,128]{1,0:T(8,128)S(1)}, f32[128,128]{1,0:T(8,128)S(1)}, u32[]{:S(2)}, u32[]{:S(2)}) collective-permute-start(f32[128,128]{1,0:T(8,128)S(1)} %add_add_fusion.2), channel_id=1, source_target_pairs={{0,8},{1,9},{2,10},{3,11},{4,12},{5,13},{6,14},{7,15},{8,16},{9,17... | collective-permute-start | bytes 196616 | tf_op jit(solution)/shard_map/ppermute | solution.py:334
  96.4 5.0 %collective-permute-start.26 = (f32[128,128]{1,0:T(8,128)S(1)}, f32[128,128]{1,0:T(8,128)S(1)}, u32[]{:S(2)}, u32[]{:S(2)}) collective-permute-start(f32[128,128]{1,0:T(8,128)S(1)} %add_add_fusion.2), channel_id=1, source_target_pairs={{0,16},{1,17},{2,18},{3,19},{4,20},{5,21},{6,22},{7,23},{8,24},{9,... | collective-permute-start | bytes 196616 | tf_op jit(solution)/shard_map/ppermute | solution.py:334
  101.4 3.9 %collective-permute-start.31 = (f32[128,128]{1,0:T(8,128)S(1)}, f32[128,128]{1,0:T(8,128)S(1)}, u32[]{:S(2)}, u32[]{:S(2)}) collective-permute-start(f32[128,128]{1,0:T(8,128)S(1)} %add_add_fusion.1), channel_id=1, source_target_pairs={{0,6},{1,7},{2,0},{3,1},{4,2},{5,3},{6,4},{7,5},{8,14},{9,15},{10,... | collective-permute-start | bytes 196616 | tf_op jit(solution)/shard_map/ppermute | solution.py:334
  104.0 5.0 %collective-permute-start.30 = (f32[128,128]{1,0:T(8,128)S(1)}, f32[128,128]{1,0:T(8,128)S(1)}, u32[]{:S(2)}, u32[]{:S(2)}) collective-permute-start(f32[128,128]{1,0:T(8,128)S(1)} %add_add_fusion.1), channel_id=1, source_target_pairs={{0,2},{1,3},{2,4},{3,5},{4,6},{5,7},{6,0},{7,1},{8,10},{9,11},{10,... | collective-permute-start | bytes 196616 | tf_op jit(solution)/shard_map/ppermute | solution.py:334
  104.0 5.0 %collective-permute-start.29 = (f32[128,128]{1,0:T(8,128)S(1)}, f32[128,128]{1,0:T(8,128)S(1)}, u32[]{:S(2)}, u32[]{:S(2)}) collective-permute-start(f32[128,128]{1,0:T(8,128)S(1)} %add_add_fusion.1), channel_id=1, source_target_pairs={{0,4},{1,5},{2,6},{3,7},{4,0},{5,1},{6,2},{7,3},{8,12},{9,13},{10,... | collective-permute-start | bytes 196616 | tf_op jit(solution)/shard_map/ppermute | solution.py:334
  114.4 4.7 %collective-permute-start.34 = (f32[192,128]{1,0:T(8,128)S(1)}, f32[192,128]{1,0:T(8,128)S(1)}, u32[]{:S(2)}, u32[]{:S(2)}) collective-permute-start(f32[192,128]{1,0:T(8,128)S(1)} %get-tuple-element.50), channel_id=1, source_target_pairs={{0,1},{1,0},{2,3},{3,2},{4,5},{5,4},{6,7},{7,6},{8,9},{9,8},{10,11... | collective-permute-start | bytes 294920 | tf_op jit(solution)/shard_map/ppermute | solution.py:334
  119.1 8.7 %collective-permute-start.35 = (f32[128,128]{1,0:T(8,128)S(1)}, f32[128,128]{1,0:T(8,128)S(1)}, u32[]{:S(2)}, u32[]{:S(2)}) collective-permute-start(f32[128,128]{1,0:T(8,128)S(1)} %slice_add_fusion), channel_id=1, source_target_pairs={{0,126},{1,3},{2,0},{3,5},{4,2},{5,7},{6,4},{7,9},{8,6},{9,11},{10... | collective-permute-start | bytes 196616 | tf_op jit(solution)/shard_map/ppermute | solution.py:440
  119.2 9.3 %collective-permute-start.32 = (f32[64,128]{1,0:T(8,128)S(1)}, f32[64,128]{1,0:T(8,128)S(1)}, u32[]{:S(2)}, u32[]{:S(2)}) collective-permute-start(f32[64,128]{1,0:T(8,128)S(1)} %get-tuple-element.48), channel_id=1, source_target_pairs={{0,64},{1,65},{2,66},{3,67},{4,68},{5,69},{6,70},{7,71},{8,72},{9,... | collective-permute-start | bytes 98312 | tf_op jit(solution)/shard_map/ppermute | solution.py:372
  119.8 8.7 %collective-permute-start.33 = (f32[64,128]{1,0:T(8,128)S(1)}, f32[64,128]{1,0:T(8,128)S(1)}, u32[]{:S(2)}, u32[]{:S(2)}) collective-permute-start(f32[64,128]{1,0:T(8,128)S(1)} %get-tuple-element.49), channel_id=1, source_target_pairs={{0,125},{1,4},{2,127},{3,6},{4,1},{5,8},{6,3},{7,10},{8,5},{9,12},... | collective-permute-start | bytes 98312 | tf_op jit(solution)/shard_map/ppermute | solution.py:438
  127.9 1.5 collective-permute-start.36

commit v2 on v1

--- a/solution.py
+++ b/solution.py
@@ -82,8 +82,8 @@
 
 def ionic_kernel(
     states_hbm, region_hbm, half_hbm, slope_hbm, rate_hbm, cond_hbm, rev_hbm,
-    slots_hbm, conduct_hbm, gain_hbm, stiff_hbm, precond_hbm,
-    states_out, resid_out, update_out, payload_out, slots_out, gain_out, stiff_out, precond_out,
+    slots_hbm, conduct_hbm, gain_hbm, precond_hbm,
+    states_out, resid_out, update_out, payload_out, slots_out, gain_out, precond_out,
     states_ref, region_ref, half_ref, slope_ref, rate_ref, cond_ref, rev_ref,
     conduct_ref, table_ref, volt_ref, row_ref, col_ref, sems,
 ):
@@ -91,7 +91,7 @@
         (half_hbm, half_ref), (slope_hbm, slope_ref), (rate_hbm, rate_ref), (cond_hbm, cond_ref),
         (rev_hbm, rev_ref), (region_hbm, region_ref), (states_hbm, states_ref),
         (slots_hbm, slots_out), (conduct_hbm, conduct_ref),
-        (stiff_hbm, stiff_out), (precond_hbm, precond_out), (gain_hbm, gain_out),
+        (gain_hbm, gain_out), (precond_hbm, precond_out),
     )
     copies = [pltpu.make_async_copy(x, y, sems.at[k]) for k, (x, y) in enumerate(pairs)]
     for copy in copies:
@@ -133,26 +133,24 @@
     for copy in copies[7:9]:
         copy.wait()
     payload_out[SLOT_ROWS:, :] = jnp.min(conduct_ref[...].reshape(8, 8, LANES), axis=0)
-    copies[9].wait()
-    tile_products(stiff_out, volt_ref, resid_out)
-    copies[10].wait()
-    tile_products(precond_out, resid_out, update_out)
-    copies[11].wait()
-    update_out[...] = update_out[...] * (1.0 / CENTER)
+    volt = volt_ref[...]
+    resid_out[...] = volt
+    update_out[...] = volt * (1.0 / CENTER)
     payload_out[0:SLOT_ROWS, :] = slot_sums(slots_out, update_out, row_ref, col_ref)
+    for copy in copies[9:]:
+        copy.wait()
 
 
 def heart_step(
-    index, payload_ref, gain_ref, slots_ref, stiff_ref, precond_ref, resid_ref, update_ref,
+    index, payload_ref, gain_ref, slots_ref, precond_ref, resid_ref, update_ref,
     potential_ref, coupled_ref, work_ref, pick_ref, resid_out, update_out, potential_out,
 ):
     slot_values(slots_ref, gain_ref[...] * payload_ref[0:SLOT_ROWS, :], pick_ref, coupled_ref)
-    tile_products(stiff_ref, update_ref, work_ref)
-    resid = resid_ref[...] - (work_ref[...] + coupled_ref[...])
+    tile_products(precond_ref, coupled_ref, work_ref)
+    resid = resid_ref[...] - (update_ref[...] + work_ref[...])
     resid_out[...] = resid
-    tile_products(precond_ref, resid_out, work_ref)
     keep, add = FACTORS[index]
-    update = keep * update_ref[...] + add * work_ref[...]
+    update = keep * update_ref[...] + add * resid
     update_out[...] = update
     potential_out[...] = potential_ref[...] + update
 
@@ -193,12 +191,12 @@
 
 
 def first_step_kernel(
-    here_ref, payload_ref, gain_ref, slots_ref, stiff_ref, precond_ref, resid_ref, update_ref, conduct_ref,
+    here_ref, payload_ref, gain_ref, slots_ref, precond_ref, resid_ref, update_ref, conduct_ref,
     resid_out, update_out, potential_out, payload_out, weight_out, smallest_out,
     coupled_ref, work_ref, pick_ref, row_ref, col_ref,
 ):
     heart_step(
-        0, payload_ref, gain_ref, slots_ref, stiff_ref, precond_ref, resid_ref, update_ref,
+        0, payload_ref, gain_ref, slots_ref, precond_ref, resid_ref, update_ref,
         update_ref, coupled_ref, work_ref, pick_ref, resid_out, update_out, potential_out,
     )
     payload_out[...] = slot_sums(slots_ref, update_out, row_ref, col_ref)
@@ -212,25 +210,25 @@
 
 
 def second_step_kernel(
-    payload_ref, gain_ref, slots_ref, stiff_ref, precond_ref, resid_ref, update_ref, potential_ref,
+    payload_ref, gain_ref, slots_ref, precond_ref, resid_ref, update_ref, potential_ref,
     resid_out, update_out, potential_out, payload_out,
     coupled_ref, work_ref, pick_ref, row_ref, col_ref,
 ):
     heart_step(
-        1, payload_ref, gain_ref, slots_ref, stiff_ref, precond_ref, resid_ref, update_ref,
+        1, payload_ref, gain_ref, slots_ref, precond_ref, resid_ref, update_ref,
         potential_ref, coupled_ref, work_ref, pick_ref, resid_out, update_out, potential_out,
     )
     payload_out[...] = slot_sums(slots_ref, update_out, row_ref, col_ref)
 
 
 def last_step_kernel(
-    here_ref, payload_ref, gain_ref, slots_ref, stiff_ref, precond_ref, resid_ref, update_ref,
+    here_ref, payload_ref, gain_ref, slots_ref, precond_ref, resid_ref, update_ref,
     potential_ref, owner_ref, cell_ref, scale_ref,
     potential_out, own_out, across_out, far_out, partner_out, next_out,
     coupled_ref, work_ref, pick_ref, resid_out, update_out, row_ref, col_ref,
 ):
     heart_step(
-        2, payload_ref, gain_ref, slots_ref, stiff_ref, precond_ref, resid_ref, update_ref,
+        2, payload_ref, gain_ref, slots_ref, precond_ref, resid_ref, update_ref,
         potential_ref, coupled_ref, work_ref, pick_ref, resid_out, update_out, potential_out,
     )
     devices = here_ref[1]
@@ -317,7 +315,7 @@
         in_specs=spec,
         out_specs=[pl.BlockSpec(memory_space=pltpu.VMEM)] * len(outs),
         scratch_shapes=scratch,
-        compiler_params=pltpu.CompilerParams(vmem_limit_bytes=16 * 1024 * 1024),
+        compiler_params=pltpu.CompilerParams(vmem_limit_bytes=24 * 1024 * 1024),
         cost_estimate=pl.CostEstimate(flops=flops, bytes_accessed=1 << 20, transcendentals=0),
     )(*args)
 
@@ -386,7 +384,6 @@
     )
     gain = slot_gain.reshape(grid)
     whom = jnp.stack([here, jnp.int32(devices)]).astype(jnp.int32)
-    mats = stiffness.shape
     rowspace = pltpu.VMEM((256, 4096), BF16)
     colspace = pltpu.VMEM((128, 4096), BF16)
     nodespace = pltpu.VMEM(node, F32)
@@ -394,15 +391,15 @@
     tablespace = pltpu.VMEM((3, 18), F32)
     indexspace = pltpu.VMEM(node, jnp.int32)
 
-    new_states, resid, update, payload, slots, gain, stiffness, preconditioner = call(
+    new_states, resid, update, payload, slots, gain, preconditioner = call(
         ionic_kernel,
-        [states.shape, node, node, (PAYLOAD, LANES), jax.ShapeDtypeStruct(node, jnp.int32), grid, mats, mats],
+        [states.shape, node, node, (PAYLOAD, LANES), jax.ShapeDtypeStruct(node, jnp.int32), grid, preconditioner.shape],
         [pltpu.VMEM(states.shape, F32), indexspace] + [tablespace] * 5
         + [pltpu.VMEM(tile, F32), pltpu.VMEM((128, 128), F32), nodespace, rowspace,
-           colspace, pltpu.SemaphoreType.DMA((12,))],
+           colspace, pltpu.SemaphoreType.DMA((11,))],
         0, 40000000,
         (states, region, half_volt, slopes, rates, conductance, reversal, slots, torso_conduct,
-         gain, stiffness, preconditioner),
+         gain, preconditioner),
         pltpu.HBM,
     )
     above = from_behind(torso_conduct[TORSO - 8 :], 1, devices)
@@ -414,7 +411,7 @@
         [node, node, node, grid, tile, (8, LANES)],
         [nodespace, nodespace, pickspace, rowspace, colspace],
         1, 40000000,
-        (whom, payload, gain, slots, stiffness, preconditioner, resid, update, conduct),
+        (whom, payload, gain, slots, preconditioner, resid, update, conduct),
     )
     payload = over_all(payload)
     resid, update, potential, payload = call(
@@ -422,7 +419,7 @@
         [node, node, node, grid],
         [nodespace, nodespace, pickspace, rowspace, colspace],
         0, 40000000,
-        (payload, gain, slots, stiffness, preconditioner, resid, update, potential),
+        (payload, gain, slots, preconditioner, resid, update, potential),
     )
     payload = over_all(payload)
     potential, own, across, far, partner, nearby = call(
@@ -431,7 +428,7 @@
         [nodespace, nodespace, pickspace, nodespace, nodespace,
          pltpu.VMEM((512, 4096), BF16), pltpu.VMEM((256, 4096), BF16)],
         1, 40000000,
-        (whom, payload, gain, slots, stiffness, preconditioner, resid, update, potential,
+        (whom, payload, gain, slots, preconditioner, resid, update, potential,
          owner, cell, source_gain),
     )
     partner = permuted(partner, other_core)

time: 152 us -> 146 us (0.961)
  local copies, waits for them, and re-layouts: 3.87 us -> 1.01 us
  Pallas kernels: 19.7 us -> 17 us
    unnamed x15 -> x11, local copies, waits for them, and re-layouts: 2.96 us -> 0.04 us
    pallas_call x6, Pallas kernels: 19.7 us -> 17 us  [call(): pl.pallas_call(kernel, out_shape=[s if isinstance(s, jax.ShapeDtypeStruct...]
where the time goes in v2:
time: 146 us
  starting transfers between devices  58.7 us (40%)
  waiting for transfers between devices  48 us (33%)
  blocking collectives  19.7 us (13%)
  Pallas kernels  17 us (12%)
    ppermute x32, starting transfers between devices, permuted(): lax.ppermute(x, AXES, [(i, index(move(place(i)))) for i in range(128)])  52.9 us
    ppermute x32, waiting for transfers between devices, permuted(): lax.ppermute(x, AXES, [(i, index(move(place(i)))) for i in range(128)])  42.4 us
    all_to_all x1, blocking collectives, body(): blocks = lax.all_to_all(blocks, AXES, 0, 0, tiled=True)  19.7 us
    pallas_call x6, Pallas kernels, call(): pl.pallas_call(kernel, out_shape=[s if isinstance(s, jax.ShapeDtypeStruct...  17 us
    ppermute x1, waiting for transfers between devices, body(): lax.ppermute(nearby + partner[TORSO:], AXES, [(i, (i + 2 if i % 2 else i...  5.66 us
    ppermute x3, starting transfers between devices, from_behind(): return lax.ppermute(x, AXES, [(i, (i + by) % count) for i in range(count)])  3.3 us
  transfers between devices with their start and end apart: 37, of which 26 were waited for; matrix products, arithmetic and copies ran while one was open for 0% of the time, Pallas kernels for 3%

profile of v2, /device:TPU:1, one launch (start us, length us, event | category | flops | bytes accessed | tf_op | source)
XLA Modules:
  0.0 145.8 jit_solution(3742635006131507977)
XLA Ops:
  0.6 0.8 fusion
  1.4 1.4 collective-permute-start.11
  2.8 1.3 collective-permute-start.10
  4.1 4.0 %shard_map.157 = (f32[19,4096]{1,0:T(8,128)}, f32[32,128]{1,0:T(8,128)S(1)}, f32[32,128]{1,0:T(8,128)S(1)}, f32[136,128]{1,0:T(8,128)S(1)}, s32[32,128]{1,0:T(8,...) custom-call(f32[19,4096]{1,0:T(8,128)} %states_hbm.1, s32[32,128]{1,0:T(8,128)} %bitcast.18, ...), custom_call_target="tpu_custom_call" | custom-call | flops 40000000 | bytes 1048576 | tf_op jit(solution)/shard_map/pallas_call | solution.py:312
  8.1 7.0 %collective-permute-start = (f32[136,128]{1,0:T(8,128)S(1)}, f32[136,128]{1,0:T(8,128)S(1)}, u32[]{:S(2)}, u32[]{:S(2)}) collective-permute-start(f32[136,128]{1,0:T(8,128)S(1)} %get-tuple-element.29), channel_id=1, source_target_pairs={{0,1},{1,0},{2,3},{3,2},{4,5},{5,4},{6,7},{7,6},{8,9},{9,8},{10,11... | collective-permute-start | bytes 208904 | tf_op jit(solution)/shard_map/ppermute | solution.py:332
  15.1 0.1 pad_add_fusion.here_ref
  15.2 0.8 collective-permute-done
  16.0 0.1 minimum_select_fusion.3
  16.1 0.6 collective-permute-start.3
  16.7 0.9 collective-permute-start.2
  17.7 0.5 collective-permute-start.1
  18.2 1.2 collective-permute-done.3
  19.4 1.8 %collective-permute-done.2 = f32[136,128]{1,0:T(8,128)S(1)} collective-permute-done((f32[136,128]{1,0:T(8,128)S(1)}, f32[136,128]{1,0:T(8,128)S(1)}, u32[]{:S(2)}, u32[]{:S(2)}) %collective-permute-start.2) | collective-permute-done | bytes 69664 | tf_op jit(solution)/shard_map/ppermute | solution.py:332
  21.1 1.3 collective-permute-done.1
  22.4 0.1 minimum_select_fusion.2
  22.5 0.1 collective-permute-start.6
  22.6 1.5 collective-permute-start.5
  24.1 1.7 %collective-permute-done.6 = f32[136,128]{1,0:T(8,128)S(1)} collective-permute-done((f32[136,128]{1,0:T(8,128)S(1)}, f32[136,128]{1,0:T(8,128)S(1)}, u32[]{:S(2)}, u32[]{:S(2)}) %collective-permute-start.6) | collective-permute-done | bytes 69664 | tf_op jit(solution)/shard_map/ppermute | solution.py:332
  25.8 1.3 collective-permute-done.5
  27.0 1.7 %collective-permute-done.4 = f32[136,128]{1,0:T(8,128)S(1)} collective-permute-done((f32[136,128]{1,0:T(8,128)S(1)}, f32[136,128]{1,0:T(8,128)S(1)}, u32[]{:S(2)}, u32[]{:S(2)}) %collective-permute-start.4) | collective-permute-done | bytes 69664 | tf_op jit(solution)/shard_map/ppermute | solution.py:332
  28.7 0.1 minimum_select_fusion.1
  28.8 7.0 %collective-permute-start.9 = (f32[136,128]{1,0:T(8,128)S(1)}, f32[136,128]{1,0:T(8,128)S(1)}, u32[]{:S(2)}, u32[]{:S(2)}) collective-permute-start(f32[136,128]{1,0:T(8,128)S(1)} %minimum_select_fusion.1), channel_id=1, source_target_pairs={{0,6},{1,7},{2,0},{3,1},{4,2},{5,3},{6,4},{7,5},{8,14},{9,15},{10,... | collective-permute-start | bytes 208904 | tf_op jit(solution)/shard_map/ppermute | solution.py:332
  35.9 1.3 collective-permute-start.7
  37.1 0.1 collective-permute-done.9
  37.2 3.7 %collective-permute-done.8 = f32[136,128]{1,0:T(8,128)S(1)} collective-permute-done((f32[136,128]{1,0:T(8,128)S(1)}, f32[136,128]{1,0:T(8,128)S(1)}, u32[]{:S(2)}, u32[]{:S(2)}) %collective-permute-start.8) | collective-permute-done | bytes 69664 | tf_op jit(solution)/shard_map/ppermute | solution.py:332
  41.0 0.1 minimum_select_fusion.payload_ref
  41.1 3.4 %shard_map.158 = (f32[32,128]{1,0:T(8,128)S(1)}, f32[32,128]{1,0:T(8,128)S(1)}, f32[32,128]{1,0:T(8,128)S(1)}, f32[128,128]{1,0:T(8,128)S(1)}, f32[64,128]{1,0:T(8,128)S(1)}, /*index=5*/f32[8,128]{1,0:T(8,128)S(1)}) custom-call(s32[2]{0:T(128)S(1)} %pad_add_fusion.here_ref, f32[136,128]{1,0:T(8,128)S(1)} %minimum_select_fusion.payload_ref, ...), custom_call_target="tpu_custom_call" | custom-call | flops 40000000 | bytes 1048576 | tf_op jit(solution)/shard_map/pallas_call | solution.py:312
  44.5 3.7 %collective-permute-start.12 = (f32[128,128]{1,0:T(8,128)S(1)}, f32[128,128]{1,0:T(8,128)S(1)}, u32[]{:S(2)}, u32[]{:S(2)}) collective-permute-start(f32[128,128]{1,0:T(8,128)S(1)} %get-tuple-element.35), channel_id=1, source_target_pairs={{0,1},{1,0},{2,3},{3,2},{4,5},{5,4},{6,7},{7,6},{8,9},{9,8},{10,11... | collective-permute-start | bytes 196616 | tf_op jit(solution)/shard_map/ppermute | solution.py:332
  48.2 0.9 collective-permute-done.12
  49.1 2.0 %collective-permute-start.15 = (f32[128,128]{1,0:T(8,128)S(1)}, f32[128,128]{1,0:T(8,128)S(1)}, u32[]{:S(2)}, u32[]{:S(2)}) collective-permute-start(f32[128,128]{1,0:T(8,128)S(1)} %add.115), channel_id=1, source_target_pairs={{0,96},{1,97},{2,98},{3,99},{4,100},{5,101},{6,102},{7,103},{8,104... | collective-permute-start | bytes 196616 | tf_op jit(solution)/shard_map/ppermute | solution.py:332
  51.1 1.3 collective-permute-start.13
  52.4 5.0 %collective-permute-done.14 = f32[128,128]{1,0:T(8,128)S(1)} collective-permute-done((f32[128,128]{1,0:T(8,128)S(1)}, f32[128,128]{1,0:T(8,128)S(1)}, u32[]{:S(2)}, u32[]{:S(2)}) %collective-permute-start.14) | collective-permute-done | bytes 65568 | tf_op jit(solution)/shard_map/ppermute | solution.py:332
  57.5 2.6 %collective-permute-start.18 = (f32[128,128]{1,0:T(8,128)S(1)}, f32[128,128]{1,0:T(8,128)S(1)}, u32[]{:S(2)}, u32[]{:S(2)}) collective-permute-start(f32[128,128]{1,0:T(8,128)S(1)} %add_add_fusion.5), channel_id=1, source_target_pairs={{0,24},{1,25},{2,26},{3,27},{4,28},{5,29},{6,30},{7,31},{8,0},{9,1... | collective-permute-start | bytes 196616 | tf_op jit(solution)/shard_map/ppermute | solution.py:332
  60.1 1.3 collective-permute-start.16
  61.3 0.1 collective-permute-done.18
  61.4 3.7 %collective-permute-done.17 = f32[128,128]{1,0:T(8,128)S(1)} collective-permute-done((f32[128,128]{1,0:T(8,128)S(1)}, f32[128,128]{1,0:T(8,128)S(1)}, u32[]{:S(2)}, u32[]{:S(2)}) %collective-permute-start.17) | collective-permute-done | bytes 65568 | tf_op jit(solution)/shard_map/ppermute | solution.py:332
  65.1 2.6 %collective-permute-start.21 = (f32[128,128]{1,0:T(8,128)S(1)}, f32[128,128]{1,0:T(8,128)S(1)}, u32[]{:S(2)}, u32[]{:S(2)}) collective-permute-start(f32[128,128]{1,0:T(8,128)S(1)} %add_add_fusion.4), channel_id=1, source_target_pairs={{0,6},{1,7},{2,0},{3,1},{4,2},{5,3},{6,4},{7,5},{8,14},{9,15},{10,... | collective-permute-start | bytes 196616 | tf_op jit(solution)/shard_map/ppermute | solution.py:332
  67.7 1.3 collective-permute-start.19
  69.0 3.7 %collective-permute-done.20 = f32[128,128]{1,0:T(8,128)S(1)} collective-permute-done((f32[128,128]{1,0:T(8,128)S(1)}, f32[128,128]{1,0:T(8,128)S(1)}, u32[]{:S(2)}, u32[]{:S(2)}) %collective-permute-start.20) | collective-permute-done | bytes 65568 | tf_op jit(solution)/shard_map/ppermute | solution.py:332
  72.7 2.8 %shard_map.159 = (f32[32,128]{1,0:T(8,128)S(1)}, f32[32,128]{1,0:T(8,128)S(1)}, f32[32,128]{1,0:T(8,128)S(1)}, f32[128,128]{1,0:T(8,128)S(1)}) custom-call(f32[128,128]{1,0:T(8,128)S(1)} %add_add_fusion.3.payload_ref, f32[128,128]{1,0:T(8,128)S(1)} %get-tuple-element.30.gain_ref, s32[32,128]{1,0:T(8,128)S(1)} %get-tuple-element.31.slots_ref, ...), custom_call_target="tpu_custom_call" | custom-call | flops 40000000 | bytes 1048576 | tf_op jit(solution)/shard_map/pallas_call | solution.py:312
  75.6 3.7 %collective-permute-start.22 = (f32[128,128]{1,0:T(8,128)S(1)}, f32[128,128]{1,0:T(8,128)S(1)}, u32[]{:S(2)}, u32[]{:S(2)}) collective-permute-start(f32[128,128]{1,0:T(8,128)S(1)} %get-tuple-element.39), channel_id=1, source_target_pairs={{0,1},{1,0},{2,3},{3,2},{4,5},{5,4},{6,7},{7,6},{8,9},{9,8},{10,11... | collective-permute-start | bytes 196616 | tf_op jit(solution)/shard_map/ppermute | solution.py:332
  79.3 0.9 collective-permute-done.22
  80.2 2.3 %collective-permute-start.25 = (f32[128,128]{1,0:T(8,128)S(1)}, f32[128,128]{1,0:T(8,128)S(1)}, u32[]{:S(2)}, u32[]{:S(2)}) collective-permute-start(f32[128,128]{1,0:T(8,128)S(1)} %add.125), channel_id=1, source_target_pairs={{0,96},{1,97},{2,98},{3,99},{4,100},{5,101},{6,102},{7,103},{8,104... | collective-permute-start | bytes 196616 | tf_op jit(solution)/shard_map/ppermute | solution.py:332
  82.5 1.3 collective-permute-start.23
  83.8 5.0 %collective-permute-done.24 = f32[128,128]{1,0:T(8,128)S(1)} collective-permute-done((f32[128,128]{1,0:T(8,128)S(1)}, f32[128,128]{1,0:T(8,128)S(1)}, u32[]{:S(2)}, u32[]{:S(2)}) %collective-permute-start.24) | collective-permute-done | bytes 65568 | tf_op jit(solution)/shard_map/ppermute | solution.py:332
  88.9 2.6 %collective-permute-start.28 = (f32[128,128]{1,0:T(8,128)S(1)}, f32[128,128]{1,0:T(8,128)S(1)}, u32[]{:S(2)}, u32[]{:S(2)}) collective-permute-start(f32[128,128]{1,0:T(8,128)S(1)} %add_add_fusion.2), channel_id=1, source_target_pairs={{0,24},{1,25},{2,26},{3,27},{4,28},{5,29},{6,30},{7,31},{8,0},{9,1... | collective-permute-start | bytes 196616 | tf_op jit(solution)/shard_map/ppermute | solution.py:332
  91.5 1.3 collective-permute-start.26
  92.8 3.7 %collective-permute-done.27 = f32[128,128]{1,0:T(8,128)S(1)} collective-permute-done((f32[128,128]{1,0:T(8,128)S(1)}, f32[128,128]{1,0:T(8,128)S(1)}, u32[]{:S(2)}, u32[]{:S(2)}) %collective-permute-start.27) | collective-permute-done | bytes 65568 | tf_op jit(solution)/shard_map/ppermute | solution.py:332
  96.5 2.6 %collective-permute-start.31 = (f32[128,128]{1,0:T(8,128)S(1)}, f32[128,128]{1,0:T(8,128)S(1)}, u32[]{:S(2)}, u32[]{:S(2)}) collective-permute-start(f32[128,128]{1,0:T(8,128)S(1)} %add_add_fusion.1), channel_id=1, source_target_pairs={{0,6},{1,7},{2,0},{3,1},{4,2},{5,3},{6,4},{7,5},{8,14},{9,15},{10,... | collective-permute-start | bytes 196616 | tf_op jit(solution)/shard_map/ppermute | solution.py:332
  99.1 1.3 collective-permute-start.29
  100.5 3.7 %collective-permute-done.30 = f32[128,128]{1,0:T(8,128)S(1)} collective-permute-done((f32[128,128]{1,0:T(8,128)S(1)}, f32[128,128]{1,0:T(8,128)S(1)}, u32[]{:S(2)}, u32[]{:S(2)}) %collective-permute-start.30) | collective-permute-done | bytes 65568 | tf_op jit(solution)/shard_map/ppermute | solution.py:332
  104.2 4.7 %shard_map.160 = (f32[32,128]{1,0:T(8,128)}, f32[64,128]{1,0:T(8,128)S(1)}, f32[64,128]{1,0:T(8,128)S(1)}, f32[64,128]{1,0:T(8,128)S(1)}, f32[192,128]{1,0:T(8,128)S(1)}, /*index=5*/f32[128,128]{1,0:T(8,128)S(1)}) custom-call(s32[2]{0:T(128)S(1)} %pad_add_fusion.here_ref, f32[128,128]{1,0:T(8,128)S(1)} %add_add_fusion.payload_ref, ...), custom_call_target="tpu_custom_call" | custom-call | flops 40000000 | bytes 1048576 | tf_op jit(solution)/shard_map/pallas_call | solution.py:312
  109.0 3.7 %collective-permute-start.34 = (f32[192,128]{1,0:T(8,128)S(1)}, f32[192,128]{1,0:T(8,128)S(1)}, u32[]{:S(2)}, u32[]{:S(2)}) collective-permute-start(f32[192,128]{1,0:T(8,128)S(1)} %get-tuple-element.48), channel_id=1, source_target_pairs={{0,1},{1,0},{2,3},{3,2},{4,5},{5,4},{6,7},{7,6},{8,9},{9,8},{10,11... | collective-permute-start | bytes 294920 | tf_op jit(solution)/shard_map/ppermute | solution.py:332
  112.7 0.9 collective-permute-done.34.partner_ref
  113.6 0.1 collective-permute-start.35
  113.7 0.6 collective-permute-start.32
  114.4 2.4 %collective-permute-start.33 = (f32[64,128]{1,0:T(8,128)S(1)}, f32[64,128]{1,0:T(8,128)S(1)}, u32[]{:S(2)}, u32[]{:S(2)}) collective-permute-start(f32[64,128]{1,0:T(8,128)S(1)} %get-tuple-element.47), channel_id=1, source_target_pairs={{0,125},{1,4},{2,127},{3,6},{4,1},{5,8},{6,3},{7,10},{8,5},{9,12},... | collective-permute-start | bytes 98312 | tf_op jit(solution)/shard_map/ppermute | solution.py:435
  116.7 5.7 %collective-permute-done.35.next_ref = f32[128,128]{1,0:T(8,128)S(1)} collective-permute-done((f32[128,128]{1,0:T(8,128)S(1)}, f32[128,128]{1,0:T(8,128)S(1)}, u32[]{:S(2)}, u32[]{:S(2)}) %collective-permute-start.35) | collective-permute-done | bytes 65568 | tf_op jit(solution)/shard_map/ppermute | solution.py:437
  122.4 0.6 collective-permute-start.36
  123.0 0.9 collective-permute-done.36.handed_ref
  123.9 0.6 shard_map.161
  124.5 0.2 copy.17
  124.7 19.7 %all_to_all.11 = f32[128,1,384]{2,1,0:T(1,128)S(1)} all-to-all(f32[128,1,384]{2,1,0:T(1,128)S(1)} %copy.17), channel_id=1, replica_groups=mesh['a'=4,'b'=4,'c'=4,'d'=2] {'a','b','c','d'}, dimensions={0} | all-to-all | bytes 393216 | tf_op jit(solution)/shard_map/all_to_all | solution.py:447
  144.4 1.4 shard_map.162
  (47 shorter events, 0.6 us)
Async XLA Ops:
  0.6 23.4 %copy-start.3 = (f32[64,128]{1,0:T(8,128)S(1)}, f32[64,128]{1,0:T(8,128)}, u32[]{:S(2)}) copy-start(f32[64,128]{1,0:T(8,128)} %conduct_hbm.1) | copy-start | bytes 98308
  1.4 35.7 %collective-permute-start.11 = (f32[8,128]{1,0:T(8,128)S(1)}, f32[8,128]{1,0:T(8,128)S(1)}, u32[]{:S(2)}, u32[]{:S(2)}) collective-permute-start(f32[8,128]{1,0:T(8,128)S(1)} %get-tuple-element.53), channel_id=1, source_target_pairs={{0,127},{1,0},{2,1},{3,2},{4,3},{5,4},{6,5},{7,6},{8,7},{9,8},{10,... | collective-permute-start | bytes 12296 | tf_op jit(solution)/shard_map/ppermute | solution.py:370
  2.8 15.4 %collective-permute-start.10 = (f32[8,128]{1,0:T(8,128)S(1)}, f32[8,128]{1,0:T(8,128)S(1)}, u32[]{:S(2)}, u32[]{:S(2)}) collective-permute-start(f32[8,128]{1,0:T(8,128)S(1)} %get-tuple-element.54), channel_id=1, source_target_pairs={{0,1},{1,2},{2,3},{3,4},{4,5},{5,6},{6,7},{7,8},{8,9},{9,10},{10,1... | collective-permute-start | bytes 12296 | tf_op jit(solution)/shard_map/ppermute | solution.py:370
  8.1 7.9 %collective-permute-start = (f32[136,128]{1,0:T(8,128)S(1)}, f32[136,128]{1,0:T(8,128)S(1)}, u32[]{:S(2)}, u32[]{:S(2)}) collective-permute-start(f32[136,128]{1,0:T(8,128)S(1)} %get-tuple-element.29), channel_id=1, source_target_pairs={{0,1},{1,0},{2,3},{3,2},{4,5},{5,4},{6,7},{7,6},{8,9},{9,8},{10,11... | collective-permute-start | bytes 208904 | tf_op jit(solution)/shard_map/ppermute | solution.py:332
  16.1 3.2 %collective-permute-start.3 = (f32[136,128]{1,0:T(8,128)S(1)}, f32[136,128]{1,0:T(8,128)S(1)}, u32[]{:S(2)}, u32[]{:S(2)}) collective-permute-start(f32[136,128]{1,0:T(8,128)S(1)} %minimum_select_fusion.3), channel_id=1, source_target_pairs={{0,96},{1,97},{2,98},{3,99},{4,100},{5,101},{6,102},{7,103},{8,104... | collective-permute-start | bytes 208904 | tf_op jit(solution)/shard_map/ppermute | solution.py:332
  16.7 4.4 %collective-permute-start.2 = (f32[136,128]{1,0:T(8,128)S(1)}, f32[136,128]{1,0:T(8,128)S(1)}, u32[]{:S(2)}, u32[]{:S(2)}) collective-permute-start(f32[136,128]{1,0:T(8,128)S(1)} %minimum_select_fusion.3), channel_id=1, source_target_pairs={{0,32},{1,33},{2,34},{3,35},{4,36},{5,37},{6,38},{7,39},{8,40},{9,... | collective-permute-start | bytes 208904 | tf_op jit(solution)/shard_map/ppermute | solution.py:332
  17.7 4.8 %collective-permute-start.1 = (f32[136,128]{1,0:T(8,128)S(1)}, f32[136,128]{1,0:T(8,128)S(1)}, u32[]{:S(2)}, u32[]{:S(2)}) collective-permute-start(f32[136,128]{1,0:T(8,128)S(1)} %minimum_select_fusion.3), channel_id=1, source_target_pairs={{0,64},{1,65},{2,66},{3,67},{4,68},{5,69},{6,70},{7,71},{8,72},{9,... | collective-permute-start | bytes 208904 | tf_op jit(solution)/shard_map/ppermute | solution.py:332
  22.5 3.2 %collective-permute-start.6 = (f32[136,128]{1,0:T(8,128)S(1)}, f32[136,128]{1,0:T(8,128)S(1)}, u32[]{:S(2)}, u32[]{:S(2)}) collective-permute-start(f32[136,128]{1,0:T(8,128)S(1)} %minimum_select_fusion.2), channel_id=1, source_target_pairs={{0,24},{1,25},{2,26},{3,27},{4,28},{5,29},{6,30},{7,31},{8,0},{9,1... | collective-permute-start | bytes 208904 | tf_op jit(solution)/shard_map/ppermute | solution.py:332
  22.6 4.4 %collective-permute-start.5 = (f32[136,128]{1,0:T(8,128)S(1)}, f32[136,128]{1,0:T(8,128)S(1)}, u32[]{:S(2)}, u32[]{:S(2)}) collective-permute-start(f32[136,128]{1,0:T(8,128)S(1)} %minimum_select_fusion.2), channel_id=1, source_target_pairs={{0,8},{1,9},{2,10},{3,11},{4,12},{5,13},{6,14},{7,15},{8,16},{9,17... | collective-permute-start | bytes 208904 | tf_op jit(solution)/shard_map/ppermute | solution.py:332
  24.1 4.7 %collective-permute-start.4 = (f32[136,128]{1,0:T(8,128)S(1)}, f32[136,128]{1,0:T(8,128)S(1)}, u32[]{:S(2)}, u32[]{:S(2)}) collective-permute-start(f32[136,128]{1,0:T(8,128)S(1)} %minimum_select_fusion.2), channel_id=1, source_target_pairs={{0,16},{1,17},{2,18},{3,19},{4,20},{5,21},{6,22},{7,23},{8,24},{9,... | collective-permute-start | bytes 208904 | tf_op jit(solution)/shard_map/ppermute | solution.py:332
  28.8 8.4 %collective-permute-start.9 = (f32[136,128]{1,0:T(8,128)S(1)}, f32[136,128]{1,0:T(8,128)S(1)}, u32[]{:S(2)}, u32[]{:S(2)}) collective-permute-start(f32[136,128]{1,0:T(8,128)S(1)} %minimum_select_fusion.1), channel_id=1, source_target_pairs={{0,6},{1,7},{2,0},{3,1},{4,2},{5,3},{6,4},{7,5},{8,14},{9,15},{10,... | collective-permute-start | bytes 208904 | tf_op jit(solution)/shard_map/ppermute | solution.py:332
  35.9 5.1 %collective-permute-start.8 = (f32[136,128]{1,0:T(8,128)S(1)}, f32[136,128]{1,0:T(8,128)S(1)}, u32[]{:S(2)}, u32[]{:S(2)}) collective-permute-start(f32[136,128]{1,0:T(8,128)S(1)} %minimum_select_fusion.1), channel_id=1, source_target_pairs={{0,2},{1,3},{2,4},{3,5},{4,6},{5,7},{6,0},{7,1},{8,10},{9,11},{10,... | collective-permute-start | bytes 208904 | tf_op jit(solution)/shard_map/ppermute | solution.py:332
  35.9 5.1 %collective-permute-start.7 = (f32[136,128]{1,0:T(8,128)S(1)}, f32[136,128]{1,0:T(8,128)S(1)}, u32[]{:S(2)}, u32[]{:S(2)}) collective-permute-start(f32[136,128]{1,0:T(8,128)S(1)} %minimum_select_fusion.1), channel_id=1, source_target_pairs={{0,4},{1,5},{2,6},{3,7},{4,0},{5,1},{6,2},{7,3},{8,12},{9,13},{10,... | collective-permute-start | bytes 208904 | tf_op jit(solution)/shard_map/ppermute | solution.py:332
  44.5 4.6 %collective-permute-start.12 = (f32[128,128]{1,0:T(8,128)S(1)}, f32[128,128]{1,0:T(8,128)S(1)}, u32[]{:S(2)}, u32[]{:S(2)}) collective-permute-start(f32[128,128]{1,0:T(8,128)S(1)} %get-tuple-element.35), channel_id=1, source_target_pairs={{0,1},{1,0},{2,3},{3,2},{4,5},{5,4},{6,7},{7,6},{8,9},{9,8},{10,11... | collective-permute-start | bytes 196616 | tf_op jit(solution)/shard_map/ppermute | solution.py:332
  49.1 3.3 %collective-permute-start.15 = (f32[128,128]{1,0:T(8,128)S(1)}, f32[128,128]{1,0:T(8,128)S(1)}, u32[]{:S(2)}, u32[]{:S(2)}) collective-permute-start(f32[128,128]{1,0:T(8,128)S(1)} %add.115), channel_id=1, source_target_pairs={{0,96},{1,97},{2,98},{3,99},{4,100},{5,101},{6,102},{7,103},{8,104... | collective-permute-start | bytes 196616 | tf_op jit(solution)/shard_map/ppermute | solution.py:332
  51.1 6.3 %collective-permute-start.14 = (f32[128,128]{1,0:T(8,128)S(1)}, f32[128,128]{1,0:T(8,128)S(1)}, u32[]{:S(2)}, u32[]{:S(2)}) collective-permute-start(f32[128,128]{1,0:T(8,128)S(1)} %add.115), channel_id=1, source_target_pairs={{0,32},{1,33},{2,34},{3,35},{4,36},{5,37},{6,38},{7,39},{8,40},{9,... | collective-permute-start | bytes 196616 | tf_op jit(solution)/shard_map/ppermute | solution.py:332
  51.1 6.3 %collective-permute-start.13 = (f32[128,128]{1,0:T(8,128)S(1)}, f32[128,128]{1,0:T(8,128)S(1)}, u32[]{:S(2)}, u32[]{:S(2)}) collective-permute-start(f32[128,128]{1,0:T(8,128)S(1)} %add.115), channel_id=1, source_target_pairs={{0,64},{1,65},{2,66},{3,67},{4,68},{5,69},{6,70},{7,71},{8,72},{9,... | collective-permute-start | bytes 196616 | tf_op jit(solution)/shard_map/ppermute | solution.py:332
  57.5 46.7 %copy-start = (s32[4096,1]{0,1:T(1,128)S(1)}, s32[4096,1]{0,1:T(1,128)}, u32[]{:S(2)}) copy-start(s32[4096,1]{0,1:T(1,128)} %param.25) | copy-start | bytes 49156
  57.5 46.7 %copy-start.1 = (s32[4096]{0:T(1024)S(1)}, s32[4096]{0:T(1024)}, u32[]{:S(2)}) copy-start(s32[4096]{0:T(1024)} %param.26) | copy-start | bytes 49156
  57.5 46.7 %copy-start.2 = (f32[4096]{0:T(1024)S(1)}, f32[4096]{0:T(1024)}, u32[]{:S(2)}) copy-start(f32[4096]{0:T(1024)} %param.27) | copy-start | bytes 49156
  57.5 3.9 %collective-permute-start.18 = (f32[128,128]{1,0:T(8,128)S(1)}, f32[128,128]{1,0:T(8,128)S(1)}, u32[]{:S(2)}, u32[]{:S(2)}) collective-permute-start(f32[128,128]{1,0:T(8,128)S(1)} %add_add_fusion.5), channel_id=1, source_target_pairs={{0,24},{1,25},{2,26},{3,27},{4,28},{5,29},{6,30},{7,31},{8,0},{9,1... | collective-permute-start | bytes 196616 | tf_op jit(solution)/shard_map/ppermute | solution.py:332
  60.1 5.0 %collective-permute-start.17 = (f32[128,128]{1,0:T(8,128)S(1)}, f32[128,128]{1,0:T(8,128)S(1)}, u32[]{:S(2)}, u32[]{:S(2)}) collective-permute-start(f32[128,128]{1,0:T(8,128)S(1)} %add_add_fusion.5), channel_id=1, source_target_pairs={{0,8},{1,9},{2,10},{3,11},{4,12},{5,13},{6,14},{7,15},{8,16},{9,17... | collective-permute-start | bytes 196616 | tf_op jit(solution)/shard_map/ppermute | solution.py:332
  60.1 5.0 %collective-permute-start.16 = (f32[128,128]{1,0:T(8,128)S(1)}, f32[128,128]{1,0:T(8,128)S(1)}, u32[]{:S(2)}, u32[]{:S(2)}) collective-permute-start(f32[128,128]{1,0:T(8,128)S(1)} %add_add_fusion.5), channel_id=1, source_target_pairs={{0,16},{1,17},{2,18},{3,19},{4,20},{5,21},{6,22},{7,23},{8,24},{9,... | collective-permute-start | bytes 196616 | tf_op jit(solution)/shard_map/ppermute | solution.py:332
  65.1 3.9 %collective-permute-start.21 = (f32[128,128]{1,0:T(8,128)S(1)}, f32[128,128]{1,0:T(8,128)S(1)}, u32[]{:S(2)}, u32[]{:S(2)}) collective-permute-start(f32[128,128]{1,0:T(8,128)S(1)} %add_add_fusion.4), channel_id=1, source_target_pairs={{0,6},{1,7},{2,0},{3,1},{4,2},{5,3},{6,4},{7,5},{8,14},{9,15},{10,... | collective-permute-start | bytes 196616 | tf_op jit(solution)/shard_map/ppermute | solution.py:332
  67.7 5.0 %collective-permute-start.20 = (f32[128,128]{1,0:T(8,128)S(1)}, f32[128,128]{1,0:T(8,128)S(1)}, u32[]{:S(2)}, u32[]{:S(2)}) collective-permute-start(f32[128,128]{1,0:T(8,128)S(1)} %add_add_fusion.4), channel_id=1, source_target_pairs={{0,2},{1,3},{2,4},{3,5},{4,6},{5,7},{6,0},{7,1},{8,10},{9,11},{10,... | collective-permute-start | bytes 196616 | tf_op jit(solution)/shard_map/ppermute | solution.py:332
  67.7 5.0 %collective-permute-start.19 = (f32[128,128]{1,0:T(8,128)S(1)}, f32[128,128]{1,0:T(8,128)S(1)}, u32[]{:S(2)}, u32[]{:S(2)}) collective-permute-start(f32[128,128]{1,0:T(8,128)S(1)} %add_add_fusion.4), channel_id=1, source_target_pairs={{0,4},{1,5},{2,6},{3,7},{4,0},{5,1},{6,2},{7,3},{8,12},{9,13},{10,... | collective-permute-start | bytes 196616 | tf_op jit(solution)/shard_map/ppermute | solution.py:332
  75.6 4.6 %collective-permute-start.22 = (f32[128,128]{1,0:T(8,128)S(1)}, f32[128,128]{1,0:T(8,128)S(1)}, u32[]{:S(2)}, u32[]{:S(2)}) collective-permute-start(f32[128,128]{1,0:T(8,128)S(1)} %get-tuple-element.39), channel_id=1, source_target_pairs={{0,1},{1,0},{2,3},{3,2},{4,5},{5,4},{6,7},{7,6},{8,9},{9,8},{10,11... | collective-permute-start | bytes 196616 | tf_op jit(solution)/shard_map/ppermute | solution.py:332
  80.2 3.6 %collective-permute-start.25 = (f32[128,128]{1,0:T(8,128)S(1)}, f32[128,128]{1,0:T(8,128)S(1)}, u32[]{:S(2)}, u32[]{:S(2)}) collective-permute-start(f32[128,128]{1,0:T(8,128)S(1)} %add.125), channel_id=1, source_target_pairs={{0,96},{1,97},{2,98},{3,99},{4,100},{5,101},{6,102},{7,103},{8,104... | collective-permute-start | bytes 196616 | tf_op jit(solution)/shard_map/ppermute | solution.py:332
  82.5 6.3 %collective-permute-start.24 = (f32[128,128]{1,0:T(8,128)S(1)}, f32[128,128]{1,0:T(8,128)S(1)}, u32[]{:S(2)}, u32[]{:S(2)}) collective-permute-start(f32[128,128]{1,0:T(8,128)S(1)} %add.125), channel_id=1, source_target_pairs={{0,32},{1,33},{2,34},{3,35},{4,36},{5,37},{6,38},{7,39},{8,40},{9,... | collective-permute-start | bytes 196616 | tf_op jit(solution)/shard_map/ppermute | solution.py:332
  82.5 6.3 %collective-permute-start.23 = (f32[128,128]{1,0:T(8,128)S(1)}, f32[128,128]{1,0:T(8,128)S(1)}, u32[]{:S(2)}, u32[]{:S(2)}) collective-permute-start(f32[128,128]{1,0:T(8,128)S(1)} %add.125), channel_id=1, source_target_pairs={{0,64},{1,65},{2,66},{3,67},{4,68},{5,69},{6,70},{7,71},{8,72},{9,... | collective-permute-start | bytes 196616 | tf_op jit(solution)/shard_map/ppermute | solution.py:332
  88.9 3.9 %collective-permute-start.28 = (f32[128,128]{1,0:T(8,128)S(1)}, f32[128,128]{1,0:T(8,128)S(1)}, u32[]{:S(2)}, u32[]{:S(2)}) collective-permute-start(f32[128,128]{1,0:T(8,128)S(1)} %add_add_fusion.2), channel_id=1, source_target_pairs={{0,24},{1,25},{2,26},{3,27},{4,28},{5,29},{6,30},{7,31},{8,0},{9,1... | collective-permute-start | bytes 196616 | tf_op jit(solution)/shard_map/ppermute | solution.py:332
  91.5 5.0 %collective-permute-start.27 = (f32[128,128]{1,0:T(8,128)S(1)}, f32[128,128]{1,0:T(8,128)S(1)}, u32[]{:S(2)}, u32[]{:S(2)}) collective-permute-start(f32[128,128]{1,0:T(8,128)S(1)} %add_add_fusion.2), channel_id=1, source_target_pairs={{0,8},{1,9},{2,10},{3,11},{4,12},{5,13},{6,14},{7,15},{8,16},{9,17... | collective-permute-start | bytes 196616 | tf_op jit(solution)/shard_map/ppermute | solution.py:332
  91.5 5.0 %collective-permute-start.26 = (f32[128,128]{1,0:T(8,128)S(1)}, f32[128,128]{1,0:T(8,128)S(1)}, u32[]{:S(2)}, u32[]{:S(2)}) collective-permute-start(f32[128,128]{1,0:T(8,128)S(1)} %add_add_fusion.2), channel_id=1, source_target_pairs={{0,16},{1,17},{2,18},{3,19},{4,20},{5,21},{6,22},{7,23},{8,24},{9,... | collective-permute-start | bytes 196616 | tf_op jit(solution)/shard_map/ppermute | solution.py:332
  96.5 3.9 %collective-permute-start.31 = (f32[128,128]{1,0:T(8,128)S(1)}, f32[128,128]{1,0:T(8,128)S(1)}, u32[]{:S(2)}, u32[]{:S(2)}) collective-permute-start(f32[128,128]{1,0:T(8,128)S(1)} %add_add_fusion.1), channel_id=1, source_target_pairs={{0,6},{1,7},{2,0},{3,1},{4,2},{5,3},{6,4},{7,5},{8,14},{9,15},{10,... | collective-permute-start | bytes 196616 | tf_op jit(solution)/shard_map/ppermute | solution.py:332
  99.1 5.0 %collective-permute-start.30 = (f32[128,128]{1,0:T(8,128)S(1)}, f32[128,128]{1,0:T(8,128)S(1)}, u32[]{:S(2)}, u32[]{:S(2)}) collective-permute-start(f32[128,128]{1,0:T(8,128)S(1)} %add_add_fusion.1), channel_id=1, source_target_pairs={{0,2},{1,3},{2,4},{3,5},{4,6},{5,7},{6,0},{7,1},{8,10},{9,11},{10,... | collective-permute-start | bytes 196616 | tf_op jit(solution)/shard_map/ppermute | solution.py:332
  99.1 5.0 %collective-permute-start.29 = (f32[128,128]{1,0:T(8,128)S(1)}, f32[128,128]{1,0:T(8,128)S(1)}, u32[]{:S(2)}, u32[]{:S(2)}) collective-permute-start(f32[128,128]{1,0:T(8,128)S(1)} %add_add_fusion.1), channel_id=1, source_target_pairs={{0,4},{1,5},{2,6},{3,7},{4,0},{5,1},{6,2},{7,3},{8,12},{9,13},{10,... | collective-permute-start | bytes 196616 | tf_op jit(solution)/shard_map/ppermute | solution.py:332
  109.0 4.7 %collective-permute-start.34 = (f32[192,128]{1,0:T(8,128)S(1)}, f32[192,128]{1,0:T(8,128)S(1)}, u32[]{:S(2)}, u32[]{:S(2)}) collective-permute-start(f32[192,128]{1,0:T(8,128)S(1)} %get-tuple-element.48), channel_id=1, source_target_pairs={{0,1},{1,0},{2,3},{3,2},{4,5},{5,4},{6,7},{7,6},{8,9},{9,8},{10,11... | collective-permute-start | bytes 294920 | tf_op jit(solution)/shard_map/ppermute | solution.py:332
  113.6 8.7 %collective-permute-start.35 = (f32[128,128]{1,0:T(8,128)S(1)}, f32[128,128]{1,0:T(8,128)S(1)}, u32[]{:S(2)}, u32[]{:S(2)}) collective-permute-start(f32[128,128]{1,0:T(8,128)S(1)} %slice_add_fusion), channel_id=1, source_target_pairs={{0,126},{1,3},{2,0},{3,5},{4,2},{5,7},{6,4},{7,9},{8,6},{9,11},{10... | collective-permute-start | bytes 196616 | tf_op jit(solution)/shard_map/ppermute | solution.py:437
  113.7 9.3 %collective-permute-start.32 = (f32[64,128]{1,0:T(8,128)S(1)}, f32[64,128]{1,0:T(8,128)S(1)}, u32[]{:S(2)}, u32[]{:S(2)}) collective-permute-start(f32[64,128]{1,0:T(8,128)S(1)} %get-tuple-element.46), channel_id=1, source_target_pairs={{0,64},{1,65},{2,66},{3,67},{4,68},{5,69},{6,70},{7,71},{8,72},{9,... | collective-permute-start | bytes 98312 | tf_op jit(solution)/shard_map/ppermute | solution.py:370
  114.4 8.7 %collective-permute-start.33 = (f32[64,128]{1,0:T(8,128)S(1)}, f32[64,128]{1,0:T(8,128)S(1)}, u32[]{:S(2)}, u32[]{:S(2)}) collective-permute-start(f32[64,128]{1,0:T(8,128)S(1)} %get-tuple-element.47), channel_id=1, source_target_pairs={{0,125},{1,4},{2,127},{3,6},{4,1},{5,8},{6,3},{7,10},{8,5},{9,12},... | collective-permute-start | bytes 98312 | tf_op jit(solution)/shard_map/ppermute | solution.py:435
  122.4 1.5 %collective-permute-start.36 = (f32[64,128]{1,0:T(8,128)S(1)}, f32[64,128]{1,0:T(8,128)S(1)}, u32[]{:S(2)}, u32[]{:S(2)}) collective-permute-start(f32[64,128]{1,0:T(8,128)S(1)} %slice.17), channel_id=1, source_target_pairs={{0,1},{1,0},{2,3},{3,2},{4,5},{5,4},{6,7},{7,6},{8,9},{9,8},{10,11... | collective-permute-start | bytes 98312 | tf_op jit(solution)/shard_map/ppermute | solution.py:332

commit v3 on v2

--- a/solution.py
+++ b/solution.py
@@ -48,34 +48,48 @@
     out_ref[...] = jnp.transpose(columns)[:TILES, :]
 
 
-def slot_sums(slots_ref, w_ref, row_ref, col_ref):
+def one_hot_rows(slots_ref, pick_ref):
     down = lax.broadcasted_iota(jnp.int32, (LANES, LANES), 0)
     for t in range(TILES):
         here = slice(t * LANES, (t + 1) * LANES)
-        slot = slots_ref[t : t + 1, :]
-        high, low = high_low(w_ref[t : t + 1, :])
-        match = down == (slot >> 7)
-        row_ref[0:LANES, here] = jnp.where(match, high, 0.0).astype(BF16)
-        row_ref[LANES:, here] = jnp.where(match, low, 0.0).astype(BF16)
-        col_ref[:, here] = jnp.where(down == (slot & 127), 1.0, 0.0).astype(BF16)
+        match = down == (slots_ref[t : t + 1, :] >> 7)
+        pick_ref[:, here] = jnp.where(match, 1.0, 0.0).astype(BF16)
+
+
+def scaled_rows(w, pick_ref, count, row_ref):
+    high, low = high_low(w)
+    high, low = high.astype(BF16), low.astype(BF16)
+    for t in range(TILES):
+        here = slice(t * LANES, (t + 1) * LANES)
+        row_ref[0:count, here] = pick_ref[0:count, here] * high[t : t + 1, :]
+        row_ref[count:, here] = pick_ref[0:count, here] * low[t : t + 1, :]
+
+
+def products(row_ref, col_ref, count):
     both = lax.dot_general(
         row_ref[...], col_ref[...], (((1,), (1,)), ((), ())), preferred_element_type=F32
     )
-    return both[:LANES] + both[LANES:]
+    return both[:count] + both[count:]
+
+
+def slot_sums(slots_ref, w_ref, pick_ref, col_ref, row_ref):
+    down = lax.broadcasted_iota(jnp.int32, (LANES, LANES), 0)
+    for t in range(TILES):
+        here = slice(t * LANES, (t + 1) * LANES)
+        match = down == (slots_ref[t : t + 1, :] & 127)
+        col_ref[:, here] = jnp.where(match, 1.0, 0.0).astype(BF16)
+    scaled_rows(w_ref[...], pick_ref, LANES, row_ref)
+    return products(row_ref, col_ref, LANES)
 
 
 def slot_values(slots_ref, values, pick_ref, out_ref):
     down = lax.broadcasted_iota(jnp.int32, (LANES, LANES), 0)
     high, low = high_low(jnp.transpose(values))
-    table = jnp.concatenate([high.astype(BF16), low.astype(BF16)], axis=1)
-    for t in range(TILES):
-        here = slice(t * LANES, (t + 1) * LANES)
-        match = jnp.where(down == (slots_ref[t : t + 1, :] >> 7), 1.0, 0.0).astype(BF16)
-        pick_ref[0:LANES, here] = match
-        pick_ref[LANES:, here] = match
-    for t in range(TILES):
-        here = slice(t * LANES, (t + 1) * LANES)
-        rows = jnp.dot(table, pick_ref[:, here], preferred_element_type=F32)
+    high, low = high.astype(BF16), low.astype(BF16)
+    for t in range(TILES):
+        here = slice(t * LANES, (t + 1) * LANES)
+        rows = jnp.dot(high, pick_ref[:, here], preferred_element_type=F32)
+        rows = rows + jnp.dot(low, pick_ref[:, here], preferred_element_type=F32)
         chosen = jnp.where(down == (slots_ref[t : t + 1, :] & 127), rows, 0.0)
         out_ref[t : t + 1, :] = jnp.sum(chosen, axis=0, keepdims=True)
 
@@ -84,6 +98,7 @@
     states_hbm, region_hbm, half_hbm, slope_hbm, rate_hbm, cond_hbm, rev_hbm,
     slots_hbm, conduct_hbm, gain_hbm, precond_hbm,
     states_out, resid_out, update_out, payload_out, slots_out, gain_out, precond_out,
+    pick_out, top_out, bottom_out,
     states_ref, region_ref, half_ref, slope_ref, rate_ref, cond_ref, rev_ref,
     conduct_ref, table_ref, volt_ref, row_ref, col_ref, sems,
 ):
@@ -132,11 +147,16 @@
         volt_ref[t : t + 1, :] = new_volt
     for copy in copies[7:9]:
         copy.wait()
+    top_out[...] = conduct_ref[0:8, :]
+    bottom_out[...] = conduct_ref[TORSO - 8 :, :]
     payload_out[SLOT_ROWS:, :] = jnp.min(conduct_ref[...].reshape(8, 8, LANES), axis=0)
     volt = volt_ref[...]
     resid_out[...] = volt
     update_out[...] = volt * (1.0 / CENTER)
-    payload_out[0:SLOT_ROWS, :] = slot_sums(slots_out, update_out, row_ref, col_ref)
+    one_hot_rows(slots_out, pick_out)
+    payload_out[0:SLOT_ROWS, :] = slot_sums(
+        slots_out, update_out, pick_out, col_ref, row_ref
+    )
     for copy in copies[9:]:
         copy.wait()
 
@@ -191,15 +211,15 @@
 
 
 def first_step_kernel(
-    here_ref, payload_ref, gain_ref, slots_ref, precond_ref, resid_ref, update_ref, conduct_ref,
+    here_ref, payload_ref, gain_ref, slots_ref, precond_ref, pick_ref, resid_ref, update_ref, conduct_ref,
     resid_out, update_out, potential_out, payload_out, weight_out, smallest_out,
-    coupled_ref, work_ref, pick_ref, row_ref, col_ref,
+    coupled_ref, work_ref, row_ref, col_ref,
 ):
     heart_step(
         0, payload_ref, gain_ref, slots_ref, precond_ref, resid_ref, update_ref,
         update_ref, coupled_ref, work_ref, pick_ref, resid_out, update_out, potential_out,
     )
-    payload_out[...] = slot_sums(slots_ref, update_out, row_ref, col_ref)
+    payload_out[...] = slot_sums(slots_ref, update_out, pick_ref, col_ref, row_ref)
     smallest = jnp.min(jnp.min(payload_ref[SLOT_ROWS:, :], axis=0, keepdims=True), axis=1, keepdims=True)
     smallest_out[...] = jnp.broadcast_to(smallest, (8, LANES))
     ones = jnp.ones((TORSO + 16, LANES), F32)
@@ -210,27 +230,18 @@
 
 
 def second_step_kernel(
-    payload_ref, gain_ref, slots_ref, precond_ref, resid_ref, update_ref, potential_ref,
+    payload_ref, gain_ref, slots_ref, precond_ref, pick_ref, resid_ref, update_ref, potential_ref,
     resid_out, update_out, potential_out, payload_out,
-    coupled_ref, work_ref, pick_ref, row_ref, col_ref,
+    coupled_ref, work_ref, row_ref, col_ref,
 ):
     heart_step(
         1, payload_ref, gain_ref, slots_ref, precond_ref, resid_ref, update_ref,
         potential_ref, coupled_ref, work_ref, pick_ref, resid_out, update_out, potential_out,
     )
-    payload_out[...] = slot_sums(slots_ref, update_out, row_ref, col_ref)
-
-
-def last_step_kernel(
-    here_ref, payload_ref, gain_ref, slots_ref, precond_ref, resid_ref, update_ref,
-    potential_ref, owner_ref, cell_ref, scale_ref,
-    potential_out, own_out, across_out, far_out, partner_out, next_out,
-    coupled_ref, work_ref, pick_ref, resid_out, update_out, row_ref, col_ref,
-):
-    heart_step(
-        2, payload_ref, gain_ref, slots_ref, precond_ref, resid_ref, update_ref,
-        potential_ref, coupled_ref, work_ref, pick_ref, resid_out, update_out, potential_out,
-    )
+    payload_out[...] = slot_sums(slots_ref, update_out, pick_ref, col_ref, row_ref)
+
+
+def target_kernel(here_ref, after_ref, owner_ref, cell_ref, row_out, col_out):
     devices = here_ref[1]
     me = here_ref[0]
     ahead = owner_ref[...] - me + devices
@@ -242,19 +253,25 @@
     cell = cell_ref[...]
     row = (kind & 3) * TORSO + (cell >> 7)
     col = (kind >> 2) * LANES + (cell & 127)
-    deposit = potential_out[...] * scale_ref[...]
     down = lax.broadcasted_iota(jnp.int32, (256, LANES), 0)
     for t in range(TILES):
         here = slice(t * LANES, (t + 1) * LANES)
-        high, low = high_low(deposit[t : t + 1, :])
-        match = down == row[t : t + 1, :]
-        row_ref[0:256, here] = jnp.where(match, high, 0.0).astype(BF16)
-        row_ref[256:, here] = jnp.where(match, low, 0.0).astype(BF16)
-        col_ref[:, here] = jnp.where(down == col[t : t + 1, :], 1.0, 0.0).astype(BF16)
-    both = lax.dot_general(
-        row_ref[...], col_ref[...], (((1,), (1,)), ((), ())), preferred_element_type=F32
-    )
-    both = both[:256] + both[256:]
+        row_out[:, here] = jnp.where(down == row[t : t + 1, :], 1.0, 0.0).astype(BF16)
+        col_out[:, here] = jnp.where(down == col[t : t + 1, :], 1.0, 0.0).astype(BF16)
+
+
+def last_step_kernel(
+    payload_ref, gain_ref, slots_ref, precond_ref, pick_ref, resid_ref, update_ref,
+    potential_ref, to_row_ref, to_col_ref, scale_ref,
+    potential_out, own_out, across_out, far_out, partner_out, next_out,
+    coupled_ref, work_ref, resid_out, update_out, row_ref,
+):
+    heart_step(
+        2, payload_ref, gain_ref, slots_ref, precond_ref, resid_ref, update_ref,
+        potential_ref, coupled_ref, work_ref, pick_ref, resid_out, update_out, potential_out,
+    )
+    scaled_rows(potential_out[...] * scale_ref[...], to_row_ref, 256, row_ref)
+    both = products(row_ref, to_col_ref, 256)
 
     def deposited(k):
         return both[(k % 4) * TORSO : (k % 4 + 1) * TORSO, (k // 4) * LANES : (k // 4 + 1) * LANES]
@@ -273,7 +290,7 @@
     source_out, block_out,
 ):
     source = own_ref[...] + across_ref[...] + far_ref[...] + partner_ref[0:TORSO]
-    source = source + next_ref[0:TORSO] + handed_ref[...]
+    source = source + next_ref[TORSO:] + handed_ref[...]
     source_out[...] = source
     share = jnp.sum(jnp.sum(source * weight_ref[...], axis=0, keepdims=True), axis=1, keepdims=True)
     block_out[:, 0:LANES] = jnp.broadcast_to(share, (block_out.shape[0], LANES))
@@ -336,10 +353,12 @@
     return c[:3] + [1 - c[3]]
 
 
-def shifted(axis, by):
+def swapped(axis, pairing):
+    partner = ((1, 0, 3, 2), (3, 2, 1, 0), (2, 3, 0, 1))[pairing]
+
     def move(c):
         c = list(c)
-        c[axis] = (c[axis] + by) % 4
+        c[axis] = partner[c[axis]]
         return c
 
     return move
@@ -349,20 +368,19 @@
     total = parts[0]
     for part in parts[1:]:
         total = total + part
-    if rows == SLOT_ROWS:
+    if rows == total.shape[0]:
         return total
     least = parts[0]
     for part in parts[1:]:
         least = jnp.minimum(least, part)
     line = lax.broadcasted_iota(jnp.int32, total.shape, 0)
-    return jnp.where(line < SLOT_ROWS, total, least)
+    return jnp.where(line < rows, total, least)
 
 
 def over_all(x):
-    rows = x.shape[0]
-    x = combined([x, permuted(x, other_core)], rows)
+    x = combined([x, permuted(x, other_core)], SLOT_ROWS)
     for axis in range(3):
-        x = combined([x] + [permuted(x, shifted(axis, k)) for k in (2, 1, 3)], rows)
+        x = combined([x] + [permuted(x, swapped(axis, k)) for k in (0, 1, 2)], SLOT_ROWS)
     return x
 
 
@@ -387,13 +405,15 @@
     rowspace = pltpu.VMEM((256, 4096), BF16)
     colspace = pltpu.VMEM((128, 4096), BF16)
     nodespace = pltpu.VMEM(node, F32)
-    pickspace = pltpu.VMEM((256, 4096), BF16)
     tablespace = pltpu.VMEM((3, 18), F32)
     indexspace = pltpu.VMEM(node, jnp.int32)
 
-    new_states, resid, update, payload, slots, gain, preconditioner = call(
+    pick = jax.ShapeDtypeStruct((128, 4096), BF16)
+    target = jax.ShapeDtypeStruct((256, 4096), BF16)
+    new_states, resid, update, payload, slots, gain, preconditioner, picks, top, bottom = call(
         ionic_kernel,
-        [states.shape, node, node, (PAYLOAD, LANES), jax.ShapeDtypeStruct(node, jnp.int32), grid, preconditioner.shape],
+        [states.shape, node, node, (PAYLOAD, LANES), jax.ShapeDtypeStruct(node, jnp.int32), grid,
+         preconditioner.shape, pick, (8, LANES), (8, LANES)],
         [pltpu.VMEM(states.shape, F32), indexspace] + [tablespace] * 5
         + [pltpu.VMEM(tile, F32), pltpu.VMEM((128, 128), F32), nodespace, rowspace,
            colspace, pltpu.SemaphoreType.DMA((11,))],
@@ -402,42 +422,44 @@
          gain, preconditioner),
         pltpu.HBM,
     )
-    above = from_behind(torso_conduct[TORSO - 8 :], 1, devices)
-    below = from_behind(torso_conduct[:8], -1, devices)
+    above = from_behind(bottom, 1, devices)
+    below = from_behind(top, -1, devices)
     conduct = jnp.concatenate([above, torso_conduct, below], axis=0)
     payload = over_all(payload)
     resid, update, potential, payload, weight, smallest = call(
         first_step_kernel,
         [node, node, node, grid, tile, (8, LANES)],
-        [nodespace, nodespace, pickspace, rowspace, colspace],
+        [nodespace, nodespace, rowspace, colspace],
         1, 40000000,
-        (whom, payload, gain, slots, preconditioner, resid, update, conduct),
+        (whom, payload, gain, slots, preconditioner, picks, resid, update, conduct),
+    )
+    to_row, to_col = call(
+        target_kernel, [target, target], [], 1, 10000000, (whom, smallest, owner, cell)
     )
     payload = over_all(payload)
     resid, update, potential, payload = call(
         second_step_kernel,
         [node, node, node, grid],
-        [nodespace, nodespace, pickspace, rowspace, colspace],
+        [nodespace, nodespace, rowspace, colspace],
         0, 40000000,
-        (payload, gain, slots, preconditioner, resid, update, potential),
+        (payload, gain, slots, preconditioner, picks, resid, update, potential),
     )
     payload = over_all(payload)
     potential, own, across, far, partner, nearby = call(
         last_step_kernel,
         [node, tile, tile, tile, (3 * TORSO, LANES), (2 * TORSO, LANES)],
-        [nodespace, nodespace, pickspace, nodespace, nodespace,
-         pltpu.VMEM((512, 4096), BF16), pltpu.VMEM((256, 4096), BF16)],
-        1, 40000000,
-        (whom, payload, gain, slots, preconditioner, resid, update, potential,
-         owner, cell, source_gain),
-    )
-    partner = permuted(partner, other_core)
+        [nodespace, nodespace, nodespace, nodespace, pltpu.VMEM((512, 4096), BF16)],
+        0, 40000000,
+        (payload, gain, slots, preconditioner, picks, resid, update, potential,
+         to_row, to_col, source_gain),
+    )
     far = lax.ppermute(far, AXES, [(i, (i + 3 if i % 2 else i - 3) % devices) for i in range(devices)])
     across = from_behind(across, devices // 2, devices)
+    partner = permuted(partner, other_core)
     nearby = lax.ppermute(
-        nearby + partner[TORSO:], AXES, [(i, (i + 2 if i % 2 else i - 2) % devices) for i in range(devices)]
-    )
-    handed = permuted(nearby[TORSO:], other_core)
+        nearby + partner[TORSO:], AXES, [(i, (i + 1 if i % 2 else i - 1) % devices) for i in range(devices)]
+    )
+    handed = permuted(nearby[:TORSO], other_core)
     source, blocks = call(
         source_kernel,
         [tile, (devices, 3 * LANES)],

time: 146 us -> 124 us (0.85)
  waiting for transfers between devices: 48 us -> 33.6 us
  starting transfers between devices: 58.7 us -> 55.7 us
  blocking collectives: 19.7 us -> 17.3 us
    ppermute x32, waiting for transfers between devices: 42.4 us -> 33.5 us  [permuted(): lax.ppermute(x, AXES, [(i, index(move(place(i)))) for i in range(128)])]
    ppermute x1, waiting for transfers between devices: 5.66 us -> 0.01 us  [body(): lax.ppermute(nearby + partner[TORSO:], AXES, [(i, (i + 1 if i % 2 else i...]
    ppermute x32, starting transfers between devices: 52.9 us -> 49.1 us  [permuted(): lax.ppermute(x, AXES, [(i, index(move(place(i)))) for i in range(128)])]
    all_to_all x1, blocking collectives: 19.7 us -> 17.3 us  [body(): blocks = lax.all_to_all(blocks, AXES, 0, 0, tiled=True)]
    pallas_call x6 -> x7, Pallas kernels: 17 us -> 15.8 us  [call(): pl.pallas_call(kernel, out_shape=[s if isinstance(s, jax.ShapeDtypeStruct...]
  transfers between devices with their start and end apart: 37 -> 37, of which waited for: 26 -> 24; matrix products, arithmetic and copies ran while one was open for 0% -> 0% of each run, Pallas kernels for 3% -> 2%
where the time goes in v3:
time: 124 us
  starting transfers between devices  55.7 us (45%)
  waiting for transfers between devices  33.6 us (27%)
  blocking collectives  17.3 us (14%)
  Pallas kernels  15.8 us (13%)
    ppermute x32, starting transfers between devices, permuted(): lax.ppermute(x, AXES, [(i, index(move(place(i)))) for i in range(128)])  49.1 us
    ppermute x32, waiting for transfers between devices, permuted(): lax.ppermute(x, AXES, [(i, index(move(place(i)))) for i in range(128)])  33.5 us
    all_to_all x1, blocking collectives, body(): blocks = lax.all_to_all(blocks, AXES, 0, 0, tiled=True)  17.3 us
    pallas_call x7, Pallas kernels, call(): pl.pallas_call(kernel, out_shape=[s if isinstance(s, jax.ShapeDtypeStruct...  15.8 us
    ppermute x3, starting transfers between devices, from_behind(): return lax.ppermute(x, AXES, [(i, (i + by) % count) for i in range(count)])  3.67 us
  transfers between devices with their start and end apart: 37, of which 24 were waited for; matrix products, arithmetic and copies ran while one was open for 0% of the time, Pallas kernels for 2%

profile of v3, /device:TPU:1, one launch (start us, length us, event | category | flops | bytes accessed | tf_op | source)
XLA Modules:
  0.0 124.0 jit_solution(1673042127173452217)
XLA Ops:
  0.6 4.0 %shard_map.157 = (f32[19,4096]{1,0:T(8,128)}, f32[32,128]{1,0:T(8,128)S(1)}, f32[32,128]{1,0:T(8,128)S(1)}, f32[136,128]{1,0:T(8,128)S(1)}, s32[32,128]{1,0:T(8,...) custom-call(f32[19,4096]{1,0:T(8,128)} %states_hbm.1, ...), custom_call_target="tpu_custom_call" | custom-call | flops 40000000 | bytes 1048576 | tf_op jit(solution)/shard_map/pallas_call | solution.py:329
  4.6 2.7 %collective-permute-start.10 = (f32[8,128]{1,0:T(8,128)S(1)}, f32[8,128]{1,0:T(8,128)S(1)}, u32[]{:S(2)}, u32[]{:S(2)}) collective-permute-start(f32[8,128]{1,0:T(8,128)S(1)} %get-tuple-element.41), channel_id=1, source_target_pairs={{0,1},{1,2},{2,3},{3,4},{4,5},{5,6},{6,7},{7,8},{8,9},{9,10},{10,1... | collective-permute-start | bytes 12296 | tf_op jit(solution)/shard_map/ppermute | solution.py:388
  7.4 7.0 %collective-permute-start = (f32[136,128]{1,0:T(8,128)S(1)}, f32[136,128]{1,0:T(8,128)S(1)}, u32[]{:S(2)}, u32[]{:S(2)}) collective-permute-start(f32[136,128]{1,0:T(8,128)S(1)} %get-tuple-element.34), channel_id=1, source_target_pairs={{0,1},{1,0},{2,3},{3,2},{4,5},{5,4},{6,7},{7,6},{8,9},{9,8},{10,11... | collective-permute-start | bytes 208904 | tf_op jit(solution)/shard_map/ppermute | solution.py:349
  14.5 0.8 collective-permute-done
  15.4 0.6 collective-permute-start.3
  16.0 0.9 collective-permute-start.2
  16.9 1.3 %collective-permute-start.1 = (f32[136,128]{1,0:T(8,128)S(1)}, f32[136,128]{1,0:T(8,128)S(1)}, u32[]{:S(2)}, u32[]{:S(2)}) collective-permute-start(f32[136,128]{1,0:T(8,128)S(1)} %minimum_select_fusion.3), channel_id=1, source_target_pairs={{0,32},{1,33},{2,34},{3,35},{4,36},{5,37},{6,38},{7,39},{8,40},{9,... | collective-permute-start | bytes 208904 | tf_op jit(solution)/shard_map/ppermute | solution.py:349
  18.1 2.1 %collective-permute-done.3 = f32[136,128]{1,0:T(8,128)S(1)} collective-permute-done((f32[136,128]{1,0:T(8,128)S(1)}, f32[136,128]{1,0:T(8,128)S(1)}, u32[]{:S(2)}, u32[]{:S(2)}) %collective-permute-start.3) | collective-permute-done | bytes 69664 | tf_op jit(solution)/shard_map/ppermute | solution.py:349
  20.2 2.4 %collective-permute-done.2 = f32[136,128]{1,0:T(8,128)S(1)} collective-permute-done((f32[136,128]{1,0:T(8,128)S(1)}, f32[136,128]{1,0:T(8,128)S(1)}, u32[]{:S(2)}, u32[]{:S(2)}) %collective-permute-start.2) | collective-permute-done | bytes 69664 | tf_op jit(solution)/shard_map/ppermute | solution.py:349
  22.6 0.1 minimum_select_fusion.2
  22.9 2.5 %collective-permute-start.4 = (f32[136,128]{1,0:T(8,128)S(1)}, f32[136,128]{1,0:T(8,128)S(1)}, u32[]{:S(2)}, u32[]{:S(2)}) collective-permute-start(f32[136,128]{1,0:T(8,128)S(1)} %minimum_select_fusion.2), channel_id=1, source_target_pairs={{0,8},{1,9},{2,10},{3,11},{4,12},{5,13},{6,14},{7,15},{8,0},{9,1},... | collective-permute-start | bytes 208904 | tf_op jit(solution)/shard_map/ppermute | solution.py:349
  25.4 2.1 %collective-permute-done.6 = f32[136,128]{1,0:T(8,128)S(1)} collective-permute-done((f32[136,128]{1,0:T(8,128)S(1)}, f32[136,128]{1,0:T(8,128)S(1)}, u32[]{:S(2)}, u32[]{:S(2)}) %collective-permute-start.6) | collective-permute-done | bytes 69664 | tf_op jit(solution)/shard_map/ppermute | solution.py:349
  27.5 1.3 %collective-permute-done.5 = f32[136,128]{1,0:T(8,128)S(1)} collective-permute-done((f32[136,128]{1,0:T(8,128)S(1)}, f32[136,128]{1,0:T(8,128)S(1)}, u32[]{:S(2)}, u32[]{:S(2)}) %collective-permute-start.5) | collective-permute-done | bytes 69664 | tf_op jit(solution)/shard_map/ppermute | solution.py:349
  28.8 0.1 minimum_select_fusion.1
  29.1 2.5 %collective-permute-start.7 = (f32[136,128]{1,0:T(8,128)S(1)}, f32[136,128]{1,0:T(8,128)S(1)}, u32[]{:S(2)}, u32[]{:S(2)}) collective-permute-start(f32[136,128]{1,0:T(8,128)S(1)} %minimum_select_fusion.1), channel_id=1, source_target_pairs={{0,2},{1,3},{2,0},{3,1},{4,6},{5,7},{6,4},{7,5},{8,10},{9,11},{10,... | collective-permute-start | bytes 208904 | tf_op jit(solution)/shard_map/ppermute | solution.py:349
  31.6 2.1 %collective-permute-done.9 = f32[136,128]{1,0:T(8,128)S(1)} collective-permute-done((f32[136,128]{1,0:T(8,128)S(1)}, f32[136,128]{1,0:T(8,128)S(1)}, u32[]{:S(2)}, u32[]{:S(2)}) %collective-permute-start.9) | collective-permute-done | bytes 69664 | tf_op jit(solution)/shard_map/ppermute | solution.py:349
  33.7 0.4 collective-permute-done.8
  34.2 0.1 minimum_select_fusion.payload_ref
  34.3 2.6 %shard_map.158 = (f32[32,128]{1,0:T(8,128)S(1)}, f32[32,128]{1,0:T(8,128)S(1)}, f32[32,128]{1,0:T(8,128)S(1)}, f32[128,128]{1,0:T(8,128)S(1)}, f32[64,128]{1,0:T(8,128)S(1)}, /*index=5*/f32[8,128]{1,0:T(8,128)S(1)}) custom-call(s32[2]{0:T(128)S(1)} %pad_add_fusion.here_ref, f32[136,128]{1,0:T(8,128)S(1)} %minimum_select_fusion.payload_ref, ...), custom_call_target="tpu_custom_call" | custom-call | flops 40000000 | bytes 1048576 | tf_op jit(solution)/shard_map/pallas_call | solution.py:329
  36.8 2.8 %collective-permute-start.12 = (f32[128,128]{1,0:T(8,128)S(1)}, f32[128,128]{1,0:T(8,128)S(1)}, u32[]{:S(2)}, u32[]{:S(2)}) collective-permute-start(f32[128,128]{1,0:T(8,128)S(1)} %get-tuple-element.43), channel_id=1, source_target_pairs={{0,1},{1,0},{2,3},{3,2},{4,5},{5,4},{6,7},{7,6},{8,9},{9,8},{10,11... | collective-permute-start | bytes 196616 | tf_op jit(solution)/shard_map/ppermute | solution.py:349
  39.6 0.9 collective-permute-done.12
  40.5 0.9 collective-permute-start.15
  41.4 1.6 %collective-permute-start.14 = (f32[128,128]{1,0:T(8,128)S(1)}, f32[128,128]{1,0:T(8,128)S(1)}, u32[]{:S(2)}, u32[]{:S(2)}) collective-permute-start(f32[128,128]{1,0:T(8,128)S(1)} %add.115), channel_id=1, source_target_pairs={{0,96},{1,97},{2,98},{3,99},{4,100},{5,101},{6,102},{7,103},{8,104... | collective-permute-start | bytes 196616 | tf_op jit(solution)/shard_map/ppermute | solution.py:349
  43.0 0.2 collective-permute-start.13
  43.3 2.0 %collective-permute-done.15 = f32[128,128]{1,0:T(8,128)S(1)} collective-permute-done((f32[128,128]{1,0:T(8,128)S(1)}, f32[128,128]{1,0:T(8,128)S(1)}, u32[]{:S(2)}, u32[]{:S(2)}) %collective-permute-start.15) | collective-permute-done | bytes 65568 | tf_op jit(solution)/shard_map/ppermute | solution.py:349
  45.3 2.2 %collective-permute-done.14 = f32[128,128]{1,0:T(8,128)S(1)} collective-permute-done((f32[128,128]{1,0:T(8,128)S(1)}, f32[128,128]{1,0:T(8,128)S(1)}, u32[]{:S(2)}, u32[]{:S(2)}) %collective-permute-start.14) | collective-permute-done | bytes 65568 | tf_op jit(solution)/shard_map/ppermute | solution.py:349
  47.5 1.2 collective-permute-start.18
  48.7 1.7 %collective-permute-start.17 = (f32[128,128]{1,0:T(8,128)S(1)}, f32[128,128]{1,0:T(8,128)S(1)}, u32[]{:S(2)}, u32[]{:S(2)}) collective-permute-start(f32[128,128]{1,0:T(8,128)S(1)} %add_add_fusion.5), channel_id=1, source_target_pairs={{0,24},{1,25},{2,26},{3,27},{4,28},{5,29},{6,30},{7,31},{8,16},{9,... | collective-permute-start | bytes 196616 | tf_op jit(solution)/shard_map/ppermute | solution.py:349
  50.5 1.8 %collective-permute-done.18 = f32[128,128]{1,0:T(8,128)S(1)} collective-permute-done((f32[128,128]{1,0:T(8,128)S(1)}, f32[128,128]{1,0:T(8,128)S(1)}, u32[]{:S(2)}, u32[]{:S(2)}) %collective-permute-start.18) | collective-permute-done | bytes 65568 | tf_op jit(solution)/shard_map/ppermute | solution.py:349
  52.2 1.5 %collective-permute-done.17 = f32[128,128]{1,0:T(8,128)S(1)} collective-permute-done((f32[128,128]{1,0:T(8,128)S(1)}, f32[128,128]{1,0:T(8,128)S(1)}, u32[]{:S(2)}, u32[]{:S(2)}) %collective-permute-start.17) | collective-permute-done | bytes 65568 | tf_op jit(solution)/shard_map/ppermute | solution.py:349
  53.8 1.1 collective-permute-start.21
  54.9 2.6 %collective-permute-start.20 = (f32[128,128]{1,0:T(8,128)S(1)}, f32[128,128]{1,0:T(8,128)S(1)}, u32[]{:S(2)}, u32[]{:S(2)}) collective-permute-start(f32[128,128]{1,0:T(8,128)S(1)} %add_add_fusion.4), channel_id=1, source_target_pairs={{0,6},{1,7},{2,4},{3,5},{4,2},{5,3},{6,0},{7,1},{8,14},{9,15},{10,... | collective-permute-start | bytes 196616 | tf_op jit(solution)/shard_map/ppermute | solution.py:349
  57.5 0.9 collective-permute-done.21
  58.5 0.7 collective-permute-done.20
  59.2 1.8 %collective-permute-done.19 = f32[128,128]{1,0:T(8,128)S(1)} collective-permute-done((f32[128,128]{1,0:T(8,128)S(1)}, f32[128,128]{1,0:T(8,128)S(1)}, u32[]{:S(2)}, u32[]{:S(2)}) %collective-permute-start.19) | collective-permute-done | bytes 65568 | tf_op jit(solution)/shard_map/ppermute | solution.py:349
  61.1 2.0 %shard_map.159 = (f32[32,128]{1,0:T(8,128)S(1)}, f32[32,128]{1,0:T(8,128)S(1)}, f32[32,128]{1,0:T(8,128)S(1)}, f32[128,128]{1,0:T(8,128)S(1)}) custom-call(f32[128,128]{1,0:T(8,128)S(1)} %add_add_fusion.3.payload_ref, f32[128,128]{1,0:T(8,128)S(1)} %get-tuple-element.35.gain_ref, s32[32,128]{1,0:T(8,128)S(1)} %get-tuple-element.36.slots_ref, ...), custom_call_target="tpu_custom_call" | custom-call | flops 40000000 | bytes 1048576 | tf_op jit(solution)/shard_map/pallas_call | solution.py:329
  63.0 3.9 %collective-permute-start.22 = (f32[128,128]{1,0:T(8,128)S(1)}, f32[128,128]{1,0:T(8,128)S(1)}, u32[]{:S(2)}, u32[]{:S(2)}) collective-permute-start(f32[128,128]{1,0:T(8,128)S(1)} %get-tuple-element.47), channel_id=1, source_target_pairs={{0,1},{1,0},{2,3},{3,2},{4,5},{5,4},{6,7},{7,6},{8,9},{9,8},{10,11... | collective-permute-start | bytes 196616 | tf_op jit(solution)/shard_map/ppermute | solution.py:349
  67.0 0.9 collective-permute-done.22
  67.9 0.6 collective-permute-start.25
  68.5 1.8 %collective-permute-start.24 = (f32[128,128]{1,0:T(8,128)S(1)}, f32[128,128]{1,0:T(8,128)S(1)}, u32[]{:S(2)}, u32[]{:S(2)}) collective-permute-start(f32[128,128]{1,0:T(8,128)S(1)} %add.125), channel_id=1, source_target_pairs={{0,96},{1,97},{2,98},{3,99},{4,100},{5,101},{6,102},{7,103},{8,104... | collective-permute-start | bytes 196616 | tf_op jit(solution)/shard_map/ppermute | solution.py:349
  70.4 0.3 collective-permute-start.23
  70.6 2.0 %collective-permute-done.25 = f32[128,128]{1,0:T(8,128)S(1)} collective-permute-done((f32[128,128]{1,0:T(8,128)S(1)}, f32[128,128]{1,0:T(8,128)S(1)}, u32[]{:S(2)}, u32[]{:S(2)}) %collective-permute-start.25) | collective-permute-done | bytes 65568 | tf_op jit(solution)/shard_map/ppermute | solution.py:349
  72.7 2.2 %collective-permute-done.24 = f32[128,128]{1,0:T(8,128)S(1)} collective-permute-done((f32[128,128]{1,0:T(8,128)S(1)}, f32[128,128]{1,0:T(8,128)S(1)}, u32[]{:S(2)}, u32[]{:S(2)}) %collective-permute-start.24) | collective-permute-done | bytes 65568 | tf_op jit(solution)/shard_map/ppermute | solution.py:349
  75.0 2.0 %collective-permute-start.27 = (f32[128,128]{1,0:T(8,128)S(1)}, f32[128,128]{1,0:T(8,128)S(1)}, u32[]{:S(2)}, u32[]{:S(2)}) collective-permute-start(f32[128,128]{1,0:T(8,128)S(1)} %add_add_fusion.2), channel_id=1, source_target_pairs={{0,24},{1,25},{2,26},{3,27},{4,28},{5,29},{6,30},{7,31},{8,16},{9,... | collective-permute-start | bytes 196616 | tf_op jit(solution)/shard_map/ppermute | solution.py:349
  77.0 0.6 collective-permute-start.26
  77.6 2.1 %collective-permute-done.28 = f32[128,128]{1,0:T(8,128)S(1)} collective-permute-done((f32[128,128]{1,0:T(8,128)S(1)}, f32[128,128]{1,0:T(8,128)S(1)}, u32[]{:S(2)}, u32[]{:S(2)}) %collective-permute-start.28) | collective-permute-done | bytes 65568 | tf_op jit(solution)/shard_map/ppermute | solution.py:349
  79.7 0.8 collective-permute-done.27
  80.6 2.1 %collective-permute-start.30 = (f32[128,128]{1,0:T(8,128)S(1)}, f32[128,128]{1,0:T(8,128)S(1)}, u32[]{:S(2)}, u32[]{:S(2)}) collective-permute-start(f32[128,128]{1,0:T(8,128)S(1)} %add_add_fusion.1), channel_id=1, source_target_pairs={{0,6},{1,7},{2,4},{3,5},{4,2},{5,3},{6,0},{7,1},{8,14},{9,15},{10,... | collective-permute-start | bytes 196616 | tf_op jit(solution)/shard_map/ppermute | solution.py:349
  82.7 0.5 collective-permute-start.29
  83.3 2.2 %shard_map.160 = (bf16[256,4096]{1,0:T(8,128)(2,1)S(1)}, bf16[256,4096]{1,0:T(8,128)(2,1)S(1)}) custom-call(s32[2]{0:T(128)S(1)} %pad_add_fusion.here_ref, f32[8,128]{1,0:T(8,128)S(1)} %get-tuple-element.51.after_ref.smallest_ref, s32[32,128]{1,0:T(8,128)S(1)} %bitcast.15, s32[32,128]{1,0:T(8,128)S(1)} %bitcast.16), custom_call_target="tpu_custom_call" | custom-call | flops 10000000 | bytes 1048576 | tf_op jit(solution)/shard_map/pallas_call | solution.py:329
  85.5 0.3 collective-permute-done.30
  85.7 0.4 collective-permute-done.29
  86.1 3.1 %shard_map.161 = (f32[32,128]{1,0:T(8,128)}, f32[64,128]{1,0:T(8,128)S(1)}, f32[64,128]{1,0:T(8,128)S(1)}, f32[64,128]{1,0:T(8,128)S(1)}, f32[192,128]{1,0:T(8,128)S(1)}, /*index=5*/f32[128,128]{1,0:T(8,128)S(1)}) custom-call(f32[128,128]{1,0:T(8,128)S(1)} %add_add_fusion.payload_ref, f32[128,128]{1,0:T(8,128)S(1)} %get-tuple-element.35.gain_ref, ...), custom_call_target="tpu_custom_call" | custom-call | flops 40000000 | bytes 1048576 | tf_op jit(solution)/shard_map/pallas_call | solution.py:329
  89.2 3.5 %collective-permute-start.34 = (f32[192,128]{1,0:T(8,128)S(1)}, f32[192,128]{1,0:T(8,128)S(1)}, u32[]{:S(2)}, u32[]{:S(2)}) collective-permute-start(f32[192,128]{1,0:T(8,128)S(1)} %get-tuple-element.59), channel_id=1, source_target_pairs={{0,1},{1,0},{2,3},{3,2},{4,5},{5,4},{6,7},{7,6},{8,9},{9,8},{10,11... | collective-permute-start | bytes 294920 | tf_op jit(solution)/shard_map/ppermute | solution.py:349
  92.7 0.9 collective-permute-done.34.partner_ref
  93.7 0.9 collective-permute-start.35
  94.5 0.9 collective-permute-start.32
  95.5 2.1 %collective-permute-start.33 = (f32[64,128]{1,0:T(8,128)S(1)}, f32[64,128]{1,0:T(8,128)S(1)}, u32[]{:S(2)}, u32[]{:S(2)}) collective-permute-start(f32[64,128]{1,0:T(8,128)S(1)} %get-tuple-element.58), channel_id=1, source_target_pairs={{0,125},{1,4},{2,127},{3,6},{4,1},{5,8},{6,3},{7,10},{8,5},{9,12},... | collective-permute-start | bytes 98312 | tf_op jit(solution)/shard_map/ppermute | solution.py:456
  97.6 6.0 %collective-permute-start.36 = (f32[64,128]{1,0:T(8,128)S(1)}, f32[64,128]{1,0:T(8,128)S(1)}, u32[]{:S(2)}, u32[]{:S(2)}) collective-permute-start(f32[64,128]{1,0:T(8,128)S(1)} %slice.9), channel_id=1, source_target_pairs={{0,1},{1,0},{2,3},{3,2},{4,5},{5,4},{6,7},{7,6},{8,9},{9,8},{10,11... | collective-permute-start | bytes 98312 | tf_op jit(solution)/shard_map/ppermute | solution.py:349
  103.6 0.9 collective-permute-done.36.handed_ref
  104.5 0.6 shard_map.162
  105.1 0.2 copy.17
  105.3 17.3 %all_to_all.11 = f32[128,1,384]{2,1,0:T(1,128)S(1)} all-to-all(f32[128,1,384]{2,1,0:T(1,128)S(1)} %copy.17), channel_id=1, replica_groups=mesh['a'=4,'b'=4,'c'=4,'d'=2] {'a','b','c','d'}, dimensions={0} | all-to-all | bytes 393216 | tf_op jit(solution)/shard_map/all_to_all | solution.py:469
  122.6 1.4 %shard_map.163 = f32[64,128]{1,0:T(8,128)} custom-call(s32[2]{0:T(128)S(1)} %pad_add_fusion.here_ref, f32[128,384]{1,0:T(8,128)S(1)} %bitcast.12, f32[64,128]{1,0:T(8,128)S(1)} %get-tuple-element.62.source_ref, f32[80,128]{1,0:T(8,128)S(1)} %constant_dynamic-update-slice_fusion.conduct_ref, f32[8,128]{1,0:T(8,128)S(1)} %get-tuple-element.51.after_ref.smallest_ref), custom_call_target="tpu_custom_call" | custom-call | flops 4000000 | bytes 1048576 | tf_op jit(solution)/shard_map/pallas_call | solution.py:329
  (47 shorter events, 0.9 us)
Async XLA Ops:
  0.6 24.8 %copy-start.3 = (f32[64,128]{1,0:T(8,128)S(1)}, f32[64,128]{1,0:T(8,128)}, u32[]{:S(2)}) copy-start(f32[64,128]{1,0:T(8,128)} %conduct_hbm.1) | copy-start | bytes 98308
  4.6 13.5 %collective-permute-start.10 = (f32[8,128]{1,0:T(8,128)S(1)}, f32[8,128]{1,0:T(8,128)S(1)}, u32[]{:S(2)}, u32[]{:S(2)}) collective-permute-start(f32[8,128]{1,0:T(8,128)S(1)} %get-tuple-element.41), channel_id=1, source_target_pairs={{0,1},{1,2},{2,3},{3,4},{4,5},{5,6},{6,7},{7,8},{8,9},{9,10},{10,1... | collective-permute-start | bytes 12296 | tf_op jit(solution)/shard_map/ppermute | solution.py:388
  7.4 24.2 %collective-permute-start.11 = (f32[8,128]{1,0:T(8,128)S(1)}, f32[8,128]{1,0:T(8,128)S(1)}, u32[]{:S(2)}, u32[]{:S(2)}) collective-permute-start(f32[8,128]{1,0:T(8,128)S(1)} %get-tuple-element.42), channel_id=1, source_target_pairs={{0,127},{1,0},{2,1},{3,2},{4,3},{5,4},{6,5},{7,6},{8,7},{9,8},{10,... | collective-permute-start | bytes 12296 | tf_op jit(solution)/shard_map/ppermute | solution.py:388
  7.4 7.9 %collective-permute-start = (f32[136,128]{1,0:T(8,128)S(1)}, f32[136,128]{1,0:T(8,128)S(1)}, u32[]{:S(2)}, u32[]{:S(2)}) collective-permute-start(f32[136,128]{1,0:T(8,128)S(1)} %get-tuple-element.34), channel_id=1, source_target_pairs={{0,1},{1,0},{2,3},{3,2},{4,5},{5,4},{6,7},{7,6},{8,9},{9,8},{10,11... | collective-permute-start | bytes 208904 | tf_op jit(solution)/shard_map/ppermute | solution.py:349
  15.4 4.8 %collective-permute-start.3 = (f32[136,128]{1,0:T(8,128)S(1)}, f32[136,128]{1,0:T(8,128)S(1)}, u32[]{:S(2)}, u32[]{:S(2)}) collective-permute-start(f32[136,128]{1,0:T(8,128)S(1)} %minimum_select_fusion.3), channel_id=1, source_target_pairs={{0,64},{1,65},{2,66},{3,67},{4,68},{5,69},{6,70},{7,71},{8,72},{9,... | collective-permute-start | bytes 208904 | tf_op jit(solution)/shard_map/ppermute | solution.py:349
  16.0 6.6 %collective-permute-start.2 = (f32[136,128]{1,0:T(8,128)S(1)}, f32[136,128]{1,0:T(8,128)S(1)}, u32[]{:S(2)}, u32[]{:S(2)}) collective-permute-start(f32[136,128]{1,0:T(8,128)S(1)} %minimum_select_fusion.3), channel_id=1, source_target_pairs={{0,96},{1,97},{2,98},{3,99},{4,100},{5,101},{6,102},{7,103},{8,104... | collective-permute-start | bytes 208904 | tf_op jit(solution)/shard_map/ppermute | solution.py:349
  16.9 5.7 %collective-permute-start.1 = (f32[136,128]{1,0:T(8,128)S(1)}, f32[136,128]{1,0:T(8,128)S(1)}, u32[]{:S(2)}, u32[]{:S(2)}) collective-permute-start(f32[136,128]{1,0:T(8,128)S(1)} %minimum_select_fusion.3), channel_id=1, source_target_pairs={{0,32},{1,33},{2,34},{3,35},{4,36},{5,37},{6,38},{7,39},{8,40},{9,... | collective-permute-start | bytes 208904 | tf_op jit(solution)/shard_map/ppermute | solution.py:349
  22.7 4.8 %collective-permute-start.6 = (f32[136,128]{1,0:T(8,128)S(1)}, f32[136,128]{1,0:T(8,128)S(1)}, u32[]{:S(2)}, u32[]{:S(2)}) collective-permute-start(f32[136,128]{1,0:T(8,128)S(1)} %minimum_select_fusion.2), channel_id=1, source_target_pairs={{0,16},{1,17},{2,18},{3,19},{4,20},{5,21},{6,22},{7,23},{8,24},{9,... | collective-permute-start | bytes 208904 | tf_op jit(solution)/shard_map/ppermute | solution.py:349
  22.8 6.0 %collective-permute-start.5 = (f32[136,128]{1,0:T(8,128)S(1)}, f32[136,128]{1,0:T(8,128)S(1)}, u32[]{:S(2)}, u32[]{:S(2)}) collective-permute-start(f32[136,128]{1,0:T(8,128)S(1)} %minimum_select_fusion.2), channel_id=1, source_target_pairs={{0,24},{1,25},{2,26},{3,27},{4,28},{5,29},{6,30},{7,31},{8,16},{9,... | collective-permute-start | bytes 208904 | tf_op jit(solution)/shard_map/ppermute | solution.py:349
  22.9 5.9 %collective-permute-start.4 = (f32[136,128]{1,0:T(8,128)S(1)}, f32[136,128]{1,0:T(8,128)S(1)}, u32[]{:S(2)}, u32[]{:S(2)}) collective-permute-start(f32[136,128]{1,0:T(8,128)S(1)} %minimum_select_fusion.2), channel_id=1, source_target_pairs={{0,8},{1,9},{2,10},{3,11},{4,12},{5,13},{6,14},{7,15},{8,0},{9,1},... | collective-permute-start | bytes 208904 | tf_op jit(solution)/shard_map/ppermute | solution.py:349
  28.9 4.8 %collective-permute-start.9 = (f32[136,128]{1,0:T(8,128)S(1)}, f32[136,128]{1,0:T(8,128)S(1)}, u32[]{:S(2)}, u32[]{:S(2)}) collective-permute-start(f32[136,128]{1,0:T(8,128)S(1)} %minimum_select_fusion.1), channel_id=1, source_target_pairs={{0,4},{1,5},{2,6},{3,7},{4,0},{5,1},{6,2},{7,3},{8,12},{9,13},{10,... | collective-permute-start | bytes 208904 | tf_op jit(solution)/shard_map/ppermute | solution.py:349
  29.0 5.2 %collective-permute-start.8 = (f32[136,128]{1,0:T(8,128)S(1)}, f32[136,128]{1,0:T(8,128)S(1)}, u32[]{:S(2)}, u32[]{:S(2)}) collective-permute-start(f32[136,128]{1,0:T(8,128)S(1)} %minimum_select_fusion.1), channel_id=1, source_target_pairs={{0,6},{1,7},{2,4},{3,5},{4,2},{5,3},{6,0},{7,1},{8,14},{9,15},{10,... | collective-permute-start | bytes 208904 | tf_op jit(solution)/shard_map/ppermute | solution.py:349
  29.1 5.1 %collective-permute-start.7 = (f32[136,128]{1,0:T(8,128)S(1)}, f32[136,128]{1,0:T(8,128)S(1)}, u32[]{:S(2)}, u32[]{:S(2)}) collective-permute-start(f32[136,128]{1,0:T(8,128)S(1)} %minimum_select_fusion.1), channel_id=1, source_target_pairs={{0,2},{1,3},{2,0},{3,1},{4,6},{5,7},{6,4},{7,5},{8,10},{9,11},{10,... | collective-permute-start | bytes 208904 | tf_op jit(solution)/shard_map/ppermute | solution.py:349
  36.8 3.7 %collective-permute-start.12 = (f32[128,128]{1,0:T(8,128)S(1)}, f32[128,128]{1,0:T(8,128)S(1)}, u32[]{:S(2)}, u32[]{:S(2)}) collective-permute-start(f32[128,128]{1,0:T(8,128)S(1)} %get-tuple-element.43), channel_id=1, source_target_pairs={{0,1},{1,0},{2,3},{3,2},{4,5},{5,4},{6,7},{7,6},{8,9},{9,8},{10,11... | collective-permute-start | bytes 196616 | tf_op jit(solution)/shard_map/ppermute | solution.py:349
  40.5 4.7 %collective-permute-start.15 = (f32[128,128]{1,0:T(8,128)S(1)}, f32[128,128]{1,0:T(8,128)S(1)}, u32[]{:S(2)}, u32[]{:S(2)}) collective-permute-start(f32[128,128]{1,0:T(8,128)S(1)} %add.115), channel_id=1, source_target_pairs={{0,64},{1,65},{2,66},{3,67},{4,68},{5,69},{6,70},{7,71},{8,72},{9,... | collective-permute-start | bytes 196616 | tf_op jit(solution)/shard_map/ppermute | solution.py:349
  41.4 6.1 %collective-permute-start.14 = (f32[128,128]{1,0:T(8,128)S(1)}, f32[128,128]{1,0:T(8,128)S(1)}, u32[]{:S(2)}, u32[]{:S(2)}) collective-permute-start(f32[128,128]{1,0:T(8,128)S(1)} %add.115), channel_id=1, source_target_pairs={{0,96},{1,97},{2,98},{3,99},{4,100},{5,101},{6,102},{7,103},{8,104... | collective-permute-start | bytes 196616 | tf_op jit(solution)/shard_map/ppermute | solution.py:349
  43.0 4.5 %collective-permute-start.13 = (f32[128,128]{1,0:T(8,128)S(1)}, f32[128,128]{1,0:T(8,128)S(1)}, u32[]{:S(2)}, u32[]{:S(2)}) collective-permute-start(f32[128,128]{1,0:T(8,128)S(1)} %add.115), channel_id=1, source_target_pairs={{0,32},{1,33},{2,34},{3,35},{4,36},{5,37},{6,38},{7,39},{8,40},{9,... | collective-permute-start | bytes 196616 | tf_op jit(solution)/shard_map/ppermute | solution.py:349
  47.5 4.7 %collective-permute-start.18 = (f32[128,128]{1,0:T(8,128)S(1)}, f32[128,128]{1,0:T(8,128)S(1)}, u32[]{:S(2)}, u32[]{:S(2)}) collective-permute-start(f32[128,128]{1,0:T(8,128)S(1)} %add_add_fusion.5), channel_id=1, source_target_pairs={{0,16},{1,17},{2,18},{3,19},{4,20},{5,21},{6,22},{7,23},{8,24},{9,... | collective-permute-start | bytes 196616 | tf_op jit(solution)/shard_map/ppermute | solution.py:349
  48.7 5.0 %collective-permute-start.17 = (f32[128,128]{1,0:T(8,128)S(1)}, f32[128,128]{1,0:T(8,128)S(1)}, u32[]{:S(2)}, u32[]{:S(2)}) collective-permute-start(f32[128,128]{1,0:T(8,128)S(1)} %add_add_fusion.5), channel_id=1, source_target_pairs={{0,24},{1,25},{2,26},{3,27},{4,28},{5,29},{6,30},{7,31},{8,16},{9,... | collective-permute-start | bytes 196616 | tf_op jit(solution)/shard_map/ppermute | solution.py:349
  50.5 3.3 %collective-permute-start.16 = (f32[128,128]{1,0:T(8,128)S(1)}, f32[128,128]{1,0:T(8,128)S(1)}, u32[]{:S(2)}, u32[]{:S(2)}) collective-permute-start(f32[128,128]{1,0:T(8,128)S(1)} %add_add_fusion.5), channel_id=1, source_target_pairs={{0,8},{1,9},{2,10},{3,11},{4,12},{5,13},{6,14},{7,15},{8,0},{9,1},... | collective-permute-start | bytes 196616 | tf_op jit(solution)/shard_map/ppermute | solution.py:349
  53.8 4.7 %collective-permute-start.21 = (f32[128,128]{1,0:T(8,128)S(1)}, f32[128,128]{1,0:T(8,128)S(1)}, u32[]{:S(2)}, u32[]{:S(2)}) collective-permute-start(f32[128,128]{1,0:T(8,128)S(1)} %add_add_fusion.4), channel_id=1, source_target_pairs={{0,4},{1,5},{2,6},{3,7},{4,0},{5,1},{6,2},{7,3},{8,12},{9,13},{10,... | collective-permute-start | bytes 196616 | tf_op jit(solution)/shard_map/ppermute | solution.py:349
  54.9 4.3 %collective-permute-start.20 = (f32[128,128]{1,0:T(8,128)S(1)}, f32[128,128]{1,0:T(8,128)S(1)}, u32[]{:S(2)}, u32[]{:S(2)}) collective-permute-start(f32[128,128]{1,0:T(8,128)S(1)} %add_add_fusion.4), channel_id=1, source_target_pairs={{0,6},{1,7},{2,4},{3,5},{4,2},{5,3},{6,0},{7,1},{8,14},{9,15},{10,... | collective-permute-start | bytes 196616 | tf_op jit(solution)/shard_map/ppermute | solution.py:349
  57.5 3.5 %collective-permute-start.19 = (f32[128,128]{1,0:T(8,128)S(1)}, f32[128,128]{1,0:T(8,128)S(1)}, u32[]{:S(2)}, u32[]{:S(2)}) collective-permute-start(f32[128,128]{1,0:T(8,128)S(1)} %add_add_fusion.4), channel_id=1, source_target_pairs={{0,2},{1,3},{2,0},{3,1},{4,6},{5,7},{6,4},{7,5},{8,10},{9,11},{10,... | collective-permute-start | bytes 196616 | tf_op jit(solution)/shard_map/ppermute | solution.py:349
  61.0 22.2 %copy-start.1 = (s32[4096,1]{0,1:T(1,128)S(1)}, s32[4096,1]{0,1:T(1,128)}, u32[]{:S(2)}) copy-start(s32[4096,1]{0,1:T(1,128)} %param.25) | copy-start | bytes 49156
  61.0 22.2 %copy-start.2 = (s32[4096]{0:T(1024)S(1)}, s32[4096]{0:T(1024)}, u32[]{:S(2)}) copy-start(s32[4096]{0:T(1024)} %param.26) | copy-start | bytes 49156
  61.0 25.1 %copy-start = (f32[4096]{0:T(1024)S(1)}, f32[4096]{0:T(1024)}, u32[]{:S(2)}) copy-start(f32[4096]{0:T(1024)} %param.27) | copy-start | bytes 49156
  63.0 4.8 %collective-permute-start.22 = (f32[128,128]{1,0:T(8,128)S(1)}, f32[128,128]{1,0:T(8,128)S(1)}, u32[]{:S(2)}, u32[]{:S(2)}) collective-permute-start(f32[128,128]{1,0:T(8,128)S(1)} %get-tuple-element.47), channel_id=1, source_target_pairs={{0,1},{1,0},{2,3},{3,2},{4,5},{5,4},{6,7},{7,6},{8,9},{9,8},{10,11... | collective-permute-start | bytes 196616 | tf_op jit(solution)/shard_map/ppermute | solution.py:349
  67.9 4.7 %collective-permute-start.25 = (f32[128,128]{1,0:T(8,128)S(1)}, f32[128,128]{1,0:T(8,128)S(1)}, u32[]{:S(2)}, u32[]{:S(2)}) collective-permute-start(f32[128,128]{1,0:T(8,128)S(1)} %add.125), channel_id=1, source_target_pairs={{0,64},{1,65},{2,66},{3,67},{4,68},{5,69},{6,70},{7,71},{8,72},{9,... | collective-permute-start | bytes 196616 | tf_op jit(solution)/shard_map/ppermute | solution.py:349
  68.5 6.3 %collective-permute-start.24 = (f32[128,128]{1,0:T(8,128)S(1)}, f32[128,128]{1,0:T(8,128)S(1)}, u32[]{:S(2)}, u32[]{:S(2)}) collective-permute-start(f32[128,128]{1,0:T(8,128)S(1)} %add.125), channel_id=1, source_target_pairs={{0,96},{1,97},{2,98},{3,99},{4,100},{5,101},{6,102},{7,103},{8,104... | collective-permute-start | bytes 196616 | tf_op jit(solution)/shard_map/ppermute | solution.py:349
  70.4 4.5 %collective-permute-start.23 = (f32[128,128]{1,0:T(8,128)S(1)}, f32[128,128]{1,0:T(8,128)S(1)}, u32[]{:S(2)}, u32[]{:S(2)}) collective-permute-start(f32[128,128]{1,0:T(8,128)S(1)} %add.125), channel_id=1, source_target_pairs={{0,32},{1,33},{2,34},{3,35},{4,36},{5,37},{6,38},{7,39},{8,40},{9,... | collective-permute-start | bytes 196616 | tf_op jit(solution)/shard_map/ppermute | solution.py:349
  74.9 4.8 %collective-permute-start.28 = (f32[128,128]{1,0:T(8,128)S(1)}, f32[128,128]{1,0:T(8,128)S(1)}, u32[]{:S(2)}, u32[]{:S(2)}) collective-permute-start(f32[128,128]{1,0:T(8,128)S(1)} %add_add_fusion.2), channel_id=1, source_target_pairs={{0,16},{1,17},{2,18},{3,19},{4,20},{5,21},{6,22},{7,23},{8,24},{9,... | collective-permute-start | bytes 196616 | tf_op jit(solution)/shard_map/ppermute | solution.py:349
  75.0 5.5 %collective-permute-start.27 = (f32[128,128]{1,0:T(8,128)S(1)}, f32[128,128]{1,0:T(8,128)S(1)}, u32[]{:S(2)}, u32[]{:S(2)}) collective-permute-start(f32[128,128]{1,0:T(8,128)S(1)} %add_add_fusion.2), channel_id=1, source_target_pairs={{0,24},{1,25},{2,26},{3,27},{4,28},{5,29},{6,30},{7,31},{8,16},{9,... | collective-permute-start | bytes 196616 | tf_op jit(solution)/shard_map/ppermute | solution.py:349
  77.0 3.5 %collective-permute-start.26 = (f32[128,128]{1,0:T(8,128)S(1)}, f32[128,128]{1,0:T(8,128)S(1)}, u32[]{:S(2)}, u32[]{:S(2)}) collective-permute-start(f32[128,128]{1,0:T(8,128)S(1)} %add_add_fusion.2), channel_id=1, source_target_pairs={{0,8},{1,9},{2,10},{3,11},{4,12},{5,13},{6,14},{7,15},{8,0},{9,1},... | collective-permute-start | bytes 196616 | tf_op jit(solution)/shard_map/ppermute | solution.py:349
  80.5 4.9 %collective-permute-start.31 = (f32[128,128]{1,0:T(8,128)S(1)}, f32[128,128]{1,0:T(8,128)S(1)}, u32[]{:S(2)}, u32[]{:S(2)}) collective-permute-start(f32[128,128]{1,0:T(8,128)S(1)} %add_add_fusion.1), channel_id=1, source_target_pairs={{0,4},{1,5},{2,6},{3,7},{4,0},{5,1},{6,2},{7,3},{8,12},{9,13},{10,... | collective-permute-start | bytes 196616 | tf_op jit(solution)/shard_map/ppermute | solution.py:349
  80.6 5.1 %collective-permute-start.30 = (f32[128,128]{1,0:T(8,128)S(1)}, f32[128,128]{1,0:T(8,128)S(1)}, u32[]{:S(2)}, u32[]{:S(2)}) collective-permute-start(f32[128,128]{1,0:T(8,128)S(1)} %add_add_fusion.1), channel_id=1, source_target_pairs={{0,6},{1,7},{2,4},{3,5},{4,2},{5,3},{6,0},{7,1},{8,14},{9,15},{10,... | collective-permute-start | bytes 196616 | tf_op jit(solution)/shard_map/ppermute | solution.py:349
  82.7 3.4 %collective-permute-start.29 = (f32[128,128]{1,0:T(8,128)S(1)}, f32[128,128]{1,0:T(8,128)S(1)}, u32[]{:S(2)}, u32[]{:S(2)}) collective-permute-start(f32[128,128]{1,0:T(8,128)S(1)} %add_add_fusion.1), channel_id=1, source_target_pairs={{0,2},{1,3},{2,0},{3,1},{4,6},{5,7},{6,4},{7,5},{8,10},{9,11},{10,... | collective-permute-start | bytes 196616 | tf_op jit(solution)/shard_map/ppermute | solution.py:349
  89.2 4.5 %collective-permute-start.34 = (f32[192,128]{1,0:T(8,128)S(1)}, f32[192,128]{1,0:T(8,128)S(1)}, u32[]{:S(2)}, u32[]{:S(2)}) collective-permute-start(f32[192,128]{1,0:T(8,128)S(1)} %get-tuple-element.59), channel_id=1, source_target_pairs={{0,1},{1,0},{2,3},{3,2},{4,5},{5,4},{6,7},{7,6},{8,9},{9,8},{10,11... | collective-permute-start | bytes 294920 | tf_op jit(solution)/shard_map/ppermute | solution.py:349
  93.7 3.9 %collective-permute-start.35 = (f32[128,128]{1,0:T(8,128)S(1)}, f32[128,128]{1,0:T(8,128)S(1)}, u32[]{:S(2)}, u32[]{:S(2)}) collective-permute-start(f32[128,128]{1,0:T(8,128)S(1)} %slice_add_fusion), channel_id=1, source_target_pairs={{0,127},{1,2},{2,1},{3,4},{4,3},{5,6},{6,5},{7,8},{8,7},{9,10},{10... | collective-permute-start | bytes 196616 | tf_op jit(solution)/shard_map/ppermute | solution.py:459
  94.5 9.1 %collective-permute-start.32 = (f32[64,128]{1,0:T(8,128)S(1)}, f32[64,128]{1,0:T(8,128)S(1)}, u32[]{:S(2)}, u32[]{:S(2)}) collective-permute-start(f32[64,128]{1,0:T(8,128)S(1)} %get-tuple-element.57), channel_id=1, source_target_pairs={{0,64},{1,65},{2,66},{3,67},{4,68},{5,69},{6,70},{7,71},{8,72},{9,... | collective-permute-start | bytes 98312 | tf_op jit(solution)/shard_map/ppermute | solution.py:388
  95.5 8.1 %collective-permute-start.33 = (f32[64,128]{1,0:T(8,128)S(1)}, f32[64,128]{1,0:T(8,128)S(1)}, u32[]{:S(2)}, u32[]{:S(2)}) collective-permute-start(f32[64,128]{1,0:T(8,128)S(1)} %get-tuple-element.58), channel_id=1, source_target_pairs={{0,125},{1,4},{2,127},{3,6},{4,1},{5,8},{6,3},{7,10},{8,5},{9,12},... | collective-permute-start | bytes 98312 | tf_op jit(solution)/shard_map/ppermute | solution.py:456
  97.6 6.9 %collective-permute-start.36 = (f32[64,128]{1,0:T(8,128)S(1)}, f32[64,128]{1,0:T(8,128)S(1)}, u32[]{:S(2)}, u32[]{:S(2)}) collective-permute-start(f32[64,128]{1,0:T(8,128)S(1)} %slice.9), channel_id=1, source_target_pairs={{0,1},{1,0},{2,3},{3,2},{4,5},{5,4},{6,7},{7,6},{8,9},{9,8},{10,11... | collective-permute-start | bytes 98312 | tf_op jit(solution)/shard_map/ppermute | solution.py:349

commit v4 on v3

--- a/solution.py
+++ b/solution.py
@@ -72,12 +72,15 @@
     return both[:count] + both[count:]
 
 
-def slot_sums(slots_ref, w_ref, pick_ref, col_ref, row_ref):
+def one_hot_columns(slots_ref, col_ref):
     down = lax.broadcasted_iota(jnp.int32, (LANES, LANES), 0)
     for t in range(TILES):
         here = slice(t * LANES, (t + 1) * LANES)
         match = down == (slots_ref[t : t + 1, :] & 127)
         col_ref[:, here] = jnp.where(match, 1.0, 0.0).astype(BF16)
+
+
+def slot_sums(w_ref, pick_ref, col_ref, row_ref):
     scaled_rows(w_ref[...], pick_ref, LANES, row_ref)
     return products(row_ref, col_ref, LANES)
 
@@ -103,16 +106,19 @@
     conduct_ref, table_ref, volt_ref, row_ref, col_ref, sems,
 ):
     pairs = (
-        (half_hbm, half_ref), (slope_hbm, slope_ref), (rate_hbm, rate_ref), (cond_hbm, cond_ref),
-        (rev_hbm, rev_ref), (region_hbm, region_ref), (states_hbm, states_ref),
-        (slots_hbm, slots_out), (conduct_hbm, conduct_ref),
+        (slots_hbm, slots_out), (half_hbm, half_ref), (slope_hbm, slope_ref), (rate_hbm, rate_ref),
+        (cond_hbm, cond_ref), (rev_hbm, rev_ref), (region_hbm, region_ref), (states_hbm, states_ref),
+        (conduct_hbm, conduct_ref),
         (gain_hbm, gain_out), (precond_hbm, precond_out),
     )
     copies = [pltpu.make_async_copy(x, y, sems.at[k]) for k, (x, y) in enumerate(pairs)]
     for copy in copies:
         copy.start()
     table_ref[...] = jnp.zeros_like(table_ref)
-    for copy in copies[:7]:
+    copies[0].wait()
+    one_hot_rows(slots_out, pick_out)
+    one_hot_columns(slots_out, col_ref)
+    for copy in copies[1:8]:
         copy.wait()
     for k, ref in enumerate((half_ref, slope_ref, rate_ref, cond_ref, rev_ref)):
         table_ref[8 * k : 8 * k + 3, 0:18] = ref[...]
@@ -145,18 +151,14 @@
         new_volt = volt - TIME_STEP * current
         states_out[:, here] = jnp.where(first, new_volt, gates)
         volt_ref[t : t + 1, :] = new_volt
-    for copy in copies[7:9]:
-        copy.wait()
+    copies[8].wait()
     top_out[...] = conduct_ref[0:8, :]
     bottom_out[...] = conduct_ref[TORSO - 8 :, :]
     payload_out[SLOT_ROWS:, :] = jnp.min(conduct_ref[...].reshape(8, 8, LANES), axis=0)
     volt = volt_ref[...]
     resid_out[...] = volt
     update_out[...] = volt * (1.0 / CENTER)
-    one_hot_rows(slots_out, pick_out)
-    payload_out[0:SLOT_ROWS, :] = slot_sums(
-        slots_out, update_out, pick_out, col_ref, row_ref
-    )
+    payload_out[0:SLOT_ROWS, :] = slot_sums(update_out, pick_out, col_ref, row_ref)
     for copy in copies[9:]:
         copy.wait()
 
@@ -211,20 +213,24 @@
 
 
 def first_step_kernel(
-    here_ref, payload_ref, gain_ref, slots_ref, precond_ref, pick_ref, resid_ref, update_ref, conduct_ref,
-    resid_out, update_out, potential_out, payload_out, weight_out, smallest_out,
+    payload_ref, gain_ref, slots_ref, precond_ref, pick_ref, resid_ref, update_ref,
+    resid_out, update_out, potential_out, payload_out, smallest_out,
     coupled_ref, work_ref, row_ref, col_ref,
 ):
     heart_step(
         0, payload_ref, gain_ref, slots_ref, precond_ref, resid_ref, update_ref,
         update_ref, coupled_ref, work_ref, pick_ref, resid_out, update_out, potential_out,
     )
-    payload_out[...] = slot_sums(slots_ref, update_out, pick_ref, col_ref, row_ref)
+    one_hot_columns(slots_ref, col_ref)
+    payload_out[...] = slot_sums(update_out, pick_ref, col_ref, row_ref)
     smallest = jnp.min(jnp.min(payload_ref[SLOT_ROWS:, :], axis=0, keepdims=True), axis=1, keepdims=True)
     smallest_out[...] = jnp.broadcast_to(smallest, (8, LANES))
+
+
+def weight_kernel(here_ref, smallest_ref, conduct_ref, weight_out):
     ones = jnp.ones((TORSO + 16, LANES), F32)
     field = torso_solve(
-        ones, conduct_ref[...], smallest, here_ref[0] == 0, here_ref[0] == here_ref[1] - 1
+        ones, conduct_ref[...], smallest_ref[0:1, 0:1], here_ref[0] == 0, here_ref[0] == here_ref[1] - 1
     )
     weight_out[...] = field[8 : 8 + TORSO]
 
@@ -238,7 +244,8 @@
         1, payload_ref, gain_ref, slots_ref, precond_ref, resid_ref, update_ref,
         potential_ref, coupled_ref, work_ref, pick_ref, resid_out, update_out, potential_out,
     )
-    payload_out[...] = slot_sums(slots_ref, update_out, pick_ref, col_ref, row_ref)
+    one_hot_columns(slots_ref, col_ref)
+    payload_out[...] = slot_sums(update_out, pick_ref, col_ref, row_ref)
 
 
 def target_kernel(here_ref, after_ref, owner_ref, cell_ref, row_out, col_out):
@@ -377,11 +384,22 @@
     return jnp.where(line < rows, total, least)
 
 
+RING_ORDER = (2, 1, 0)
+
+
 def over_all(x):
-    x = combined([x, permuted(x, other_core)], SLOT_ROWS)
     for axis in range(3):
-        x = combined([x] + [permuted(x, swapped(axis, k)) for k in (0, 1, 2)], SLOT_ROWS)
+        parts = [x]
+        for k in RING_ORDER:
+            parts.append(permuted(x, swapped(axis, k)))
+        x = combined(parts, SLOT_ROWS)
+        if axis == 1:
+            x = combined([x, permuted(x, other_core)], SLOT_ROWS)
     return x
+
+
+def near(i, devices):
+    return (i + 1 if i % 2 else i - 1) % devices
 
 
 def from_behind(x, by, count):
@@ -422,17 +440,25 @@
          gain, preconditioner),
         pltpu.HBM,
     )
-    above = from_behind(bottom, 1, devices)
-    below = from_behind(top, -1, devices)
-    conduct = jnp.concatenate([above, torso_conduct, below], axis=0)
+    even = here % 2 == 0
+    inner = permuted(jnp.where(even, bottom, top), other_core)
+    outer = jnp.where(even, top, bottom)
+    outer = lax.ppermute(
+        outer, AXES,
+        [(i, i if i in (0, devices - 1) else near(i, devices)) for i in range(devices)],
+    )
+    conduct = jnp.concatenate(
+        [jnp.where(even, outer, inner), torso_conduct, jnp.where(even, inner, outer)], axis=0
+    )
     payload = over_all(payload)
-    resid, update, potential, payload, weight, smallest = call(
+    resid, update, potential, payload, smallest = call(
         first_step_kernel,
-        [node, node, node, grid, tile, (8, LANES)],
+        [node, node, node, grid, (8, LANES)],
         [nodespace, nodespace, rowspace, colspace],
-        1, 40000000,
-        (whom, payload, gain, slots, preconditioner, picks, resid, update, conduct),
-    )
+        0, 40000000,
+        (payload, gain, slots, preconditioner, picks, resid, update),
+    )
+    (weight,) = call(weight_kernel, [tile], [], 1, 4000000, (whom, smallest, conduct))
     to_row, to_col = call(
         target_kernel, [target, target], [], 1, 10000000, (whom, smallest, owner, cell)
     )
@@ -457,7 +483,7 @@
     across = from_behind(across, devices // 2, devices)
     partner = permuted(partner, other_core)
     nearby = lax.ppermute(
-        nearby + partner[TORSO:], AXES, [(i, (i + 1 if i % 2 else i - 1) % devices) for i in range(devices)]
+        nearby + partner[TORSO:], AXES, [(i, near(i, devices)) for i in range(devices)]
     )
     handed = permuted(nearby[:TORSO], other_core)
     source, blocks = call(

time: 124 us -> 126 us (1.016)
  blocking collectives: 17.3 us -> 21.9 us
  starting transfers between devices: 55.7 us -> 53.3 us
    all_to_all x1, blocking collectives: 17.3 us -> 21.9 us  [body(): blocks = lax.all_to_all(blocks, AXES, 0, 0, tiled=True)]
    ppermute x1 -> x2, starting transfers between devices: 0.85 us -> 3.72 us  [the longest x1 1.91 us: body(): lax.ppermute(outer, AXES, [(i, i if i in (0, devices - 1) else near(i, de...]
    ppermute x32 -> x33, starting transfers between devices: 49.1 us -> 46.9 us  [permuted(): lax.ppermute(x, AXES, [(i, index(move(place(i)))) for i in range(128)])]
    ppermute x1, starting transfers between devices: 2.1 us -> 0.01 us  [body(): lax.ppermute(far, AXES, [(i, (i + 3 if i % 2 else i - 3) % devices) for i...]
    ppermute x32 -> x33, waiting for transfers between devices: 33.5 us -> 32.1 us  [permuted(): lax.ppermute(x, AXES, [(i, index(move(place(i)))) for i in range(128)])]
    ppermute x3 -> x1, starting transfers between devices: 3.67 us -> 2.72 us  [from_behind(): return lax.ppermute(x, AXES, [(i, (i + by) % count) for i in range(count)])]
    pallas_call x7 -> x8, Pallas kernels: 15.8 us -> 15.5 us  [call(): pl.pallas_call(kernel, out_shape=[s if isinstance(s, jax.ShapeDtypeStruct...]
  transfers between devices with their start and end apart: 37 -> 37, of which waited for: 24 -> 22; matrix products, arithmetic and copies ran while one was open for 0% -> 0% of each run, Pallas kernels for 2% -> 2%
where the time goes in v4:
time: 126 us
  starting transfers between devices  53.3 us (42%)
  waiting for transfers between devices  33.5 us (27%)
  blocking collectives  21.9 us (17%)
  Pallas kernels  15.5 us (12%)
    ppermute x33, starting transfers between devices, permuted(): lax.ppermute(x, AXES, [(i, index(move(place(i)))) for i in range(128)])  46.9 us
    ppermute x33, waiting for transfers between devices, permuted(): lax.ppermute(x, AXES, [(i, index(move(place(i)))) for i in range(128)])  32.1 us
    all_to_all x1, blocking collectives, body(): blocks = lax.all_to_all(blocks, AXES, 0, 0, tiled=True)  21.9 us
    pallas_call x8, Pallas kernels, call(): pl.pallas_call(kernel, out_shape=[s if isinstance(s, jax.ShapeDtypeStruct...  15.5 us
    ppermute x1, starting transfers between devices, from_behind(): return lax.ppermute(x, AXES, [(i, (i + by) % count) for i in range(count)])  2.72 us
  transfers between devices with their start and end apart: 37, of which 22 were waited for; matrix products, arithmetic and copies ran while one was open for 0% of the time, Pallas kernels for 2%

profile of v4, /device:TPU:1, one launch (start us, length us, event | category | flops | bytes accessed | tf_op | source)
XLA Modules:
  0.0 126.0 jit_solution(3317489906761035328)
XLA Ops:
  0.6 3.6 %shard_map.157 = (f32[19,4096]{1,0:T(8,128)}, f32[32,128]{1,0:T(8,128)S(1)}, f32[32,128]{1,0:T(8,128)S(1)}, f32[136,128]{1,0:T(8,128)S(1)}, s32[32,128]{1,0:T(8,...) custom-call(f32[19,4096]{1,0:T(8,128)} %states_hbm.1, ...), custom_call_target="tpu_custom_call" | custom-call | flops 40000000 | bytes 1048576 | tf_op jit(solution)/shard_map/pallas_call | solution.py:336
  4.2 3.6 %collective-permute-start = (f32[136,128]{1,0:T(8,128)S(1)}, f32[136,128]{1,0:T(8,128)S(1)}, u32[]{:S(2)}, u32[]{:S(2)}) collective-permute-start(f32[136,128]{1,0:T(8,128)S(1)} %get-tuple-element.33), channel_id=1, source_target_pairs={{0,64},{1,65},{2,66},{3,67},{4,68},{5,69},{6,70},{7,71},{8,72},{9,... | collective-permute-start | bytes 208904 | tf_op jit(solution)/shard_map/ppermute | solution.py:356
  7.8 0.9 collective-permute-start.1
  8.7 0.8 collective-permute-done
  9.5 2.7 %collective-permute-done.1 = f32[136,128]{1,0:T(8,128)S(1)} collective-permute-done((f32[136,128]{1,0:T(8,128)S(1)}, f32[136,128]{1,0:T(8,128)S(1)}, u32[]{:S(2)}, u32[]{:S(2)}) %collective-permute-start.1) | collective-permute-done | bytes 69664 | tf_op jit(solution)/shard_map/ppermute | solution.py:356
  12.2 0.1 minimum_select_fusion.3
  12.3 3.7 %collective-permute-start.3 = (f32[136,128]{1,0:T(8,128)S(1)}, f32[136,128]{1,0:T(8,128)S(1)}, u32[]{:S(2)}, u32[]{:S(2)}) collective-permute-start(f32[136,128]{1,0:T(8,128)S(1)} %minimum_select_fusion.3), channel_id=1, source_target_pairs={{0,16},{1,17},{2,18},{3,19},{4,20},{5,21},{6,22},{7,23},{8,24},{9,... | collective-permute-start | bytes 208904 | tf_op jit(solution)/shard_map/ppermute | solution.py:356
  16.0 0.4 collective-permute-start.4
  16.4 0.3 collective-permute-start.5
  16.7 1.0 collective-permute-done.3
  17.7 3.0 %collective-permute-done.4 = f32[136,128]{1,0:T(8,128)S(1)} collective-permute-done((f32[136,128]{1,0:T(8,128)S(1)}, f32[136,128]{1,0:T(8,128)S(1)}, u32[]{:S(2)}, u32[]{:S(2)}) %collective-permute-start.4) | collective-permute-done | bytes 69664 | tf_op jit(solution)/shard_map/ppermute | solution.py:356
  20.8 3.3 %collective-permute-start.6 = (f32[136,128]{1,0:T(8,128)S(1)}, f32[136,128]{1,0:T(8,128)S(1)}, u32[]{:S(2)}, u32[]{:S(2)}) collective-permute-start(f32[136,128]{1,0:T(8,128)S(1)} %minimum_select_fusion.2), channel_id=1, source_target_pairs={{0,1},{1,0},{2,3},{3,2},{4,5},{5,4},{6,7},{7,6},{8,9},{9,8},{10,11... | collective-permute-start | bytes 208904 | tf_op jit(solution)/shard_map/ppermute | solution.py:356
  24.1 0.9 collective-permute-done.6
  25.1 3.0 %collective-permute-start.7 = (f32[136,128]{1,0:T(8,128)S(1)}, f32[136,128]{1,0:T(8,128)S(1)}, u32[]{:S(2)}, u32[]{:S(2)}) collective-permute-start(f32[136,128]{1,0:T(8,128)S(1)} %minimum_select_fusion.1), channel_id=1, source_target_pairs={{0,4},{1,5},{2,6},{3,7},{4,0},{5,1},{6,2},{7,3},{8,12},{9,13},{10,... | collective-permute-start | bytes 208904 | tf_op jit(solution)/shard_map/ppermute | solution.py:356
  28.1 0.8 collective-permute-start.8
  28.9 1.0 collective-permute-done.7
  29.8 2.6 %collective-permute-done.8 = f32[136,128]{1,0:T(8,128)S(1)} collective-permute-done((f32[136,128]{1,0:T(8,128)S(1)}, f32[136,128]{1,0:T(8,128)S(1)}, u32[]{:S(2)}, u32[]{:S(2)}) %collective-permute-start.8) | collective-permute-done | bytes 69664 | tf_op jit(solution)/shard_map/ppermute | solution.py:356
  32.6 2.0 %shard_map.158 = (f32[32,128]{1,0:T(8,128)S(1)}, f32[32,128]{1,0:T(8,128)S(1)}, f32[32,128]{1,0:T(8,128)S(1)}, f32[128,128]{1,0:T(8,128)S(1)}, f32[8,128]{1,0:T(8,128)S(1)}) custom-call(f32[136,128]{1,0:T(8,128)S(1)} %minimum_select_fusion.payload_ref, f32[128,128]{1,0:T(8,128)S(1)} %get-tuple-element.34.gain_ref, ...), custom_call_target="tpu_custom_call" | custom-call | flops 40000000 | bytes 1048576 | tf_op jit(solution)/shard_map/pallas_call | solution.py:336
  34.5 1.3 %collective-permute-start.10 = (f32[128,128]{1,0:T(8,128)S(1)}, f32[128,128]{1,0:T(8,128)S(1)}, u32[]{:S(2)}, u32[]{:S(2)}) collective-permute-start(f32[128,128]{1,0:T(8,128)S(1)} %get-tuple-element.40), channel_id=1, source_target_pairs={{0,64},{1,65},{2,66},{3,67},{4,68},{5,69},{6,70},{7,71},{8,72},{9,... | collective-permute-start | bytes 196616 | tf_op jit(solution)/shard_map/ppermute | solution.py:356
  35.8 0.9 collective-permute-start.11
  36.7 0.5 collective-permute-start.12
  37.3 2.0 %collective-permute-done.10 = f32[128,128]{1,0:T(8,128)S(1)} collective-permute-done((f32[128,128]{1,0:T(8,128)S(1)}, f32[128,128]{1,0:T(8,128)S(1)}, u32[]{:S(2)}, u32[]{:S(2)}) %collective-permute-start.10) | collective-permute-done | bytes 65568 | tf_op jit(solution)/shard_map/ppermute | solution.py:356
  39.2 0.9 collective-permute-done.11
  40.1 1.7 %collective-permute-start.13 = (f32[128,128]{1,0:T(8,128)S(1)}, f32[128,128]{1,0:T(8,128)S(1)}, u32[]{:S(2)}, u32[]{:S(2)}) collective-permute-start(f32[128,128]{1,0:T(8,128)S(1)} %add_add_fusion.5), channel_id=1, source_target_pairs={{0,16},{1,17},{2,18},{3,19},{4,20},{5,21},{6,22},{7,23},{8,24},{9,... | collective-permute-start | bytes 196616 | tf_op jit(solution)/shard_map/ppermute | solution.py:356
  41.8 0.3 collective-permute-start.14
  42.1 0.7 collective-permute-start.15
  42.9 2.0 %collective-permute-done.13 = f32[128,128]{1,0:T(8,128)S(1)} collective-permute-done((f32[128,128]{1,0:T(8,128)S(1)}, f32[128,128]{1,0:T(8,128)S(1)}, u32[]{:S(2)}, u32[]{:S(2)}) %collective-permute-start.13) | collective-permute-done | bytes 65568 | tf_op jit(solution)/shard_map/ppermute | solution.py:356
  44.8 1.3 %collective-permute-done.14 = f32[128,128]{1,0:T(8,128)S(1)} collective-permute-done((f32[128,128]{1,0:T(8,128)S(1)}, f32[128,128]{1,0:T(8,128)S(1)}, u32[]{:S(2)}, u32[]{:S(2)}) %collective-permute-start.14) | collective-permute-done | bytes 65568 | tf_op jit(solution)/shard_map/ppermute | solution.py:356
  46.2 4.8 %collective-permute-start.16 = (f32[128,128]{1,0:T(8,128)S(1)}, f32[128,128]{1,0:T(8,128)S(1)}, u32[]{:S(2)}, u32[]{:S(2)}) collective-permute-start(f32[128,128]{1,0:T(8,128)S(1)} %add_add_fusion.4), channel_id=1, source_target_pairs={{0,1},{1,0},{2,3},{3,2},{4,5},{5,4},{6,7},{7,6},{8,9},{9,8},{10,11... | collective-permute-start | bytes 196616 | tf_op jit(solution)/shard_map/ppermute | solution.py:356
  51.0 0.9 collective-permute-done.16
  51.9 1.4 %collective-permute-start.17 = (f32[128,128]{1,0:T(8,128)S(1)}, f32[128,128]{1,0:T(8,128)S(1)}, u32[]{:S(2)}, u32[]{:S(2)}) collective-permute-start(f32[128,128]{1,0:T(8,128)S(1)} %add.122), channel_id=1, source_target_pairs={{0,4},{1,5},{2,6},{3,7},{4,0},{5,1},{6,2},{7,3},{8,12},{9,13},{10,... | collective-permute-start | bytes 196616 | tf_op jit(solution)/shard_map/ppermute | solution.py:356
  53.2 1.0 collective-permute-start.18
  54.3 0.3 collective-permute-start.19
  54.6 2.0 %collective-permute-done.17 = f32[128,128]{1,0:T(8,128)S(1)} collective-permute-done((f32[128,128]{1,0:T(8,128)S(1)}, f32[128,128]{1,0:T(8,128)S(1)}, u32[]{:S(2)}, u32[]{:S(2)}) %collective-permute-start.17) | collective-permute-done | bytes 65568 | tf_op jit(solution)/shard_map/ppermute | solution.py:356
  56.6 1.9 %collective-permute-done.18 = f32[128,128]{1,0:T(8,128)S(1)} collective-permute-done((f32[128,128]{1,0:T(8,128)S(1)}, f32[128,128]{1,0:T(8,128)S(1)}, u32[]{:S(2)}, u32[]{:S(2)}) %collective-permute-start.18) | collective-permute-done | bytes 65568 | tf_op jit(solution)/shard_map/ppermute | solution.py:356
  58.6 2.0 %shard_map.159 = (f32[32,128]{1,0:T(8,128)S(1)}, f32[32,128]{1,0:T(8,128)S(1)}, f32[32,128]{1,0:T(8,128)S(1)}, f32[128,128]{1,0:T(8,128)S(1)}) custom-call(f32[128,128]{1,0:T(8,128)S(1)} %add_add_fusion.3.payload_ref, f32[128,128]{1,0:T(8,128)S(1)} %get-tuple-element.34.gain_ref, s32[32,128]{1,0:T(8,128)S(1)} %get-tuple-element.35.slots_ref, ...), custom_call_target="tpu_custom_call" | custom-call | flops 40000000 | bytes 1048576 | tf_op jit(solution)/shard_map/pallas_call | solution.py:336
  60.6 2.0 %collective-permute-start.20 = (f32[128,128]{1,0:T(8,128)S(1)}, f32[128,128]{1,0:T(8,128)S(1)}, u32[]{:S(2)}, u32[]{:S(2)}) collective-permute-start(f32[128,128]{1,0:T(8,128)S(1)} %get-tuple-element.44), channel_id=1, source_target_pairs={{0,64},{1,65},{2,66},{3,67},{4,68},{5,69},{6,70},{7,71},{8,72},{9,... | collective-permute-start | bytes 196616 | tf_op jit(solution)/shard_map/ppermute | solution.py:356
  62.6 0.9 collective-permute-start.21
  63.5 1.7 %collective-permute-done.20 = f32[128,128]{1,0:T(8,128)S(1)} collective-permute-done((f32[128,128]{1,0:T(8,128)S(1)}, f32[128,128]{1,0:T(8,128)S(1)}, u32[]{:S(2)}, u32[]{:S(2)}) %collective-permute-start.20) | collective-permute-done | bytes 65568 | tf_op jit(solution)/shard_map/ppermute | solution.py:356
  65.3 2.1 %collective-permute-done.21 = f32[128,128]{1,0:T(8,128)S(1)} collective-permute-done((f32[128,128]{1,0:T(8,128)S(1)}, f32[128,128]{1,0:T(8,128)S(1)}, u32[]{:S(2)}, u32[]{:S(2)}) %collective-permute-start.21) | collective-permute-done | bytes 65568 | tf_op jit(solution)/shard_map/ppermute | solution.py:356
  67.4 1.8 %collective-permute-start.23 = (f32[128,128]{1,0:T(8,128)S(1)}, f32[128,128]{1,0:T(8,128)S(1)}, u32[]{:S(2)}, u32[]{:S(2)}) collective-permute-start(f32[128,128]{1,0:T(8,128)S(1)} %add_add_fusion.2), channel_id=1, source_target_pairs={{0,16},{1,17},{2,18},{3,19},{4,20},{5,21},{6,22},{7,23},{8,24},{9,... | collective-permute-start | bytes 196616 | tf_op jit(solution)/shard_map/ppermute | solution.py:356
  69.3 0.9 collective-permute-start.24
  70.2 0.1 collective-permute-start.25
  70.3 2.0 %collective-permute-done.23 = f32[128,128]{1,0:T(8,128)S(1)} collective-permute-done((f32[128,128]{1,0:T(8,128)S(1)}, f32[128,128]{1,0:T(8,128)S(1)}, u32[]{:S(2)}, u32[]{:S(2)}) %collective-permute-start.23) | collective-permute-done | bytes 65568 | tf_op jit(solution)/shard_map/ppermute | solution.py:356
  72.3 1.3 %collective-permute-done.24 = f32[128,128]{1,0:T(8,128)S(1)} collective-permute-done((f32[128,128]{1,0:T(8,128)S(1)}, f32[128,128]{1,0:T(8,128)S(1)}, u32[]{:S(2)}, u32[]{:S(2)}) %collective-permute-start.24) | collective-permute-done | bytes 65568 | tf_op jit(solution)/shard_map/ppermute | solution.py:356
  73.6 3.4 %collective-permute-start.26 = (f32[128,128]{1,0:T(8,128)S(1)}, f32[128,128]{1,0:T(8,128)S(1)}, u32[]{:S(2)}, u32[]{:S(2)}) collective-permute-start(f32[128,128]{1,0:T(8,128)S(1)} %add_add_fusion.1), channel_id=1, source_target_pairs={{0,1},{1,0},{2,3},{3,2},{4,5},{5,4},{6,7},{7,6},{8,9},{9,8},{10,11... | collective-permute-start | bytes 196616 | tf_op jit(solution)/shard_map/ppermute | solution.py:356
  77.0 0.9 collective-permute-done.26
  77.9 1.8 %collective-permute-start.27 = (f32[128,128]{1,0:T(8,128)S(1)}, f32[128,128]{1,0:T(8,128)S(1)}, u32[]{:S(2)}, u32[]{:S(2)}) collective-permute-start(f32[128,128]{1,0:T(8,128)S(1)} %add.132), channel_id=1, source_target_pairs={{0,4},{1,5},{2,6},{3,7},{4,0},{5,1},{6,2},{7,3},{8,12},{9,13},{10,... | collective-permute-start | bytes 196616 | tf_op jit(solution)/shard_map/ppermute | solution.py:356
  79.8 0.9 collective-permute-start.28
  80.8 2.2 %shard_map.160 = (bf16[256,4096]{1,0:T(8,128)(2,1)S(1)}, bf16[256,4096]{1,0:T(8,128)(2,1)S(1)}) custom-call(s32[2]{0:T(128)S(1)} %pad_add_fusion.here_ref, f32[8,128]{1,0:T(8,128)S(1)} %get-tuple-element.48.after_ref.smallest_ref, s32[32,128]{1,0:T(8,128)S(1)} %bitcast.15, s32[32,128]{1,0:T(8,128)S(1)} %bitcast.16), custom_call_target="tpu_custom_call" | custom-call | flops 10000000 | bytes 1048576 | tf_op jit(solution)/shard_map/pallas_call | solution.py:336
  83.0 1.2 collective-permute-done.28
  84.2 3.1 %shard_map.161 = (f32[32,128]{1,0:T(8,128)}, f32[64,128]{1,0:T(8,128)S(1)}, f32[64,128]{1,0:T(8,128)S(1)}, f32[64,128]{1,0:T(8,128)S(1)}, f32[192,128]{1,0:T(8,128)S(1)}, /*index=5*/f32[128,128]{1,0:T(8,128)S(1)}) custom-call(f32[128,128]{1,0:T(8,128)S(1)} %add_add_fusion.payload_ref, f32[128,128]{1,0:T(8,128)S(1)} %get-tuple-element.34.gain_ref, ...), custom_call_target="tpu_custom_call" | custom-call | flops 40000000 | bytes 1048576 | tf_op jit(solution)/shard_map/pallas_call | solution.py:336
  87.3 1.7 %collective-permute-start.34 = (f32[192,128]{1,0:T(8,128)S(1)}, f32[192,128]{1,0:T(8,128)S(1)}, u32[]{:S(2)}, u32[]{:S(2)}) collective-permute-start(f32[192,128]{1,0:T(8,128)S(1)} %get-tuple-element.57), channel_id=1, source_target_pairs={{0,1},{1,0},{2,3},{3,2},{4,5},{5,4},{6,7},{7,6},{8,9},{9,8},{10,11... | collective-permute-start | bytes 294920 | tf_op jit(solution)/shard_map/ppermute | solution.py:356
  89.0 1.9 %collective-permute-start.30 = (f32[8,128]{1,0:T(8,128)S(1)}, f32[8,128]{1,0:T(8,128)S(1)}, u32[]{:S(2)}, u32[]{:S(2)}) collective-permute-start(f32[8,128]{1,0:T(8,128)S(1)} %get-tuple-element.63), channel_id=1, source_target_pairs={{0,0},{1,2},{2,1},{3,4},{4,3},{5,6},{6,5},{7,8},{8,7},{9,10},{10,9... | collective-permute-start | bytes 12296 | tf_op jit(solution)/shard_map/ppermute | solution.py:446
  91.0 1.8 %collective-permute-start.35 = (f32[128,128]{1,0:T(8,128)S(1)}, f32[128,128]{1,0:T(8,128)S(1)}, u32[]{:S(2)}, u32[]{:S(2)}) collective-permute-start(f32[128,128]{1,0:T(8,128)S(1)} %slice_add_fusion), channel_id=1, source_target_pairs={{0,127},{1,2},{2,1},{3,4},{4,3},{5,6},{6,5},{7,8},{8,7},{9,10},{10... | collective-permute-start | bytes 196616 | tf_op jit(solution)/shard_map/ppermute | solution.py:485
  92.8 1.1 collective-permute-done.30
  93.9 2.7 %collective-permute-start.32 = (f32[64,128]{1,0:T(8,128)S(1)}, f32[64,128]{1,0:T(8,128)S(1)}, u32[]{:S(2)}, u32[]{:S(2)}) collective-permute-start(f32[64,128]{1,0:T(8,128)S(1)} %get-tuple-element.55), channel_id=1, source_target_pairs={{0,64},{1,65},{2,66},{3,67},{4,68},{5,69},{6,70},{7,71},{8,72},{9,... | collective-permute-start | bytes 98312 | tf_op jit(solution)/shard_map/ppermute | solution.py:406
  96.6 4.1 %collective-permute-start.36 = (f32[64,128]{1,0:T(8,128)S(1)}, f32[64,128]{1,0:T(8,128)S(1)}, u32[]{:S(2)}, u32[]{:S(2)}) collective-permute-start(f32[64,128]{1,0:T(8,128)S(1)} %slice.9), channel_id=1, source_target_pairs={{0,1},{1,0},{2,3},{3,2},{4,5},{5,4},{6,7},{7,6},{8,9},{9,8},{10,11... | collective-permute-start | bytes 98312 | tf_op jit(solution)/shard_map/ppermute | solution.py:356
  100.7 0.8 shard_map.162.weight_ref
  101.5 0.3 collective-permute-done.33.far_ref
  101.8 0.6 shard_map.163
  102.5 0.2 copy.17
  102.7 21.9 %all_to_all.11 = f32[128,1,384]{2,1,0:T(1,128)S(1)} all-to-all(f32[128,1,384]{2,1,0:T(1,128)S(1)} %copy.17), channel_id=1, replica_groups=mesh['a'=4,'b'=4,'c'=4,'d'=2] {'a','b','c','d'}, dimensions={0} | all-to-all | bytes 393216 | tf_op jit(solution)/shard_map/all_to_all | solution.py:495
  124.6 1.4 %shard_map.164 = f32[64,128]{1,0:T(8,128)} custom-call(s32[2]{0:T(128)S(1)} %pad_add_fusion.here_ref, f32[128,384]{1,0:T(8,128)S(1)} %bitcast.12, f32[64,128]{1,0:T(8,128)S(1)} %get-tuple-element.60.source_ref, f32[80,128]{1,0:T(8,128)S(1)} %pad_maximum_fusion.conduct_ref, f32[8,128]{1,0:T(8,128)S(1)} %get-tuple-element.48.after_ref.smallest_ref), custom_call_target="tpu_custom_call" | custom-call | flops 4000000 | bytes 1048576 | tf_op jit(solution)/shard_map/pallas_call | solution.py:336
  (48 shorter events, 0.7 us)
Async XLA Ops:
  4.2 5.3 %collective-permute-start = (f32[136,128]{1,0:T(8,128)S(1)}, f32[136,128]{1,0:T(8,128)S(1)}, u32[]{:S(2)}, u32[]{:S(2)}) collective-permute-start(f32[136,128]{1,0:T(8,128)S(1)} %get-tuple-element.33), channel_id=1, source_target_pairs={{0,64},{1,65},{2,66},{3,67},{4,68},{5,69},{6,70},{7,71},{8,72},{9,... | collective-permute-start | bytes 208904 | tf_op jit(solution)/shard_map/ppermute | solution.py:356
  7.8 4.4 %collective-permute-start.1 = (f32[136,128]{1,0:T(8,128)S(1)}, f32[136,128]{1,0:T(8,128)S(1)}, u32[]{:S(2)}, u32[]{:S(2)}) collective-permute-start(f32[136,128]{1,0:T(8,128)S(1)} %get-tuple-element.33), channel_id=1, source_target_pairs={{0,96},{1,97},{2,98},{3,99},{4,100},{5,101},{6,102},{7,103},{8,104... | collective-permute-start | bytes 208904 | tf_op jit(solution)/shard_map/ppermute | solution.py:356
  8.7 3.5 %collective-permute-start.2 = (f32[136,128]{1,0:T(8,128)S(1)}, f32[136,128]{1,0:T(8,128)S(1)}, u32[]{:S(2)}, u32[]{:S(2)}) collective-permute-start(f32[136,128]{1,0:T(8,128)S(1)} %get-tuple-element.33), channel_id=1, source_target_pairs={{0,32},{1,33},{2,34},{3,35},{4,36},{5,37},{6,38},{7,39},{8,40},{9,... | collective-permute-start | bytes 208904 | tf_op jit(solution)/shard_map/ppermute | solution.py:356
  12.3 5.4 %collective-permute-start.3 = (f32[136,128]{1,0:T(8,128)S(1)}, f32[136,128]{1,0:T(8,128)S(1)}, u32[]{:S(2)}, u32[]{:S(2)}) collective-permute-start(f32[136,128]{1,0:T(8,128)S(1)} %minimum_select_fusion.3), channel_id=1, source_target_pairs={{0,16},{1,17},{2,18},{3,19},{4,20},{5,21},{6,22},{7,23},{8,24},{9,... | collective-permute-start | bytes 208904 | tf_op jit(solution)/shard_map/ppermute | solution.py:356
  16.0 4.7 %collective-permute-start.4 = (f32[136,128]{1,0:T(8,128)S(1)}, f32[136,128]{1,0:T(8,128)S(1)}, u32[]{:S(2)}, u32[]{:S(2)}) collective-permute-start(f32[136,128]{1,0:T(8,128)S(1)} %minimum_select_fusion.3), channel_id=1, source_target_pairs={{0,24},{1,25},{2,26},{3,27},{4,28},{5,29},{6,30},{7,31},{8,16},{9,... | collective-permute-start | bytes 208904 | tf_op jit(solution)/shard_map/ppermute | solution.py:356
  16.4 4.3 %collective-permute-start.5 = (f32[136,128]{1,0:T(8,128)S(1)}, f32[136,128]{1,0:T(8,128)S(1)}, u32[]{:S(2)}, u32[]{:S(2)}) collective-permute-start(f32[136,128]{1,0:T(8,128)S(1)} %minimum_select_fusion.3), channel_id=1, source_target_pairs={{0,8},{1,9},{2,10},{3,11},{4,12},{5,13},{6,14},{7,15},{8,0},{9,1},... | collective-permute-start | bytes 208904 | tf_op jit(solution)/shard_map/ppermute | solution.py:356
  20.8 4.2 %collective-permute-start.6 = (f32[136,128]{1,0:T(8,128)S(1)}, f32[136,128]{1,0:T(8,128)S(1)}, u32[]{:S(2)}, u32[]{:S(2)}) collective-permute-start(f32[136,128]{1,0:T(8,128)S(1)} %minimum_select_fusion.2), channel_id=1, source_target_pairs={{0,1},{1,0},{2,3},{3,2},{4,5},{5,4},{6,7},{7,6},{8,9},{9,8},{10,11... | collective-permute-start | bytes 208904 | tf_op jit(solution)/shard_map/ppermute | solution.py:356
  25.1 4.7 %collective-permute-start.7 = (f32[136,128]{1,0:T(8,128)S(1)}, f32[136,128]{1,0:T(8,128)S(1)}, u32[]{:S(2)}, u32[]{:S(2)}) collective-permute-start(f32[136,128]{1,0:T(8,128)S(1)} %minimum_select_fusion.1), channel_id=1, source_target_pairs={{0,4},{1,5},{2,6},{3,7},{4,0},{5,1},{6,2},{7,3},{8,12},{9,13},{10,... | collective-permute-start | bytes 208904 | tf_op jit(solution)/shard_map/ppermute | solution.py:356
  28.1 4.4 %collective-permute-start.8 = (f32[136,128]{1,0:T(8,128)S(1)}, f32[136,128]{1,0:T(8,128)S(1)}, u32[]{:S(2)}, u32[]{:S(2)}) collective-permute-start(f32[136,128]{1,0:T(8,128)S(1)} %minimum_select_fusion.1), channel_id=1, source_target_pairs={{0,6},{1,7},{2,4},{3,5},{4,2},{5,3},{6,0},{7,1},{8,14},{9,15},{10,... | collective-permute-start | bytes 208904 | tf_op jit(solution)/shard_map/ppermute | solution.py:356
  28.9 3.6 %collective-permute-start.9 = (f32[136,128]{1,0:T(8,128)S(1)}, f32[136,128]{1,0:T(8,128)S(1)}, u32[]{:S(2)}, u32[]{:S(2)}) collective-permute-start(f32[136,128]{1,0:T(8,128)S(1)} %minimum_select_fusion.1), channel_id=1, source_target_pairs={{0,2},{1,3},{2,0},{3,1},{4,6},{5,7},{6,4},{7,5},{8,10},{9,11},{10,... | collective-permute-start | bytes 208904 | tf_op jit(solution)/shard_map/ppermute | solution.py:356
  34.5 4.7 %collective-permute-start.10 = (f32[128,128]{1,0:T(8,128)S(1)}, f32[128,128]{1,0:T(8,128)S(1)}, u32[]{:S(2)}, u32[]{:S(2)}) collective-permute-start(f32[128,128]{1,0:T(8,128)S(1)} %get-tuple-element.40), channel_id=1, source_target_pairs={{0,64},{1,65},{2,66},{3,67},{4,68},{5,69},{6,70},{7,71},{8,72},{9,... | collective-permute-start | bytes 196616 | tf_op jit(solution)/shard_map/ppermute | solution.py:356
  35.8 4.3 %collective-permute-start.11 = (f32[128,128]{1,0:T(8,128)S(1)}, f32[128,128]{1,0:T(8,128)S(1)}, u32[]{:S(2)}, u32[]{:S(2)}) collective-permute-start(f32[128,128]{1,0:T(8,128)S(1)} %get-tuple-element.40), channel_id=1, source_target_pairs={{0,96},{1,97},{2,98},{3,99},{4,100},{5,101},{6,102},{7,103},{8,104... | collective-permute-start | bytes 196616 | tf_op jit(solution)/shard_map/ppermute | solution.py:356
  36.7 3.4 %collective-permute-start.12 = (f32[128,128]{1,0:T(8,128)S(1)}, f32[128,128]{1,0:T(8,128)S(1)}, u32[]{:S(2)}, u32[]{:S(2)}) collective-permute-start(f32[128,128]{1,0:T(8,128)S(1)} %get-tuple-element.40), channel_id=1, source_target_pairs={{0,32},{1,33},{2,34},{3,35},{4,36},{5,37},{6,38},{7,39},{8,40},{9,... | collective-permute-start | bytes 196616 | tf_op jit(solution)/shard_map/ppermute | solution.py:356
  40.1 4.7 %collective-permute-start.13 = (f32[128,128]{1,0:T(8,128)S(1)}, f32[128,128]{1,0:T(8,128)S(1)}, u32[]{:S(2)}, u32[]{:S(2)}) collective-permute-start(f32[128,128]{1,0:T(8,128)S(1)} %add_add_fusion.5), channel_id=1, source_target_pairs={{0,16},{1,17},{2,18},{3,19},{4,20},{5,21},{6,22},{7,23},{8,24},{9,... | collective-permute-start | bytes 196616 | tf_op jit(solution)/shard_map/ppermute | solution.py:356
  41.8 4.3 %collective-permute-start.14 = (f32[128,128]{1,0:T(8,128)S(1)}, f32[128,128]{1,0:T(8,128)S(1)}, u32[]{:S(2)}, u32[]{:S(2)}) collective-permute-start(f32[128,128]{1,0:T(8,128)S(1)} %add_add_fusion.5), channel_id=1, source_target_pairs={{0,24},{1,25},{2,26},{3,27},{4,28},{5,29},{6,30},{7,31},{8,16},{9,... | collective-permute-start | bytes 196616 | tf_op jit(solution)/shard_map/ppermute | solution.py:356
  42.1 4.0 %collective-permute-start.15 = (f32[128,128]{1,0:T(8,128)S(1)}, f32[128,128]{1,0:T(8,128)S(1)}, u32[]{:S(2)}, u32[]{:S(2)}) collective-permute-start(f32[128,128]{1,0:T(8,128)S(1)} %add_add_fusion.5), channel_id=1, source_target_pairs={{0,8},{1,9},{2,10},{3,11},{4,12},{5,13},{6,14},{7,15},{8,0},{9,1},... | collective-permute-start | bytes 196616 | tf_op jit(solution)/shard_map/ppermute | solution.py:356
  46.2 5.7 %collective-permute-start.16 = (f32[128,128]{1,0:T(8,128)S(1)}, f32[128,128]{1,0:T(8,128)S(1)}, u32[]{:S(2)}, u32[]{:S(2)}) collective-permute-start(f32[128,128]{1,0:T(8,128)S(1)} %add_add_fusion.4), channel_id=1, source_target_pairs={{0,1},{1,0},{2,3},{3,2},{4,5},{5,4},{6,7},{7,6},{8,9},{9,8},{10,11... | collective-permute-start | bytes 196616 | tf_op jit(solution)/shard_map/ppermute | solution.py:356
  51.9 4.7 %collective-permute-start.17 = (f32[128,128]{1,0:T(8,128)S(1)}, f32[128,128]{1,0:T(8,128)S(1)}, u32[]{:S(2)}, u32[]{:S(2)}) collective-permute-start(f32[128,128]{1,0:T(8,128)S(1)} %add.122), channel_id=1, source_target_pairs={{0,4},{1,5},{2,6},{3,7},{4,0},{5,1},{6,2},{7,3},{8,12},{9,13},{10,... | collective-permute-start | bytes 196616 | tf_op jit(solution)/shard_map/ppermute | solution.py:356
  53.2 5.3 %collective-permute-start.18 = (f32[128,128]{1,0:T(8,128)S(1)}, f32[128,128]{1,0:T(8,128)S(1)}, u32[]{:S(2)}, u32[]{:S(2)}) collective-permute-start(f32[128,128]{1,0:T(8,128)S(1)} %add.122), channel_id=1, source_target_pairs={{0,6},{1,7},{2,4},{3,5},{4,2},{5,3},{6,0},{7,1},{8,14},{9,15},{10,... | collective-permute-start | bytes 196616 | tf_op jit(solution)/shard_map/ppermute | solution.py:356
  54.3 4.3 %collective-permute-start.19 = (f32[128,128]{1,0:T(8,128)S(1)}, f32[128,128]{1,0:T(8,128)S(1)}, u32[]{:S(2)}, u32[]{:S(2)}) collective-permute-start(f32[128,128]{1,0:T(8,128)S(1)} %add.122), channel_id=1, source_target_pairs={{0,2},{1,3},{2,0},{3,1},{4,6},{5,7},{6,4},{7,5},{8,10},{9,11},{10,... | collective-permute-start | bytes 196616 | tf_op jit(solution)/shard_map/ppermute | solution.py:356
  58.5 22.3 %copy-start.1 = (s32[4096,1]{0,1:T(1,128)S(1)}, s32[4096,1]{0,1:T(1,128)}, u32[]{:S(2)}) copy-start(s32[4096,1]{0,1:T(1,128)} %param.25) | copy-start | bytes 49156
  58.5 22.2 %copy-start.2 = (s32[4096]{0:T(1024)S(1)}, s32[4096]{0:T(1024)}, u32[]{:S(2)}) copy-start(s32[4096]{0:T(1024)} %param.26) | copy-start | bytes 49156
  58.6 25.6 %copy-start = (f32[4096]{0:T(1024)S(1)}, f32[4096]{0:T(1024)}, u32[]{:S(2)}) copy-start(f32[4096]{0:T(1024)} %param.27) | copy-start | bytes 49156
  60.6 4.7 %collective-permute-start.20 = (f32[128,128]{1,0:T(8,128)S(1)}, f32[128,128]{1,0:T(8,128)S(1)}, u32[]{:S(2)}, u32[]{:S(2)}) collective-permute-start(f32[128,128]{1,0:T(8,128)S(1)} %get-tuple-element.44), channel_id=1, source_target_pairs={{0,64},{1,65},{2,66},{3,67},{4,68},{5,69},{6,70},{7,71},{8,72},{9,... | collective-permute-start | bytes 196616 | tf_op jit(solution)/shard_map/ppermute | solution.py:356
  62.6 4.8 %collective-permute-start.21 = (f32[128,128]{1,0:T(8,128)S(1)}, f32[128,128]{1,0:T(8,128)S(1)}, u32[]{:S(2)}, u32[]{:S(2)}) collective-permute-start(f32[128,128]{1,0:T(8,128)S(1)} %get-tuple-element.44), channel_id=1, source_target_pairs={{0,96},{1,97},{2,98},{3,99},{4,100},{5,101},{6,102},{7,103},{8,104... | collective-permute-start | bytes 196616 | tf_op jit(solution)/shard_map/ppermute | solution.py:356
  63.5 3.9 %collective-permute-start.22 = (f32[128,128]{1,0:T(8,128)S(1)}, f32[128,128]{1,0:T(8,128)S(1)}, u32[]{:S(2)}, u32[]{:S(2)}) collective-permute-start(f32[128,128]{1,0:T(8,128)S(1)} %get-tuple-element.44), channel_id=1, source_target_pairs={{0,32},{1,33},{2,34},{3,35},{4,36},{5,37},{6,38},{7,39},{8,40},{9,... | collective-permute-start | bytes 196616 | tf_op jit(solution)/shard_map/ppermute | solution.py:356
  67.4 4.9 %collective-permute-start.23 = (f32[128,128]{1,0:T(8,128)S(1)}, f32[128,128]{1,0:T(8,128)S(1)}, u32[]{:S(2)}, u32[]{:S(2)}) collective-permute-start(f32[128,128]{1,0:T(8,128)S(1)} %add_add_fusion.2), channel_id=1, source_target_pairs={{0,16},{1,17},{2,18},{3,19},{4,20},{5,21},{6,22},{7,23},{8,24},{9,... | collective-permute-start | bytes 196616 | tf_op jit(solution)/shard_map/ppermute | solution.py:356
  69.3 4.3 %collective-permute-start.24 = (f32[128,128]{1,0:T(8,128)S(1)}, f32[128,128]{1,0:T(8,128)S(1)}, u32[]{:S(2)}, u32[]{:S(2)}) collective-permute-start(f32[128,128]{1,0:T(8,128)S(1)} %add_add_fusion.2), channel_id=1, source_target_pairs={{0,24},{1,25},{2,26},{3,27},{4,28},{5,29},{6,30},{7,31},{8,16},{9,... | collective-permute-start | bytes 196616 | tf_op jit(solution)/shard_map/ppermute | solution.py:356
  70.2 3.4 %collective-permute-start.25 = (f32[128,128]{1,0:T(8,128)S(1)}, f32[128,128]{1,0:T(8,128)S(1)}, u32[]{:S(2)}, u32[]{:S(2)}) collective-permute-start(f32[128,128]{1,0:T(8,128)S(1)} %add_add_fusion.2), channel_id=1, source_target_pairs={{0,8},{1,9},{2,10},{3,11},{4,12},{5,13},{6,14},{7,15},{8,0},{9,1},... | collective-permute-start | bytes 196616 | tf_op jit(solution)/shard_map/ppermute | solution.py:356
  73.6 4.3 %collective-permute-start.26 = (f32[128,128]{1,0:T(8,128)S(1)}, f32[128,128]{1,0:T(8,128)S(1)}, u32[]{:S(2)}, u32[]{:S(2)}) collective-permute-start(f32[128,128]{1,0:T(8,128)S(1)} %add_add_fusion.1), channel_id=1, source_target_pairs={{0,1},{1,0},{2,3},{3,2},{4,5},{5,4},{6,7},{7,6},{8,9},{9,8},{10,11... | collective-permute-start | bytes 196616 | tf_op jit(solution)/shard_map/ppermute | solution.py:356
  77.9 5.0 %collective-permute-start.27 = (f32[128,128]{1,0:T(8,128)S(1)}, f32[128,128]{1,0:T(8,128)S(1)}, u32[]{:S(2)}, u32[]{:S(2)}) collective-permute-start(f32[128,128]{1,0:T(8,128)S(1)} %add.132), channel_id=1, source_target_pairs={{0,4},{1,5},{2,6},{3,7},{4,0},{5,1},{6,2},{7,3},{8,12},{9,13},{10,... | collective-permute-start | bytes 196616 | tf_op jit(solution)/shard_map/ppermute | solution.py:356
  79.8 4.4 %collective-permute-start.28 = (f32[128,128]{1,0:T(8,128)S(1)}, f32[128,128]{1,0:T(8,128)S(1)}, u32[]{:S(2)}, u32[]{:S(2)}) collective-permute-start(f32[128,128]{1,0:T(8,128)S(1)} %add.132), channel_id=1, source_target_pairs={{0,6},{1,7},{2,4},{3,5},{4,2},{5,3},{6,0},{7,1},{8,14},{9,15},{10,... | collective-permute-start | bytes 196616 | tf_op jit(solution)/shard_map/ppermute | solution.py:356
  80.7 3.5 %collective-permute-start.29 = (f32[128,128]{1,0:T(8,128)S(1)}, f32[128,128]{1,0:T(8,128)S(1)}, u32[]{:S(2)}, u32[]{:S(2)}) collective-permute-start(f32[128,128]{1,0:T(8,128)S(1)} %add.132), channel_id=1, source_target_pairs={{0,2},{1,3},{2,0},{3,1},{4,6},{5,7},{6,4},{7,5},{8,10},{9,11},{10,... | collective-permute-start | bytes 196616 | tf_op jit(solution)/shard_map/ppermute | solution.py:356
  84.2 16.5 %copy-start.3 = (f32[64,128]{1,0:T(8,128)S(1)}, f32[64,128]{1,0:T(8,128)}, u32[]{:S(2)}) copy-start(f32[64,128]{1,0:T(8,128)} %conduct_hbm.1) | copy-start | bytes 98308
  87.3 3.7 %collective-permute-start.34 = (f32[192,128]{1,0:T(8,128)S(1)}, f32[192,128]{1,0:T(8,128)S(1)}, u32[]{:S(2)}, u32[]{:S(2)}) collective-permute-start(f32[192,128]{1,0:T(8,128)S(1)} %get-tuple-element.57), channel_id=1, source_target_pairs={{0,1},{1,0},{2,3},{3,2},{4,5},{5,4},{6,7},{7,6},{8,9},{9,8},{10,11... | collective-permute-start | bytes 294920 | tf_op jit(solution)/shard_map/ppermute | solution.py:356
  89.0 4.9 %collective-permute-start.30 = (f32[8,128]{1,0:T(8,128)S(1)}, f32[8,128]{1,0:T(8,128)S(1)}, u32[]{:S(2)}, u32[]{:S(2)}) collective-permute-start(f32[8,128]{1,0:T(8,128)S(1)} %get-tuple-element.63), channel_id=1, source_target_pairs={{0,0},{1,2},{2,1},{3,4},{4,3},{5,6},{6,5},{7,8},{8,7},{9,10},{10,9... | collective-permute-start | bytes 12296 | tf_op jit(solution)/shard_map/ppermute | solution.py:446
  90.9 3.0 %collective-permute-start.31 = (f32[8,128]{1,0:T(8,128)S(1)}, f32[8,128]{1,0:T(8,128)S(1)}, u32[]{:S(2)}, u32[]{:S(2)}) collective-permute-start(f32[8,128]{1,0:T(8,128)S(1)} %get-tuple-element.64), channel_id=1, source_target_pairs={{0,1},{1,0},{2,3},{3,2},{4,5},{5,4},{6,7},{7,6},{8,9},{9,8},{10,11... | collective-permute-start | bytes 12296 | tf_op jit(solution)/shard_map/ppermute | solution.py:356
  91.0 5.6 %collective-permute-start.35 = (f32[128,128]{1,0:T(8,128)S(1)}, f32[128,128]{1,0:T(8,128)S(1)}, u32[]{:S(2)}, u32[]{:S(2)}) collective-permute-start(f32[128,128]{1,0:T(8,128)S(1)} %slice_add_fusion), channel_id=1, source_target_pairs={{0,127},{1,2},{2,1},{3,4},{4,3},{5,6},{6,5},{7,8},{8,7},{9,10},{10... | collective-permute-start | bytes 196616 | tf_op jit(solution)/shard_map/ppermute | solution.py:485
  93.9 7.6 %collective-permute-start.32 = (f32[64,128]{1,0:T(8,128)S(1)}, f32[64,128]{1,0:T(8,128)S(1)}, u32[]{:S(2)}, u32[]{:S(2)}) collective-permute-start(f32[64,128]{1,0:T(8,128)S(1)} %get-tuple-element.55), channel_id=1, source_target_pairs={{0,64},{1,65},{2,66},{3,67},{4,68},{5,69},{6,70},{7,71},{8,72},{9,... | collective-permute-start | bytes 98312 | tf_op jit(solution)/shard_map/ppermute | solution.py:406
  96.6 5.2 %collective-permute-start.33 = (f32[64,128]{1,0:T(8,128)S(1)}, f32[64,128]{1,0:T(8,128)S(1)}, u32[]{:S(2)}, u32[]{:S(2)}) collective-permute-start(f32[64,128]{1,0:T(8,128)S(1)} %get-tuple-element.56), channel_id=1, source_target_pairs={{0,125},{1,4},{2,127},{3,6},{4,1},{5,8},{6,3},{7,10},{8,5},{9,12},... | collective-permute-start | bytes 98312 | tf_op jit(solution)/shard_map/ppermute | solution.py:482
  96.6 5.2 %collective-permute-start.36 = (f32[64,128]{1,0:T(8,128)S(1)}, f32[64,128]{1,0:T(8,128)S(1)}, u32[]{:S(2)}, u32[]{:S(2)}) collective-permute-start(f32[64,128]{1,0:T(8,128)S(1)} %slice.9), channel_id=1, source_target_pairs={{0,1},{1,0},{2,3},{3,2},{4,5},{5,4},{6,7},{7,6},{8,9},{9,8},{10,11... | collective-permute-start | bytes 98312 | tf_op jit(solution)/shard_map/ppermute | solution.py:356
